TPU v7x, 32 devices: a whole 2x2x4 slice. The times are simulated.
32 devices in a mesh: section: 4 (over y, x), tok: 8 (over z, core).
Axes of the slice: x: 2, y: 2, z: 4, core: 2. Of those that a mesh axis runs over, the one named last changes fastest.
Arguments:
- activations: bfloat16 [8, 2048, 8192], P('section', 'tok'), may hold values from -12 to 12
- projection: bfloat16 [8192, 512], P('tok'), may hold values from -0.0625 to 0.0625
Outputs:
- sketch: float32 [8, 512, 512], P('section', None, 'tok')
- similarity: float32 [8, 2], P('section')
All inputs are finite; a program needn't handle non-finite values.
Results may differ from a plain program's by a relative error of at most 0.0003.
Values may be sent and summed in bfloat16 or wider, within the bound.
No kernel may reach another device: no remote copies, remote signals or barrier semaphores. Data moves between devices by JAX's collectives and lax.ppermute only.
A program may use at most 64 MiB of HBM per device.

v0:
```python
import functools

import jax
import jax.numpy as jnp
from jax import lax
from jax.experimental import pallas as pl
from jax.experimental.pallas import tpu as pltpu
from jax.sharding import PartitionSpec as P


F32, BF16 = jnp.float32, jnp.bfloat16
SMEM = pl.BlockSpec(memory_space=pltpu.SMEM)
VMEM = pl.BlockSpec(memory_space=pltpu.VMEM)
HBM = pl.BlockSpec(memory_space=pltpu.HBM)


def swap(block, axis, mask):
    return lax.ppermute(block, axis, [(i, i ^ mask) for i in range(lax.axis_size(axis))])


def params(mib):
    return pltpu.CompilerParams(vmem_limit_bytes=int(mib * 1024) << 10)


def cost(flops, moved):
    return pl.CostEstimate(flops=int(flops), bytes_accessed=int(moved), transcendentals=0)


def deal_kernel(width, rows, pos, proj, mine, give, block, sem):
    core, section = pos[1], pos[2]
    start = 0
    if rows < proj.shape[0]:
        start = pl.multiple_of((section % (proj.shape[0] // rows)) * rows, 16)
    copy = pltpu.make_async_copy(proj.at[pl.ds(start, rows), :], block, sem)
    copy.start()
    rank, half = proj.shape[1], mine.shape[1]
    row = lax.broadcasted_iota(jnp.int32, (rank, half), 0)
    col = lax.broadcasted_iota(jnp.int32, (rank, half), 1)
    first = (col // width) * (2 * width) + col % width
    picks = [
        jnp.where(row == first + side * width, 1.0, 0.0).astype(BF16) for side in (core, 1 - core)
    ]
    copy.wait()
    for out, pick in zip((mine, give), picks):
        out[...] = jnp.dot(block[...], pick, preferred_element_type=F32).astype(BF16)


def deal(pos, proj, width, rows):
    rank = proj.shape[1]
    half = jax.ShapeDtypeStruct((rows, rank // 2), BF16)
    return pl.pallas_call(
        functools.partial(deal_kernel, width, rows),
        out_shape=(half, half),
        in_specs=[SMEM, HBM],
        out_specs=(VMEM, VMEM),
        scratch_shapes=[pltpu.VMEM((rows, rank), BF16), pltpu.SemaphoreType.DMA],
        compiler_params=params(4 if rows == proj.shape[0] else 63.25),
        cost_estimate=cost(2 * rows * rank * rank, 4 * rows * rank),
        name="deal",
    )(pos, proj)


def stage_kernel(k, pos, source, out, sem):
    deep = out.shape[1]
    columns = pl.ds(pl.multiple_of((pos[0] ^ k) * deep, 128), deep)
    copy = pltpu.make_async_copy(source.at[:, columns], out, sem)
    copy.start()
    copy.wait()


def stage(pos, source, k, deep):
    rows = source.shape[0]
    return pl.pallas_call(
        functools.partial(stage_kernel, k),
        out_shape=jax.ShapeDtypeStruct((rows, deep), BF16),
        in_specs=[SMEM, HBM],
        out_specs=VMEM,
        scratch_shapes=[pltpu.SemaphoreType.DMA],
        compiler_params=params(3),
        cost_estimate=cost(4e9, 4 * rows * deep),
        name="stage",
    )(pos, source)


def join_kernel(upper, lower, out):
    deep = upper.shape[0]
    out[:deep, :] = upper[...]
    out[deep:, :] = lower[...]


def join(upper, lower):
    deep, half = upper.shape
    return pl.pallas_call(
        join_kernel,
        out_shape=jax.ShapeDtypeStruct((2 * deep, half), BF16),
        in_specs=[VMEM, VMEM],
        out_specs=VMEM,
        compiler_params=params(2),
        cost_estimate=cost(1e6, 8 * deep * half),
        name="join",
    )(upper, lower)


def pick_kernel(parts, j, pos, upper, lower, out):
    deep = out.shape[0] // 2
    rows = pl.ds(pl.multiple_of(((pos[2] % parts) ^ j) * deep, 16), deep)
    out[:deep, :] = upper[rows, :]
    out[deep:, :] = lower[rows, :]


def pick(pos, upper, lower, parts, j):
    rows, half = upper.shape
    return pl.pallas_call(
        functools.partial(pick_kernel, parts, j),
        out_shape=jax.ShapeDtypeStruct((2 * rows // parts, half), BF16),
        in_specs=[SMEM, VMEM, VMEM],
        out_specs=VMEM,
        compiler_params=params(4),
        cost_estimate=cost(1e6, 8 * rows * half // parts),
        name="pick",
    )(pos, upper, lower)


def project_kernel(count, parts, started, layers, pos, acts, other, *refs):
    pieces, refs = refs[:count], refs[count:]
    total = refs[0] if started else None
    outs, weights = refs[started:-1], refs[-1]
    core, part = pos[1], pos[2] % parts
    block = weights.shape[0] // 2
    if count == 2:
        for piece, side in zip(pieces, (core, 1 - core)):
            weights[pl.ds(pl.multiple_of(side * block, 16), block), :] = piece[...]
    else:
        deep = block // parts
        for j, piece in enumerate(pieces):
            for n, side in enumerate((core, 1 - core)):
                at = pl.multiple_of(side * block + (part ^ j) * deep, 16)
                weights[pl.ds(at, deep), :] = piece[n * deep : (n + 1) * deep, :]
    rows = acts.shape[0] // layers
    kept = []
    for side, source in enumerate((acts, other)):
        for layer in range(layers):
            span = pl.ds(layer * rows, rows)
            value = jnp.dot(source[span, :], weights[...], preferred_element_type=F32)
            if started:
                value = value + total[side, span, :]
            if len(outs) == 1:
                outs[0][side, span, :] = value
            else:
                kept.append(value)
    if len(outs) == 1:
        return
    split, sums = outs
    sums[...] = jnp.zeros_like(sums)
    for layer in range(layers):
        values = [kept[layer], kept[layers + layer]]
        column = jnp.sum(values[0] + values[1], axis=0, keepdims=True)
        sums[layer : layer + 1, :] = column
        mean = column / (2 * rows)
        for side in range(2):
            span = pl.ds(layer * rows, rows)
            value = values[side] - mean
            high = value.astype(BF16)
            split[0, side, span, :] = high
            split[1, side, span, :] = (value - high.astype(F32)).astype(BF16)


def project(pos, pieces, parts, total, acts, other, layers, last):
    rows, deep = acts.shape
    half = pieces[0].shape[1]
    if last:
        out_shape = (
            jax.ShapeDtypeStruct((2, 2, rows, half), BF16),
            jax.ShapeDtypeStruct((8, half), F32),
        )
        out_specs = (VMEM, VMEM)
    else:
        out_shape = jax.ShapeDtypeStruct((2, rows, half), F32)
        out_specs = VMEM
    started = [] if total is None else [total]
    return pl.pallas_call(
        functools.partial(project_kernel, len(pieces), parts, len(started), layers),
        out_shape=out_shape,
        in_specs=[SMEM] + [VMEM] * (2 + len(pieces) + len(started)),
        out_specs=out_specs,
        scratch_shapes=[pltpu.VMEM((deep, half), BF16)],
        compiler_params=params(10),
        cost_estimate=cost(4 * rows * deep * half, 4 * rows * deep),
        name="project",
    )(pos, acts, other, *pieces, *started)


def gram_kernel(layers, chips, pos, own, oth, own_sums, oth_sums, *outs):
    chip = pos[0]
    half = own.shape[3]
    rows = own.shape[2] // layers
    width = half // chips
    along_tokens = (((0,), (0,)), ((), ()))
    for layer in range(layers):
        span = pl.ds(layer * rows, rows)
        left, right = [], []
        for part in range(2):
            here = jnp.concatenate([own[part, 0, span, :], own[part, 1, span, :]], axis=0)
            there = jnp.concatenate([oth[part, 1, span, :], oth[part, 0, span, :]], axis=0)
            left.append(here)
            right.append(jnp.concatenate([here, there], axis=1))
        gram = sum(
            lax.dot_general(left[i], right[j], along_tokens, preferred_element_type=F32)
            for i, j in ((0, 0), (0, 1), (1, 0))
        )
        blocks = [gram[i * width : (i + 1) * width] for i in range(chips)]
        for k, out in enumerate(outs):
            block = blocks[k]
            for i in range(1, chips):
                block = jnp.where(chip == i, blocks[i ^ k], block)
            out[layer * width : (layer + 1) * width, :] = block
    sums = jnp.concatenate([own_sums[...], oth_sums[...]], axis=1)
    for out in outs:
        out[layers * width :, :] = sums


def gram(pos, own, oth, own_sums, oth_sums, layers, chips):
    rows, half = own.shape[2:]
    message = jax.ShapeDtypeStruct((layers * (half // chips) + 8, 2 * half), F32)
    return pl.pallas_call(
        functools.partial(gram_kernel, layers, chips),
        out_shape=(message,) * chips,
        in_specs=[SMEM] + [VMEM] * 4,
        out_specs=(VMEM,) * chips,
        compiler_params=params(10),
        cost_estimate=cost(24 * rows * half * half, 16 * rows * half),
        name="gram",
    )(pos, own, oth, own_sums, oth_sums)


def finish_kernel(layers, chips, tokens, pos, *refs):
    messages, (sketch, turned, first_out, second_out) = refs[:chips], refs[chips:]
    chip, core, section = pos[0], pos[1], pos[2]
    rank = messages[0].shape[1]
    width = (messages[0].shape[0] - 8) // layers
    half = rank // 2
    here = lax.broadcasted_iota(jnp.int32, (width, rank), 1)
    here = here == lax.broadcasted_iota(jnp.int32, (width, rank), 0) + chip * width
    kept = []
    for layer in range(layers):
        span = slice(layer * width, (layer + 1) * width)
        value = sum(message[span, :] for message in messages[1:]) + messages[0][span, :]
        at = layers * width + layer
        sums = [message[at : at + 1, :] for message in messages]
        mean = sum(sums) / tokens
        for total in sums:
            drift = total / (tokens // chips) - mean
            lifted = jnp.sum(jnp.where(here, drift, 0.0), axis=1, keepdims=True)
            value = value + (tokens // chips) * lifted * drift
        turned[layer] = value
        kept.append(value)
        flipped = value.T
        for i in range(chips):
            for side in range(2):
                at = side * half + i * width
                to = 2 * width * i + width * (core if side == 0 else 1 - core)
                rows = pl.ds(pl.multiple_of(to, 8), width)
                sketch[layer, rows, :] = flipped[at : at + width]
    odd = section % 2 == 1
    first_out[...] = jnp.where(odd, kept[0], kept[-1]).astype(BF16)
    second_out[...] = jnp.where(odd, kept[-1], kept[0]).astype(BF16)


def finish(pos, messages, layers, tokens):
    rank = messages[0].shape[1]
    width = (messages[0].shape[0] - 8) // layers
    edge = jax.ShapeDtypeStruct((width, rank), BF16)
    return pl.pallas_call(
        functools.partial(finish_kernel, layers, len(messages), tokens),
        out_shape=(
            jax.ShapeDtypeStruct((layers, rank, width), F32),
            jax.ShapeDtypeStruct((layers, width, rank), F32),
            edge,
            edge,
        ),
        in_specs=[SMEM] + [VMEM] * len(messages),
        out_specs=(VMEM,) * 4,
        compiler_params=params(6),
        cost_estimate=cost(1e6, 2e6),
        name="finish",
    )(pos, *messages)


def products_kernel(layers, sections, pos, turned, one, two, out):
    section = pos[2]
    odd = section % 2 == 1
    one, two = one[...].astype(F32), two[...].astype(F32)
    rows = [turned[i] for i in range(layers)]
    before = jnp.where(section == 0, rows[0], jnp.where(odd, one, two))
    beyond = jnp.where(section == sections - 1, rows[-1], jnp.where(odd, two, one))
    pairs = [(before, before)] + [(row, row) for row in rows] + [(beyond, beyond)]
    chain = [before] + rows + [beyond]
    pairs += list(zip(chain[:-1], chain[1:]))
    out[...] = jnp.zeros_like(out)
    for n, (a, b) in enumerate(pairs):
        out[n : n + 1, :] = jnp.full((1, out.shape[1]), jnp.sum(a * b), F32)


def products(pos, turned, one, two, sections):
    layers = turned.shape[0]
    count = -(-(2 * layers + 3) // 8) * 8
    return pl.pallas_call(
        functools.partial(products_kernel, layers, sections),
        out_shape=jax.ShapeDtypeStruct((count, 128), F32),
        in_specs=[SMEM] + [VMEM] * 3,
        out_specs=VMEM,
        compiler_params=params(4),
        cost_estimate=cost(1e6, 1e6),
        name="products",
    )(pos, turned, one, two)


def ratios_kernel(layers, one, two, out):
    value = one[...] + two[...]
    squares = value[: layers + 2]
    chained = value[layers + 2 : 2 * layers + 3]
    ratio = chained / jnp.sqrt(squares[:-1] * squares[1:])
    out[:, 0:1] = ratio[:-1, 0:1]
    out[:, 1:2] = ratio[1:, 0:1]


def ratios(one, two, layers):
    return pl.pallas_call(
        functools.partial(ratios_kernel, layers),
        out_shape=jax.ShapeDtypeStruct((layers, 2), F32),
        in_specs=[VMEM] * 2,
        out_specs=VMEM,
        compiler_params=params(4),
        cost_estimate=cost(1e4, 1e4),
        name="ratios",
    )(one, two)


def local(activations, projection):
    layers, tok_rows, model = activations.shape
    block, rank = projection.shape
    groups, sections = lax.axis_size("tok"), lax.axis_size("section")
    chips, width = groups // 2, rank // groups
    tok, section = lax.axis_index("tok"), lax.axis_index("section")
    chip, core = tok // 2, tok % 2
    pos = jnp.stack([chip, core, section]).astype(jnp.int32)
    parts = min(sections, max(1, block // 128))
    deep = block // parts

    acts = activations.reshape(layers * tok_rows, model)
    mine_part, give_part = deal(pos, projection, width, deep)
    got_part = swap(give_part, "tok", 1)
    own = join(mine_part, got_part)

    fetched = {}
    for k in range(1, chips):
        low = k & -k
        fetched[k] = swap(own if k == low else fetched[k ^ low], "tok", 2 * low)

    mine, give = deal(pos, projection, width, block)
    got = swap(give, "tok", 1)

    order = sorted(fetched, key=lambda k: (bin(k).count("1"), -k))
    staged = {}
    for k in [0, order[-1]] + order[:-1]:
        staged[k] = stage(pos, acts, k, 2 * block)
        staged[k] = (staged[k], swap(staged[k], "tok", 1))

    far = {j: pick(pos, mine, got, parts, j) for j in range(1, parts) if j & (j - 1)}
    total = project(pos, [mine, got], parts, None, *staged[0], layers, False)
    for k in order:
        pieces = [fetched[k]]
        for j in range(1, parts):
            if k & (k - 1) == 0 and j & (j - 1):
                pieces.append(swap(far[j], "tok", 2 * k))
            else:
                pieces.append(swap(fetched[k], "section", j))
        total = project(pos, pieces, parts, total, *staged[k], layers, k == order[-1])
    split, sums = total

    messages = gram(pos, split, swap(split, "tok", 1), sums, swap(sums, "tok", 1), layers, chips)
    arrived = [messages[0]]
    for k in reversed(range(1, chips)):
        arrived.append(swap(messages[k], "tok", 2 * k))
    sketch, turned, first, second = finish(pos, arrived, layers, tok_rows * groups)

    first = swap(first, "section", 1)
    route = [(i, i + 1) for i in range(1, sections - 1, 2)]
    second = lax.ppermute(second, "section", route + [(b, a) for a, b in route])
    value = products(pos, turned, first, second, sections)
    mask = 1
    while 2 * mask < groups:
        value = value + swap(value, "tok", mask)
        mask *= 2
    return sketch, ratios(value, swap(value, "tok", mask), layers)


def solution(mesh):
    return jax.shard_map(
        local,
        mesh=mesh,
        in_specs=(P("section", "tok", None), P("tok", None)),
        out_specs=(P("section", None, "tok"), P("section", None)),
        check_vma=False,
    )
```

profile of v0, /device:TPU:5, one launch (start us, length us, event | category | flops | bytes accessed | tf_op | source)
XLA Modules:
  0.0 148.9 jit_solution(11074557485532147013)
XLA Ops:
  0.7 3.4 %copy-done.5 = bf16[2,256,8192]{2,1,0:T(8,128)(2,1)S(1)} copy-done((bf16[2,256,8192]{2,1,0:T(8,128)(2,1)S(1)}, bf16[2,256,8192]{2,1,0:T(8,128)(2,1)}, u32[]{:S(2)}) %copy-start.5) | copy-done | bytes 8388632
  4.1 2.4 %stage.7.acts = bf16[512,2048]{1,0:T(8,128)(2,1)} custom-call(s32[3]{0:T(128)S(1)} %pad_add_fusion.pos, bf16[512,8192]{1,0:T(8,128)(2,1)S(1)} %bitcast.4), custom_call_target="tpu_custom_call" | custom-call | flops 4000000000 | bytes 4194304 | tf_op jit(solution)/shard_map/stage/pallas_call | solution.py:73
  6.5 0.7 collective-permute-start.17
  7.3 2.3 %deal.3 = (bf16[1024,256]{1,0:T(8,128)(2,1)S(1)}, bf16[1024,256]{1,0:T(8,128)(2,1)}) custom-call(s32[3]{0:T(128)S(1)} %pad_add_fusion.pos, bf16[1024,512]{1,0:T(8,128)(2,1)S(1)} %copy-done), custom_call_target="tpu_custom_call" | custom-call | flops 536870912 | bytes 2097152 | tf_op jit(solution)/shard_map/deal/pallas_call | solution.py:51
  9.7 2.6 %deal.2 = (bf16[256,256]{1,0:T(8,128)(2,1)}, bf16[256,256]{1,0:T(8,128)(2,1)}) custom-call(s32[3]{0:T(128)} %copy-done.2, bf16[1024,512]{1,0:T(8,128)(2,1)} %proj.3), custom_call_target="tpu_custom_call" | custom-call | flops 134217728 | bytes 524288 | tf_op jit(solution)/shard_map/deal/pallas_call | solution.py:51
  13.5 3.4 %copy-done.6 = bf16[2,256,8192]{2,1,0:T(8,128)(2,1)S(1)} copy-done((bf16[2,256,8192]{2,1,0:T(8,128)(2,1)S(1)}, bf16[2,256,8192]{2,1,0:T(8,128)(2,1)}, u32[]{:S(2)}) %copy-start.6) | copy-done | bytes 8388632
  16.9 0.8 stage.6.acts
  17.9 2.4 %collective-permute-start.2 = (bf16[512,256]{1,0:T(8,128)(2,1)S(1)}, bf16[512,256]{1,0:T(8,128)(2,1)S(1)}, u32[]{:S(2)}, u32[]{:S(2)}) collective-permute-start(bf16[512,256]{1,0:T(8,128)(2,1)S(1)} %join.1), channel_id=1, source_target_pairs={{0,4},{1,5},{2,6},{3,7},{4,0},{5,1},{6,2},{7,3},{8,12},{9,13},{10,... | collective-permute-start | bytes 786440 | tf_op jit(solution)/shard_map/ppermute | solution.py:18
  20.2 1.3 collective-permute-start.8
  21.5 0.8 stage.5.acts
  22.4 9.5 %collective-permute-done.2.refs_0_ = bf16[512,256]{1,0:T(8,128)(2,1)S(1)} collective-permute-done((bf16[512,256]{1,0:T(8,128)(2,1)S(1)}, bf16[512,256]{1,0:T(8,128)(2,1)S(1)}, u32[]{:S(2)}, u32[]{:S(2)}) %collective-permute-start.2) | collective-permute-done | bytes 262176 | tf_op jit(solution)/shard_map/ppermute | solution.py:18
  31.9 1.4 collective-permute-start.7
  33.3 1.2 collective-permute-start.14
  34.5 0.8 stage.4.acts
  35.9 5.1 %collective-permute-done.14.refs_1_ = bf16[512,256]{1,0:T(8,128)(2,1)S(1)} collective-permute-done((bf16[512,256]{1,0:T(8,128)(2,1)S(1)}, bf16[512,256]{1,0:T(8,128)(2,1)S(1)}, u32[]{:S(2)}, u32[]{:S(2)}) %collective-permute-start.14) | collective-permute-done | bytes 262176 | tf_op jit(solution)/shard_map/ppermute | solution.py:18
  41.1 6.7 %collective-permute-done.15.refs_2_ = bf16[512,256]{1,0:T(8,128)(2,1)S(1)} collective-permute-done((bf16[512,256]{1,0:T(8,128)(2,1)S(1)}, bf16[512,256]{1,0:T(8,128)(2,1)S(1)}, u32[]{:S(2)}, u32[]{:S(2)}) %collective-permute-start.15) | collective-permute-done | bytes 262176 | tf_op jit(solution)/shard_map/ppermute | solution.py:18
  47.9 5.8 %collective-permute-done.10.refs_2_ = bf16[512,256]{1,0:T(8,128)(2,1)S(1)} collective-permute-done((bf16[512,256]{1,0:T(8,128)(2,1)S(1)}, bf16[512,256]{1,0:T(8,128)(2,1)S(1)}, u32[]{:S(2)}, u32[]{:S(2)}) %collective-permute-start.10) | collective-permute-done | bytes 262176 | tf_op jit(solution)/shard_map/ppermute | solution.py:18
  53.7 1.2 collective-permute-start.9
  54.9 4.0 %collective-permute-done.9.refs_1_ = bf16[512,256]{1,0:T(8,128)(2,1)S(1)} collective-permute-done((bf16[512,256]{1,0:T(8,128)(2,1)S(1)}, bf16[512,256]{1,0:T(8,128)(2,1)S(1)}, u32[]{:S(2)}, u32[]{:S(2)}) %collective-permute-start.9) | collective-permute-done | bytes 262176 | tf_op jit(solution)/shard_map/ppermute | solution.py:18
  58.9 1.1 pick.1
  60.0 4.1 %collective-permute-done.3.refs_0_ = bf16[512,256]{1,0:T(8,128)(2,1)S(1)} collective-permute-done((bf16[512,256]{1,0:T(8,128)(2,1)S(1)}, bf16[512,256]{1,0:T(8,128)(2,1)S(1)}, u32[]{:S(2)}, u32[]{:S(2)}) %collective-permute-start.3) | collective-permute-done | bytes 262176 | tf_op jit(solution)/shard_map/ppermute | solution.py:18
  64.2 2.4 %collective-permute-start.16 = (bf16[512,256]{1,0:T(8,128)(2,1)S(1)}, bf16[512,256]{1,0:T(8,128)(2,1)S(1)}, u32[]{:S(2)}, u32[]{:S(2)}) collective-permute-start(bf16[512,256]{1,0:T(8,128)(2,1)S(1)} %pick.1), channel_id=1, source_target_pairs={{0,4},{1,5},{2,6},{3,7},{4,0},{5,1},{6,2},{7,3},{8,12},{9,13},{10,... | collective-permute-start | bytes 786440 | tf_op jit(solution)/shard_map/ppermute | solution.py:18
  66.6 6.6 %collective-permute-done.16.refs_3_ = bf16[512,256]{1,0:T(8,128)(2,1)S(1)} collective-permute-done((bf16[512,256]{1,0:T(8,128)(2,1)S(1)}, bf16[512,256]{1,0:T(8,128)(2,1)S(1)}, u32[]{:S(2)}, u32[]{:S(2)}) %collective-permute-start.16) | collective-permute-done | bytes 262176 | tf_op jit(solution)/shard_map/ppermute | solution.py:18
  73.9 7.3 %collective-permute-done.12.refs_3_ = bf16[512,256]{1,0:T(8,128)(2,1)S(1)} collective-permute-done((bf16[512,256]{1,0:T(8,128)(2,1)S(1)}, bf16[512,256]{1,0:T(8,128)(2,1)S(1)}, u32[]{:S(2)}, u32[]{:S(2)}) %collective-permute-start.12) | collective-permute-done | bytes 262176 | tf_op jit(solution)/shard_map/ppermute | solution.py:18
  81.2 1.2 collective-permute-start.4
  82.6 1.2 collective-permute-start.6
  83.8 3.6 %project.4.refs_4_ = f32[2,512,256]{2,1,0:T(8,128)S(1)} custom-call(s32[3]{0:T(128)S(1)} %copy-done.4, bf16[512,2048]{1,0:T(8,128)(2,1)} %stage.7.acts, bf16[512,2048]{1,0:T(8,128)(2,1)} %collective-permute-done.17.other, bf16[1024,256]{1,0:T(8,128)(2,1)S(1)} %get-tuple-element.18.upper.refs_0_, bf16[1024,256]{1,0:T(8,128)(2,1)} %collective-permute-done.11.lower.refs_1_), custom_call_target="tpu_custom_call" | custom-call | flops 1073741824 | bytes 4194304 | tf_op jit(solution)/shard_map/project/pallas_call | solution.py:181
  87.5 1.9 %project.5.refs_4_ = f32[2,512,256]{2,1,0:T(8,128)S(1)} custom-call(s32[3]{0:T(128)S(1)} %copy-done.4, bf16[512,2048]{1,0:T(8,128)(2,1)S(1)} %stage.6.acts, bf16[512,2048]{1,0:T(8,128)(2,1)S(1)} %collective-permute-done.13.other, bf16[512,256]{1,0:T(8,128)(2,1)S(1)} %collective-permute-done.2.refs_0_, bf16[512,256]{1,0:T(8,128)(2,1)S(1)} %collective-permute-done.14.refs_1_, ...), custom_call_target="tpu_custom_call" | custom-call | flops 1073741824 | bytes 4194304 | tf_op jit(solution)/shard_map/project/pallas_call | solution.py:181
  89.4 1.9 %project.6.refs_4_ = f32[2,512,256]{2,1,0:T(8,128)S(1)} custom-call(s32[3]{0:T(128)S(1)} %copy-done.4, bf16[512,2048]{1,0:T(8,128)(2,1)S(1)} %stage.5.acts, bf16[512,2048]{1,0:T(8,128)(2,1)S(1)} %collective-permute-done.7.other, bf16[512,256]{1,0:T(8,128)(2,1)S(1)} %collective-permute-done.8.refs_0_, bf16[512,256]{1,0:T(8,128)(2,1)S(1)} %collective-permute-done.9.refs_1_, ...), custom_call_target="tpu_custom_call" | custom-call | flops 1073741824 | bytes 4194304 | tf_op jit(solution)/shard_map/project/pallas_call | solution.py:181
  91.3 2.1 %project.7 = (bf16[2,2,512,256]{3,2,1,0:T(8,128)(2,1)S(1)}, f32[8,256]{1,0:T(8,128)S(1)}) custom-call(s32[3]{0:T(128)S(1)} %copy-done.4, bf16[512,2048]{1,0:T(8,128)(2,1)S(1)} %stage.4.acts, bf16[512,2048]{1,0:T(8,128)(2,1)S(1)} %collective-permute-done.other, bf16[512,256]{1,0:T(8,128)(2,1)S(1)} %collective-permute-done.3.refs_0_, ...), custom_call_target="tpu_custom_call" | custom-call | flops 1073741824 | bytes 4194304 | tf_op jit(solution)/shard_map/project/pallas_call | solution.py:181
  93.5 6.4 %collective-permute-start.18 = (bf16[2,2,512,256]{3,2,1,0:T(8,128)(2,1)S(1)}, bf16[2,2,512,256]{3,2,1,0:T(8,128)(2,1)S(1)}, u32[]{:S(2)}, u32[]{:S(2)}) collective-permute-start(bf16[2,2,512,256]{3,2,1,0:T(8,128)(2,1)S(1)} %get-tuple-element.20.own), channel_id=1, source_target_pairs={{0,1},{1,0},{2,3},{3,2},{4,5},{5,4},{6,7},{7,6},{8,9},{9,8},{10,11... | collective-permute-start | bytes 3145736 | tf_op jit(solution)/shard_map/ppermute | solution.py:18
  100.0 2.2 %collective-permute-done.19.oth_sums = f32[8,256]{1,0:T(8,128)S(1)} collective-permute-done((f32[8,256]{1,0:T(8,128)S(1)}, f32[8,256]{1,0:T(8,128)S(1)}, u32[]{:S(2)}, u32[]{:S(2)}) %collective-permute-start.19) | collective-permute-done | bytes 8224 | tf_op jit(solution)/shard_map/ppermute | solution.py:18
  102.2 1.6 %gram.1 = (f32[136,512]{1,0:T(8,128)S(1)}, f32[136,512]{1,0:T(8,128)S(1)}, f32[136,512]{1,0:T(8,128)S(1)}, f32[136,512]{1,0:T(8,128)S(1)}) custom-call(s32[3]{0:T(128)S(1)} %copy-done.4, bf16[2,2,512,256]{3,2,1,0:T(8,128)(2,1)S(1)} %get-tuple-element.20.own, bf16[2,2,512,256]{3,2,1,0:T(8,128)(2,1)S(1)} %collective-permute-done.18.oth, ...), custom_call_target="tpu_custom_call" | custom-call | flops 805306368 | bytes 2097152 | tf_op jit(solution)/shard_map/gram/pallas_call | solution.py:225
  103.8 2.4 %collective-permute-start.20 = (f32[136,512]{1,0:T(8,128)S(1)}, f32[136,512]{1,0:T(8,128)S(1)}, u32[]{:S(2)}, u32[]{:S(2)}) collective-permute-start(f32[136,512]{1,0:T(8,128)S(1)} %get-tuple-element.23), channel_id=1, source_target_pairs={{0,6},{1,7},{2,4},{3,5},{4,2},{5,3},{6,0},{7,1},{8,14},{9,15},{10,... | collective-permute-start | bytes 835592 | tf_op jit(solution)/shard_map/ppermute | solution.py:18
  106.2 1.2 collective-permute-start.22
  107.4 6.2 %collective-permute-done.20.refs_1_ = f32[136,512]{1,0:T(8,128)S(1)} collective-permute-done((f32[136,512]{1,0:T(8,128)S(1)}, f32[136,512]{1,0:T(8,128)S(1)}, u32[]{:S(2)}, u32[]{:S(2)}) %collective-permute-start.20) | collective-permute-done | bytes 278560 | tf_op jit(solution)/shard_map/ppermute | solution.py:18
  113.6 16.5 %collective-permute-done.21.refs_2_ = f32[136,512]{1,0:T(8,128)S(1)} collective-permute-done((f32[136,512]{1,0:T(8,128)S(1)}, f32[136,512]{1,0:T(8,128)S(1)}, u32[]{:S(2)}, u32[]{:S(2)}) %collective-permute-start.21) | collective-permute-done | bytes 278560 | tf_op jit(solution)/shard_map/ppermute | solution.py:18
  130.2 0.9 finish.1
  131.1 1.3 collective-permute-start.23
  132.4 2.1 %collective-permute-start.24 = (bf16[64,512]{1,0:T(8,128)(2,1)S(1)}, bf16[64,512]{1,0:T(8,128)(2,1)S(1)}, u32[]{:S(2)}, u32[]{:S(2)}) collective-permute-start(bf16[64,512]{1,0:T(8,128)(2,1)S(1)} %get-tuple-element.29), channel_id=1, source_target_pairs={{8,16},{16,8},{9,17},{17,9},{10,18},{18,10},{11,19},{19,11},{12,20... | collective-permute-start | bytes 196616 | tf_op jit(solution)/shard_map/ppermute | solution.py:389
  134.5 3.8 %collective-permute-done.24.two = bf16[64,512]{1,0:T(8,128)(2,1)S(1)} collective-permute-done((bf16[64,512]{1,0:T(8,128)(2,1)S(1)}, bf16[64,512]{1,0:T(8,128)(2,1)S(1)}, u32[]{:S(2)}, u32[]{:S(2)}) %collective-permute-start.24) | collective-permute-done | bytes 65568 | tf_op jit(solution)/shard_map/ppermute | solution.py:389
  138.3 0.8 products.1
  139.1 2.4 %collective-permute-start.25 = (f32[8,128]{1,0:T(8,128)S(1)}, f32[8,128]{1,0:T(8,128)S(1)}, u32[]{:S(2)}, u32[]{:S(2)}) collective-permute-start(f32[8,128]{1,0:T(8,128)S(1)} %products.1), channel_id=1, source_target_pairs={{0,1},{1,0},{2,3},{3,2},{4,5},{5,4},{6,7},{7,6},{8,9},{9,8},{10,11... | collective-permute-start | bytes 12296 | tf_op jit(solution)/shard_map/ppermute | solution.py:18
  141.5 0.8 collective-permute-done.25
  142.3 2.5 %collective-permute-done.26 = f32[8,128]{1,0:T(8,128)S(1)} collective-permute-done((f32[8,128]{1,0:T(8,128)S(1)}, f32[8,128]{1,0:T(8,128)S(1)}, u32[]{:S(2)}, u32[]{:S(2)}) %collective-permute-start.26) | collective-permute-done | bytes 4128 | tf_op jit(solution)/shard_map/ppermute | solution.py:18
  144.8 1.2 collective-permute-start.27
  146.0 0.9 copy.4
  146.9 1.3 collective-permute-done.27.two
  (42 shorter events, 4.0 us)
Async XLA Ops:
  0.7 6.6 %copy-start.2 = (s32[3]{0:T(128)}, s32[3]{0:T(128)S(1)}, u32[]{:S(2)}) copy-start(s32[3]{0:T(128)S(1)} %pad_add_fusion.pos) | copy-start | bytes 40
  0.7 3.4 %copy-start.5 = (bf16[2,256,8192]{2,1,0:T(8,128)(2,1)S(1)}, bf16[2,256,8192]{2,1,0:T(8,128)(2,1)}, u32[]{:S(2)}) copy-start(bf16[2,256,8192]{2,1,0:T(8,128)(2,1)} %param.2) | copy-start | bytes 25165828
  4.1 3.2 %copy-start = (bf16[1024,512]{1,0:T(8,128)(2,1)S(1)}, bf16[1024,512]{1,0:T(8,128)(2,1)}, u32[]{:S(2)}) copy-start(bf16[1024,512]{1,0:T(8,128)(2,1)} %proj.3) | copy-start | bytes 3145732
  6.5 75.9 %collective-permute-start.17 = (bf16[512,2048]{1,0:T(8,128)(2,1)}, bf16[512,2048]{1,0:T(8,128)(2,1)}, u32[]{:S(2)}, u32[]{:S(2)}) collective-permute-start(bf16[512,2048]{1,0:T(8,128)(2,1)} %stage.7.acts), channel_id=1, source_target_pairs={{0,1},{1,0},{2,3},{3,2},{4,5},{5,4},{6,7},{7,6},{8,9},{9,8},{10,11... | collective-permute-start | bytes 6291464 | tf_op jit(solution)/shard_map/ppermute | solution.py:18
  9.6 25.7 %collective-permute-start.11 = (bf16[1024,256]{1,0:T(8,128)(2,1)}, bf16[1024,256]{1,0:T(8,128)(2,1)}, u32[]{:S(2)}, u32[]{:S(2)}) collective-permute-start(bf16[1024,256]{1,0:T(8,128)(2,1)} %get-tuple-element.19), channel_id=1, source_target_pairs={{0,1},{1,0},{2,3},{3,2},{4,5},{5,4},{6,7},{7,6},{8,9},{9,8},{10,11... | collective-permute-start | bytes 1572872 | tf_op jit(solution)/shard_map/ppermute | solution.py:18
  12.3 5.5 %copy-start.1 = (bf16[256,256]{1,0:T(8,128)(2,1)S(1)}, bf16[256,256]{1,0:T(8,128)(2,1)}, u32[]{:S(2)}) copy-start(bf16[256,256]{1,0:T(8,128)(2,1)} %get-tuple-element.16.upper) | copy-start | bytes 393220
  12.3 5.5 %collective-permute-start.1 = (bf16[256,256]{1,0:T(8,128)(2,1)}, bf16[256,256]{1,0:T(8,128)(2,1)S(1)}, u32[]{:S(2)}, u32[]{:S(2)}) collective-permute-start(bf16[256,256]{1,0:T(8,128)(2,1)} %get-tuple-element.17), channel_id=1, source_target_pairs={{0,1},{1,0},{2,3},{3,2},{4,5},{5,4},{6,7},{7,6},{8,9},{9,8},{10,11... | collective-permute-start | bytes 393224 | tf_op jit(solution)/shard_map/ppermute | solution.py:18
  12.8 0.7 copy-start.3
  13.5 3.4 %copy-start.6 = (bf16[2,256,8192]{2,1,0:T(8,128)(2,1)S(1)}, bf16[2,256,8192]{2,1,0:T(8,128)(2,1)}, u32[]{:S(2)}) copy-start(bf16[2,256,8192]{2,1,0:T(8,128)(2,1)} %param.2) | copy-start | bytes 25165828
  17.7 64.9 %collective-permute-start.13 = (bf16[512,2048]{1,0:T(8,128)(2,1)S(1)}, bf16[512,2048]{1,0:T(8,128)(2,1)S(1)}, u32[]{:S(2)}, u32[]{:S(2)}) collective-permute-start(bf16[512,2048]{1,0:T(8,128)(2,1)S(1)} %stage.6.acts), channel_id=1, source_target_pairs={{0,1},{1,0},{2,3},{3,2},{4,5},{5,4},{6,7},{7,6},{8,9},{9,8},{10,11... | collective-permute-start | bytes 6291464 | tf_op jit(solution)/shard_map/ppermute | solution.py:18
  17.9 14.0 %collective-permute-start.2 = (bf16[512,256]{1,0:T(8,128)(2,1)S(1)}, bf16[512,256]{1,0:T(8,128)(2,1)S(1)}, u32[]{:S(2)}, u32[]{:S(2)}) collective-permute-start(bf16[512,256]{1,0:T(8,128)(2,1)S(1)} %join.1), channel_id=1, source_target_pairs={{0,4},{1,5},{2,6},{3,7},{4,0},{5,1},{6,2},{7,3},{8,12},{9,13},{10,... | collective-permute-start | bytes 786440 | tf_op jit(solution)/shard_map/ppermute | solution.py:18
  20.2 13.0 %collective-permute-start.8 = (bf16[512,256]{1,0:T(8,128)(2,1)S(1)}, bf16[512,256]{1,0:T(8,128)(2,1)S(1)}, u32[]{:S(2)}, u32[]{:S(2)}) collective-permute-start(bf16[512,256]{1,0:T(8,128)(2,1)S(1)} %join.1), channel_id=1, source_target_pairs={{0,2},{1,3},{2,0},{3,1},{4,6},{5,7},{6,4},{7,5},{8,10},{9,11},{10,... | collective-permute-start | bytes 786440 | tf_op jit(solution)/shard_map/ppermute | solution.py:18
  22.4 36.6 %copy-start.4 = (s32[3]{0:T(128)S(1)}, s32[3]{0:T(128)}, u32[]{:S(2)}) copy-start(s32[3]{0:T(128)} %copy-done.2) | copy-start | bytes 40
  31.9 57.5 %collective-permute-start.7 = (bf16[512,2048]{1,0:T(8,128)(2,1)S(1)}, bf16[512,2048]{1,0:T(8,128)(2,1)S(1)}, u32[]{:S(2)}, u32[]{:S(2)}) collective-permute-start(bf16[512,2048]{1,0:T(8,128)(2,1)S(1)} %stage.5.acts), channel_id=1, source_target_pairs={{0,1},{1,0},{2,3},{3,2},{4,5},{5,4},{6,7},{7,6},{8,9},{9,8},{10,11... | collective-permute-start | bytes 6291464 | tf_op jit(solution)/shard_map/ppermute | solution.py:18
  33.3 7.7 %collective-permute-start.14 = (bf16[512,256]{1,0:T(8,128)(2,1)S(1)}, bf16[512,256]{1,0:T(8,128)(2,1)S(1)}, u32[]{:S(2)}, u32[]{:S(2)}) collective-permute-start(bf16[512,256]{1,0:T(8,128)(2,1)S(1)} %collective-permute-done.2.refs_0_), channel_id=1, source_target_pairs={{0,8},{8,0},{16,24},{24,16},{1,9},{9,1},{17,25},{25,17},{2,10},{10... | collective-permute-start | bytes 786440 | tf_op jit(solution)/shard_map/ppermute | solution.py:18
  35.3 56.0 %collective-permute-start = (bf16[512,2048]{1,0:T(8,128)(2,1)S(1)}, bf16[512,2048]{1,0:T(8,128)(2,1)S(1)}, u32[]{:S(2)}, u32[]{:S(2)}) collective-permute-start(bf16[512,2048]{1,0:T(8,128)(2,1)S(1)} %stage.4.acts), channel_id=1, source_target_pairs={{0,1},{1,0},{2,3},{3,2},{4,5},{5,4},{6,7},{7,6},{8,9},{9,8},{10,11... | collective-permute-start | bytes 6291464 | tf_op jit(solution)/shard_map/ppermute | solution.py:18
  40.9 6.8 %collective-permute-start.15 = (bf16[512,256]{1,0:T(8,128)(2,1)S(1)}, bf16[512,256]{1,0:T(8,128)(2,1)S(1)}, u32[]{:S(2)}, u32[]{:S(2)}) collective-permute-start(bf16[512,256]{1,0:T(8,128)(2,1)S(1)} %collective-permute-done.2.refs_0_), channel_id=1, source_target_pairs={{0,16},{8,24},{16,0},{24,8},{1,17},{9,25},{17,1},{25,9},{2,18},{10... | collective-permute-start | bytes 786440 | tf_op jit(solution)/shard_map/ppermute | solution.py:18
  47.8 6.0 %collective-permute-start.10 = (bf16[512,256]{1,0:T(8,128)(2,1)S(1)}, bf16[512,256]{1,0:T(8,128)(2,1)S(1)}, u32[]{:S(2)}, u32[]{:S(2)}) collective-permute-start(bf16[512,256]{1,0:T(8,128)(2,1)S(1)} %collective-permute-done.8.refs_0_), channel_id=1, source_target_pairs={{0,16},{8,24},{16,0},{24,8},{1,17},{9,25},{17,1},{25,9},{2,18},{10... | collective-permute-start | bytes 786440 | tf_op jit(solution)/shard_map/ppermute | solution.py:18
  53.7 5.2 %collective-permute-start.9 = (bf16[512,256]{1,0:T(8,128)(2,1)S(1)}, bf16[512,256]{1,0:T(8,128)(2,1)S(1)}, u32[]{:S(2)}, u32[]{:S(2)}) collective-permute-start(bf16[512,256]{1,0:T(8,128)(2,1)S(1)} %collective-permute-done.8.refs_0_), channel_id=1, source_target_pairs={{0,8},{8,0},{16,24},{24,16},{1,9},{9,1},{17,25},{25,17},{2,10},{10... | collective-permute-start | bytes 786440 | tf_op jit(solution)/shard_map/ppermute | solution.py:18
  58.9 5.2 %collective-permute-start.3 = (bf16[512,256]{1,0:T(8,128)(2,1)S(1)}, bf16[512,256]{1,0:T(8,128)(2,1)S(1)}, u32[]{:S(2)}, u32[]{:S(2)}) collective-permute-start(bf16[512,256]{1,0:T(8,128)(2,1)S(1)} %collective-permute-done.2.refs_0_), channel_id=1, source_target_pairs={{0,2},{1,3},{2,0},{3,1},{4,6},{5,7},{6,4},{7,5},{8,10},{9,11},{10,... | collective-permute-start | bytes 786440 | tf_op jit(solution)/shard_map/ppermute | solution.py:18
  64.2 9.0 %collective-permute-start.16 = (bf16[512,256]{1,0:T(8,128)(2,1)S(1)}, bf16[512,256]{1,0:T(8,128)(2,1)S(1)}, u32[]{:S(2)}, u32[]{:S(2)}) collective-permute-start(bf16[512,256]{1,0:T(8,128)(2,1)S(1)} %pick.1), channel_id=1, source_target_pairs={{0,4},{1,5},{2,6},{3,7},{4,0},{5,1},{6,2},{7,3},{8,12},{9,13},{10,... | collective-permute-start | bytes 786440 | tf_op jit(solution)/shard_map/ppermute | solution.py:18
  73.2 8.0 %collective-permute-start.12 = (bf16[512,256]{1,0:T(8,128)(2,1)S(1)}, bf16[512,256]{1,0:T(8,128)(2,1)S(1)}, u32[]{:S(2)}, u32[]{:S(2)}) collective-permute-start(bf16[512,256]{1,0:T(8,128)(2,1)S(1)} %pick.1), channel_id=1, source_target_pairs={{0,2},{1,3},{2,0},{3,1},{4,6},{5,7},{6,4},{7,5},{8,10},{9,11},{10,... | collective-permute-start | bytes 786440 | tf_op jit(solution)/shard_map/ppermute | solution.py:18
  81.2 10.1 %collective-permute-start.4 = (bf16[512,256]{1,0:T(8,128)(2,1)S(1)}, bf16[512,256]{1,0:T(8,128)(2,1)S(1)}, u32[]{:S(2)}, u32[]{:S(2)}) collective-permute-start(bf16[512,256]{1,0:T(8,128)(2,1)S(1)} %collective-permute-done.3.refs_0_), channel_id=1, source_target_pairs={{0,8},{8,0},{16,24},{24,16},{1,9},{9,1},{17,25},{25,17},{2,10},{10... | collective-permute-start | bytes 786440 | tf_op jit(solution)/shard_map/ppermute | solution.py:18
  82.4 8.9 %collective-permute-start.5 = (bf16[512,256]{1,0:T(8,128)(2,1)S(1)}, bf16[512,256]{1,0:T(8,128)(2,1)S(1)}, u32[]{:S(2)}, u32[]{:S(2)}) collective-permute-start(bf16[512,256]{1,0:T(8,128)(2,1)S(1)} %collective-permute-done.3.refs_0_), channel_id=1, source_target_pairs={{0,16},{8,24},{16,0},{24,8},{1,17},{9,25},{17,1},{25,9},{2,18},{10... | collective-permute-start | bytes 786440 | tf_op jit(solution)/shard_map/ppermute | solution.py:18
  82.6 8.7 %collective-permute-start.6 = (bf16[512,256]{1,0:T(8,128)(2,1)S(1)}, bf16[512,256]{1,0:T(8,128)(2,1)S(1)}, u32[]{:S(2)}, u32[]{:S(2)}) collective-permute-start(bf16[512,256]{1,0:T(8,128)(2,1)S(1)} %collective-permute-done.3.refs_0_), channel_id=1, source_target_pairs={{0,24},{8,16},{16,8},{24,0},{1,25},{9,17},{17,9},{25,1},{2,26},{10... | collective-permute-start | bytes 786440 | tf_op jit(solution)/shard_map/ppermute | solution.py:18
  93.5 8.7 %collective-permute-start.18 = (bf16[2,2,512,256]{3,2,1,0:T(8,128)(2,1)S(1)}, bf16[2,2,512,256]{3,2,1,0:T(8,128)(2,1)S(1)}, u32[]{:S(2)}, u32[]{:S(2)}) collective-permute-start(bf16[2,2,512,256]{3,2,1,0:T(8,128)(2,1)S(1)} %get-tuple-element.20.own), channel_id=1, source_target_pairs={{0,1},{1,0},{2,3},{3,2},{4,5},{5,4},{6,7},{7,6},{8,9},{9,8},{10,11... | collective-permute-start | bytes 3145736 | tf_op jit(solution)/shard_map/ppermute | solution.py:18
  99.9 2.3 %collective-permute-start.19 = (f32[8,256]{1,0:T(8,128)S(1)}, f32[8,256]{1,0:T(8,128)S(1)}, u32[]{:S(2)}, u32[]{:S(2)}) collective-permute-start(f32[8,256]{1,0:T(8,128)S(1)} %get-tuple-element.21.own_sums), channel_id=1, source_target_pairs={{0,1},{1,0},{2,3},{3,2},{4,5},{5,4},{6,7},{7,6},{8,9},{9,8},{10,11... | collective-permute-start | bytes 24584 | tf_op jit(solution)/shard_map/ppermute | solution.py:18
  103.8 9.8 %collective-permute-start.20 = (f32[136,512]{1,0:T(8,128)S(1)}, f32[136,512]{1,0:T(8,128)S(1)}, u32[]{:S(2)}, u32[]{:S(2)}) collective-permute-start(f32[136,512]{1,0:T(8,128)S(1)} %get-tuple-element.23), channel_id=1, source_target_pairs={{0,6},{1,7},{2,4},{3,5},{4,2},{5,3},{6,0},{7,1},{8,14},{9,15},{10,... | collective-permute-start | bytes 835592 | tf_op jit(solution)/shard_map/ppermute | solution.py:18
  106.2 23.9 %collective-permute-start.21 = (f32[136,512]{1,0:T(8,128)S(1)}, f32[136,512]{1,0:T(8,128)S(1)}, u32[]{:S(2)}, u32[]{:S(2)}) collective-permute-start(f32[136,512]{1,0:T(8,128)S(1)} %get-tuple-element.24), channel_id=1, source_target_pairs={{0,4},{1,5},{2,6},{3,7},{4,0},{5,1},{6,2},{7,3},{8,12},{9,13},{10,... | collective-permute-start | bytes 835592 | tf_op jit(solution)/shard_map/ppermute | solution.py:18
  106.2 23.9 %collective-permute-start.22 = (f32[136,512]{1,0:T(8,128)S(1)}, f32[136,512]{1,0:T(8,128)S(1)}, u32[]{:S(2)}, u32[]{:S(2)}) collective-permute-start(f32[136,512]{1,0:T(8,128)S(1)} %get-tuple-element.25), channel_id=1, source_target_pairs={{0,2},{1,3},{2,0},{3,1},{4,6},{5,7},{6,4},{7,5},{8,10},{9,11},{10,... | collective-permute-start | bytes 835592 | tf_op jit(solution)/shard_map/ppermute | solution.py:18
  131.1 3.4 %collective-permute-start.23 = (bf16[64,512]{1,0:T(8,128)(2,1)S(1)}, bf16[64,512]{1,0:T(8,128)(2,1)S(1)}, u32[]{:S(2)}, u32[]{:S(2)}) collective-permute-start(bf16[64,512]{1,0:T(8,128)(2,1)S(1)} %get-tuple-element.28), channel_id=1, source_target_pairs={{0,8},{8,0},{16,24},{24,16},{1,9},{9,1},{17,25},{25,17},{2,10},{10... | collective-permute-start | bytes 196616 | tf_op jit(solution)/shard_map/ppermute | solution.py:18
  132.4 5.9 %collective-permute-start.24 = (bf16[64,512]{1,0:T(8,128)(2,1)S(1)}, bf16[64,512]{1,0:T(8,128)(2,1)S(1)}, u32[]{:S(2)}, u32[]{:S(2)}) collective-permute-start(bf16[64,512]{1,0:T(8,128)(2,1)S(1)} %get-tuple-element.29), channel_id=1, source_target_pairs={{8,16},{16,8},{9,17},{17,9},{10,18},{18,10},{11,19},{19,11},{12,20... | collective-permute-start | bytes 196616 | tf_op jit(solution)/shard_map/ppermute | solution.py:389
  139.1 3.3 %collective-permute-start.25 = (f32[8,128]{1,0:T(8,128)S(1)}, f32[8,128]{1,0:T(8,128)S(1)}, u32[]{:S(2)}, u32[]{:S(2)}) collective-permute-start(f32[8,128]{1,0:T(8,128)S(1)} %products.1), channel_id=1, source_target_pairs={{0,1},{1,0},{2,3},{3,2},{4,5},{5,4},{6,7},{7,6},{8,9},{9,8},{10,11... | collective-permute-start | bytes 12296 | tf_op jit(solution)/shard_map/ppermute | solution.py:18
  142.3 2.5 %collective-permute-start.26 = (f32[8,128]{1,0:T(8,128)S(1)}, f32[8,128]{1,0:T(8,128)S(1)}, u32[]{:S(2)}, u32[]{:S(2)}) collective-permute-start(f32[8,128]{1,0:T(8,128)S(1)} %add.12), channel_id=1, source_target_pairs={{0,2},{1,3},{2,0},{3,1},{4,6},{5,7},{6,4},{7,5},{8,10},{9,11},{10,... | collective-permute-start | bytes 12296 | tf_op jit(solution)/shard_map/ppermute | solution.py:18
  144.8 3.4 %collective-permute-start.27 = (f32[8,128]{1,0:T(8,128)S(1)}, f32[8,128]{1,0:T(8,128)S(1)}, u32[]{:S(2)}, u32[]{:S(2)}) collective-permute-start(f32[8,128]{1,0:T(8,128)S(1)} %add.13.one), channel_id=1, source_target_pairs={{0,4},{1,5},{2,6},{3,7},{4,0},{5,1},{6,2},{7,3},{8,12},{9,13},{10,... | collective-permute-start | bytes 12296 | tf_op jit(solution)/shard_map/ppermute | solution.py:18
where the time goes:
time: 151 us; the launch traced here: 149 us
  waiting for transfers between devices  82.4 us (55%)
  starting transfers between devices  32.7 us (22%)
  Pallas kernels  24.4 us (16%)
  local copies, waits for them, and re-layouts  8.33 us (6%)
    ppermute x27, waiting for transfers between devices, swap(): lax.ppermute(block, axis, [(i, i ^ mask) for i in range(lax.axis_size(axi...  78.7 us
    ppermute x27, starting transfers between devices, swap(): lax.ppermute(block, axis, [(i, i ^ mask) for i in range(lax.axis_size(axi...  30.6 us
    pallas_call x4, Pallas kernels, project(): pl.pallas_call(functools.partial(project_kernel, len(pieces), parts, len(...  9.55 us
    unnamed x15, local copies, waits for them, and re-layouts  8.33 us
    pallas_call x4, Pallas kernels, stage(): pl.pallas_call(functools.partial(stage_kernel, k), out_shape=jax.ShapeDty...  4.91 us
    pallas_call x2, Pallas kernels, deal(): pl.pallas_call(functools.partial(deal_kernel, width, rows), out_shape=(ha...  4.89 us
    ppermute x1, waiting for transfers between devices, local(): second = lax.ppermute(second, 'section', route + [(b, a) for a, b in route])  3.77 us
  transfers between devices with their start and end apart: 28, of which 15 were waited for; matrix products, arithmetic and copies ran while one was open for 1% of the time, Pallas kernels for 11%

commit v1 on v0

v1 whole, which is shorter than its diff:
```python
import functools

import jax
import jax.numpy as jnp
from jax import lax
from jax.experimental import pallas as pl
from jax.experimental.pallas import tpu as pltpu
from jax.sharding import PartitionSpec as P


F32, BF16 = jnp.float32, jnp.bfloat16
VMEM = pl.BlockSpec(memory_space=pltpu.VMEM)
HBM = pl.BlockSpec(memory_space=pltpu.HBM)


def swap(block, axis, mask):
    return lax.ppermute(block, axis, [(i, i ^ mask) for i in range(lax.axis_size(axis))])


def params(mib):
    return pltpu.CompilerParams(vmem_limit_bytes=int(mib * 1024) << 10)


def place():
    tok = lax.axis_index("tok")
    return tok >> 1, tok & 1, lax.axis_index("section")


def cost(flops, moved):
    return pl.CostEstimate(flops=int(flops), bytes_accessed=int(moved), transcendentals=0)


def deal_kernel(width, rows, proj, mine, give, block, sem):
    _, core, section = place()
    start = 0
    if rows < proj.shape[0]:
        start = pl.multiple_of((section % (proj.shape[0] // rows)) * rows, 16)
    copy = pltpu.make_async_copy(proj.at[pl.ds(start, rows), :], block, sem)
    copy.start()
    rank, half = proj.shape[1], mine.shape[1]
    row = lax.broadcasted_iota(jnp.int32, (rank, half), 0)
    col = lax.broadcasted_iota(jnp.int32, (rank, half), 1)
    first = (col // width) * (2 * width) + col % width
    picks = [
        jnp.where(row == first + side * width, 1.0, 0.0).astype(BF16) for side in (core, 1 - core)
    ]
    copy.wait()
    for out, pick in zip((mine, give), picks):
        out[...] = jnp.dot(block[...], pick, preferred_element_type=F32).astype(BF16)


def deal(proj, width, rows):
    rank = proj.shape[1]
    half = jax.ShapeDtypeStruct((rows, rank // 2), BF16)
    return pl.pallas_call(
        functools.partial(deal_kernel, width, rows),
        out_shape=(half, half),
        in_specs=[HBM],
        out_specs=(VMEM, VMEM),
        scratch_shapes=[pltpu.VMEM((rows, rank), BF16), pltpu.SemaphoreType.DMA],
        compiler_params=params(4),
        cost_estimate=cost(2 * rows * rank * rank, 4 * rows * rank),
        name="deal",
    )(proj)


def stage_kernel(k, source, out, sem):
    deep = out.shape[1]
    columns = pl.ds(pl.multiple_of((place()[0] ^ k) * deep, 128), deep)
    copy = pltpu.make_async_copy(source.at[:, columns], out, sem)
    copy.start()
    copy.wait()


def stage(source, k, deep):
    rows = source.shape[0]
    return pl.pallas_call(
        functools.partial(stage_kernel, k),
        out_shape=jax.ShapeDtypeStruct((rows, deep), BF16),
        in_specs=[HBM],
        out_specs=VMEM,
        scratch_shapes=[pltpu.SemaphoreType.DMA],
        compiler_params=params(3),
        cost_estimate=cost(4e9, 4 * rows * deep),
        name="stage",
    )(source)


def join_kernel(upper, lower, out):
    deep = upper.shape[0]
    out[:deep, :] = upper[...]
    out[deep:, :] = lower[...]


def join(upper, lower):
    deep, half = upper.shape
    return pl.pallas_call(
        join_kernel,
        out_shape=jax.ShapeDtypeStruct((2 * deep, half), BF16),
        in_specs=[VMEM, VMEM],
        out_specs=VMEM,
        compiler_params=params(2),
        cost_estimate=cost(1e6, 8 * deep * half),
        name="join",
    )(upper, lower)


def pick_kernel(parts, j, upper, lower, out):
    deep = out.shape[0] // 2
    rows = pl.ds(pl.multiple_of(((place()[2] % parts) ^ j) * deep, 16), deep)
    out[:deep, :] = upper[rows, :]
    out[deep:, :] = lower[rows, :]


def pick(upper, lower, parts, j):
    rows, half = upper.shape
    return pl.pallas_call(
        functools.partial(pick_kernel, parts, j),
        out_shape=jax.ShapeDtypeStruct((2 * rows // parts, half), BF16),
        in_specs=[VMEM, VMEM],
        out_specs=VMEM,
        compiler_params=params(4),
        cost_estimate=cost(1e6, 8 * rows * half // parts),
        name="pick",
    )(upper, lower)


def project_kernel(keys, parts, started, last, layers, acts, other, *refs):
    pieces, refs = refs[: len(keys)], refs[len(keys) :]
    total = refs[0] if started else None
    outs = refs[started:]
    _, core, section = place()
    part = section % parts
    block = acts.shape[1] // 2
    offs = []
    for j, piece in zip(keys, pieces):
        if j is None:
            offs += [(core * block, block)] if not offs else [((1 - core) * block, block)]
        else:
            deep = block // parts
            offs += [(side * block + (part ^ j) * deep, deep) for side in (core, 1 - core)]
    offs = [pl.ds(pl.multiple_of(at, 128), deep) for at, deep in offs]
    weights = jnp.concatenate([piece[...] for piece in pieces], axis=0)
    rows = acts.shape[0] // layers
    kept = []
    for side, source in enumerate((acts, other)):
        for layer in range(layers):
            span = pl.ds(layer * rows, rows)
            left = jnp.concatenate([source[span, columns] for columns in offs], axis=1)
            value = jnp.dot(left, weights, preferred_element_type=F32)
            if started:
                value = value + total[side, span, :]
            if last:
                kept.append(value)
            else:
                outs[0][side, span, :] = value
    if not last:
        return
    split, sums = outs
    sums[...] = jnp.zeros_like(sums)
    for layer in range(layers):
        values = [kept[layer], kept[layers + layer]]
        column = jnp.sum(values[0] + values[1], axis=0, keepdims=True)
        sums[layer : layer + 1, :] = column
        mean = column / (2 * rows)
        for side in range(2):
            span = pl.ds(layer * rows, rows)
            value = values[side] - mean
            high = value.astype(BF16)
            split[0, side, span, :] = high
            split[1, side, span, :] = (value - high.astype(F32)).astype(BF16)


def project(pieces, keys, parts, total, acts, other, layers, last):
    rows, half = acts.shape[0], pieces[0].shape[1]
    deep = sum(piece.shape[0] for piece in pieces)
    if last:
        out_shape = (
            jax.ShapeDtypeStruct((2, 2, rows, half), BF16),
            jax.ShapeDtypeStruct((8, half), F32),
        )
        out_specs = (VMEM, VMEM)
    else:
        out_shape = jax.ShapeDtypeStruct((2, rows, half), F32)
        out_specs = VMEM
    started = [] if total is None else [total]
    return pl.pallas_call(
        functools.partial(project_kernel, keys, parts, len(started), last, layers),
        out_shape=out_shape,
        in_specs=[VMEM] * (2 + len(pieces) + len(started)),
        out_specs=out_specs,
        compiler_params=params(10),
        cost_estimate=cost(4 * rows * deep * half, 4 * rows * deep),
        name="project",
    )(acts, other, *pieces, *started)


def exponent(value):
    top = jnp.max(jnp.abs(value), axis=(0, 1), keepdims=True)
    return jnp.ceil(jnp.log2(jnp.maximum(top, 1e-30))) - 14.0


def gram_kernel(layers, chips, own, oth, own_sums, oth_sums, *outs):
    chip = place()[0]
    half = own.shape[3]
    rows = own.shape[2] // layers
    width = half // chips
    along_tokens = (((0,), (0,)), ((), ()))
    sums = jnp.concatenate([own_sums[...], oth_sums[...]], axis=1)
    tail = []
    for layer in range(layers):
        span = pl.ds(layer * rows, rows)
        left, right = [], []
        for part in range(2):
            here = jnp.concatenate([own[part, 0, span, :], own[part, 1, span, :]], axis=0)
            there = jnp.concatenate([oth[part, 1, span, :], oth[part, 0, span, :]], axis=0)
            left.append(here)
            right.append(jnp.concatenate([here, there], axis=1))
        gram = sum(
            lax.dot_general(left[i], right[j], along_tokens, preferred_element_type=F32)
            for i, j in ((0, 0), (0, 1), (1, 0))
        )
        power = exponent(gram)
        gram = gram * jnp.exp2(-power)
        blocks = [gram[i * width : (i + 1) * width] for i in range(chips)]
        for k, out in enumerate(outs):
            block = blocks[k]
            for i in range(1, chips):
                block = jnp.where(chip == i, blocks[i ^ k], block)
            out[layer * width : (layer + 1) * width, :] = block
        column = sums[layer : layer + 1]
        lift = exponent(column)
        column = column * jnp.exp2(-lift)
        high = column.astype(BF16).astype(F32)
        middle = (column - high).astype(BF16).astype(F32)
        line = jnp.zeros_like(column)
        tail += [high, middle, column - high - middle, line + power, line + lift]
    for out in outs:
        out[layers * width :, :] = jnp.zeros_like(out[layers * width :, :])
        for n, line in enumerate(tail):
            out[layers * width + n : layers * width + n + 1, :] = line


def tail_rows(layers):
    return -(-5 * layers // 16) * 16


def gram(own, oth, own_sums, oth_sums, layers, chips):
    rows, half = own.shape[2:]
    height = layers * (half // chips) + tail_rows(layers)
    message = jax.ShapeDtypeStruct((height, 2 * half), F32)
    return pl.pallas_call(
        functools.partial(gram_kernel, layers, chips),
        out_shape=(message,) * chips,
        in_specs=[VMEM] * 4,
        out_specs=(VMEM,) * chips,
        compiler_params=params(10),
        cost_estimate=cost(24 * rows * half * half, 16 * rows * half),
        name="gram",
    )(own, oth, own_sums, oth_sums)


def finish_kernel(layers, tokens, *refs):
    messages, (sketch, turned, first_out, second_out) = refs[:-4], refs[-4:]
    chips = len(messages)
    chip, core, section = place()
    rank = messages[0].shape[1]
    width = (messages[0].shape[0] - tail_rows(layers)) // layers
    half = rank // 2
    here = lax.broadcasted_iota(jnp.int32, (width, rank), 1)
    here = here == lax.broadcasted_iota(jnp.int32, (width, rank), 0) + chip * width
    kept = []
    for layer in range(layers):
        span = slice(layer * width, (layer + 1) * width)
        at = layers * width + 5 * layer
        value, sums = 0.0, []
        for message in messages:
            line = [message[at + n : at + n + 1, :] for n in range(5)]
            value = value + message[span, :] * jnp.exp2(line[3])
            sums.append((line[0] + line[1] + line[2]) * jnp.exp2(line[4]))
        mean = sum(sums) / tokens
        for total in sums:
            drift = total / (tokens // chips) - mean
            lifted = jnp.sum(jnp.where(here, drift, 0.0), axis=1, keepdims=True)
            value = value + (tokens // chips) * lifted * drift
        turned[layer] = value
        kept.append(value)
        flipped = value.T
        for i in range(chips):
            for side in range(2):
                at = side * half + i * width
                to = 2 * width * i + width * (core if side == 0 else 1 - core)
                rows = pl.ds(pl.multiple_of(to, 8), width)
                sketch[layer, rows, :] = flipped[at : at + width]
    odd = section % 2 == 1
    first_out[...] = jnp.where(odd, kept[0], kept[-1]).astype(BF16)
    second_out[...] = jnp.where(odd, kept[-1], kept[0]).astype(BF16)


def finish(messages, layers, tokens):
    height, rank = messages[0].shape
    width = (height - tail_rows(layers)) // layers
    edge = jax.ShapeDtypeStruct((width, rank), BF16)
    return pl.pallas_call(
        functools.partial(finish_kernel, layers, tokens),
        out_shape=(
            jax.ShapeDtypeStruct((layers, rank, width), F32),
            jax.ShapeDtypeStruct((layers, width, rank), F32),
            edge,
            edge,
        ),
        in_specs=[VMEM] * len(messages),
        out_specs=(VMEM,) * 4,
        compiler_params=params(6),
        cost_estimate=cost(1e6, 2e6),
        name="finish",
    )(*messages)


def products_kernel(layers, sections, turned, one, two, out):
    section = place()[2]
    odd = section % 2 == 1
    one, two = one[...].astype(F32), two[...].astype(F32)
    rows = [turned[i] for i in range(layers)]
    before = jnp.where(section == 0, rows[0], jnp.where(odd, one, two))
    beyond = jnp.where(section == sections - 1, rows[-1], jnp.where(odd, two, one))
    pairs = [(before, before)] + [(row, row) for row in rows] + [(beyond, beyond)]
    chain = [before] + rows + [beyond]
    pairs += list(zip(chain[:-1], chain[1:]))
    out[...] = jnp.zeros_like(out)
    for n, (a, b) in enumerate(pairs):
        out[n : n + 1, :] = jnp.full((1, out.shape[1]), jnp.sum(a * b), F32)


def products(turned, one, two, sections):
    layers = turned.shape[0]
    count = -(-(2 * layers + 3) // 8) * 8
    return pl.pallas_call(
        functools.partial(products_kernel, layers, sections),
        out_shape=jax.ShapeDtypeStruct((count, 128), F32),
        in_specs=[VMEM] * 3,
        out_specs=VMEM,
        compiler_params=params(4),
        cost_estimate=cost(1e6, 1e6),
        name="products",
    )(turned, one, two)


def ratios_kernel(layers, one, two, out):
    value = one[...] + two[...]
    squares = value[: layers + 2]
    chained = value[layers + 2 : 2 * layers + 3]
    ratio = chained / jnp.sqrt(squares[:-1] * squares[1:])
    out[:, 0:1] = ratio[:-1, 0:1]
    out[:, 1:2] = ratio[1:, 0:1]


def ratios(one, two, layers):
    return pl.pallas_call(
        functools.partial(ratios_kernel, layers),
        out_shape=jax.ShapeDtypeStruct((layers, 2), F32),
        in_specs=[VMEM] * 2,
        out_specs=VMEM,
        compiler_params=params(4),
        cost_estimate=cost(1e4, 1e4),
        name="ratios",
    )(one, two)


def local(activations, projection):
    layers, tok_rows, model = activations.shape
    block, rank = projection.shape
    groups, sections = lax.axis_size("tok"), lax.axis_size("section")
    chips, width = groups // 2, rank // groups
    parts = min(sections, max(1, block // 128))
    deep = block // parts

    acts = activations.reshape(layers * tok_rows, model)
    mine_part, give_part = deal(projection, width, deep)
    got_part = swap(give_part, "tok", 1)
    own = join(mine_part, got_part)

    fetched = {}
    for k in range(1, chips):
        low = k & -k
        fetched[k] = swap(own if k == low else fetched[k ^ low], "tok", 2 * low)

    mine, give = deal(projection, width, block)
    got = swap(give, "tok", 1)

    order = sorted(fetched, key=lambda k: (bin(k).count("1"), k))
    staged = {}
    for k in [0] + order:
        staged[k] = stage(acts, k, 2 * block)
        staged[k] = (staged[k], swap(staged[k], "tok", 1))

    far = {j: pick(mine, got, parts, j) for j in range(1, parts) if j & (j - 1)}
    pieces = {0: {}}
    for k in order:
        pieces[k] = {0: fetched[k]}
        for j in range(1, parts):
            if 1 < k == k & -k and j in far:
                pieces[k][j] = swap(far[j], "tok", 2 * k)
            else:
                pieces[k][j] = swap(fetched[k], "section", j)

    total = project([mine, got], (None, None), parts, None, *staged[0], layers, False)
    final, keys = order[-1], tuple(range(parts))
    steps = [(k, keys) for k in order[:-2]]
    steps += [(final, keys[:-1])] + [(k, keys) for k in order[-2:-1]] + [(final, keys[-1:])]
    steps = [step for step in steps if step[1]]
    for k, js in steps:
        last = (k, js) == steps[-1]
        chosen = [pieces[k][j] for j in js]
        total = project(chosen, js, parts, total, *staged[k], layers, last)
    split, sums = total

    messages = gram(split, swap(split, "tok", 1), sums, swap(sums, "tok", 1), layers, chips)
    arrived = [messages[0]]
    for k in reversed(range(1, chips)):
        arrived.append(swap(messages[k].astype(jnp.float16), "tok", 2 * k).astype(F32))
    sketch, turned, first, second = finish(arrived, layers, tok_rows * groups)

    first = swap(first, "section", 1)
    route = [(i, i + 1) for i in range(1, sections - 1, 2)]
    second = lax.ppermute(second, "section", route + [(b, a) for a, b in route])
    value = products(turned, first, second, sections)
    mask = 1
    while 2 * mask < groups:
        value = value + swap(value, "tok", mask)
        mask *= 2
    return sketch, ratios(value, swap(value, "tok", mask), layers)


def solution(mesh):
    return jax.shard_map(
        local,
        mesh=mesh,
        in_specs=(P("section", "tok", None), P("tok", None)),
        out_specs=(P("section", None, "tok"), P("section", None)),
        check_vma=False,
    )
```

time: 151 us -> 135 us (0.89)
  the two profiles are of different devices: /device:TPU:5 before, /device:TPU:2 now
where the time goes in v1:
time: 135 us
  waiting for transfers between devices  90.1 us (67%)
  starting transfers between devices  26.9 us (20%)
  Pallas kernels  11.6 us (9%)
  local copies, waits for them, and re-layouts  5.32 us (4%)
    ppermute x27, waiting for transfers between devices, swap(): lax.ppermute(block, axis, [(i, i ^ mask) for i in range(lax.axis_size(axi...  85.3 us
    ppermute x27, starting transfers between devices, swap(): lax.ppermute(block, axis, [(i, i ^ mask) for i in range(lax.axis_size(axi...  25 us
    pallas_call x5, Pallas kernels, project(): pl.pallas_call(functools.partial(project_kernel, keys, parts, len(started...  5.43 us
    unnamed x7, local copies, waits for them, and re-layouts  5.32 us
    ppermute x1, waiting for transfers between devices, local(): second = lax.ppermute(second, 'section', route + [(b, a) for a, b in route])  4.79 us
  transfers between devices with their start and end apart: 28, of which 18 were waited for; matrix products, arithmetic and copies ran while one was open for 1% of the time, Pallas kernels for 6%

profile of v1, /device:TPU:2, one launch (start us, length us, event | category | flops | bytes accessed | tf_op | source)
XLA Modules:
  0.0 134.9 jit_solution(2575690270344525505)
XLA Ops:
  0.6 3.4 %copy-done.1 = bf16[2,256,8192]{2,1,0:T(8,128)(2,1)S(1)} copy-done((bf16[2,256,8192]{2,1,0:T(8,128)(2,1)S(1)}, bf16[2,256,8192]{2,1,0:T(8,128)(2,1)}, u32[]{:S(2)}) %copy-start.1) | copy-done | bytes 8388632
  4.0 0.5 stage.7.acts
  4.6 0.6 copy-done
  5.2 0.9 deal.3
  6.8 0.5 collective-permute-start.1
  7.7 0.5 stage.6.acts
  8.3 1.4 %collective-permute-done.1.lower = bf16[256,256]{1,0:T(8,128)(2,1)S(1)} collective-permute-done((bf16[256,256]{1,0:T(8,128)(2,1)S(1)}, bf16[256,256]{1,0:T(8,128)(2,1)S(1)}, u32[]{:S(2)}, u32[]{:S(2)}) %collective-permute-start.1) | collective-permute-done | bytes 131104 | tf_op jit(solution)/shard_map/ppermute | solution.py:17
  9.7 1.6 %collective-permute-start.13 = (bf16[512,256]{1,0:T(8,128)(2,1)S(1)}, bf16[512,256]{1,0:T(8,128)(2,1)S(1)}, u32[]{:S(2)}, u32[]{:S(2)}) collective-permute-start(bf16[512,256]{1,0:T(8,128)(2,1)S(1)} %join.1), channel_id=1, source_target_pairs={{0,2},{1,3},{2,0},{3,1},{4,6},{5,7},{6,4},{7,5},{8,10},{9,11},{10,... | collective-permute-start | bytes 786440 | tf_op jit(solution)/shard_map/ppermute | solution.py:17
  11.4 0.5 stage.4.acts
  12.0 6.2 %collective-permute-done.13.refs_0_ = bf16[512,256]{1,0:T(8,128)(2,1)S(1)} collective-permute-done((bf16[512,256]{1,0:T(8,128)(2,1)S(1)}, bf16[512,256]{1,0:T(8,128)(2,1)S(1)}, u32[]{:S(2)}, u32[]{:S(2)}) %collective-permute-start.13) | collective-permute-done | bytes 262176 | tf_op jit(solution)/shard_map/ppermute | solution.py:17
  18.1 2.6 %collective-permute-start.2 = (bf16[512,256]{1,0:T(8,128)(2,1)S(1)}, bf16[512,256]{1,0:T(8,128)(2,1)S(1)}, u32[]{:S(2)}, u32[]{:S(2)}) collective-permute-start(bf16[512,256]{1,0:T(8,128)(2,1)S(1)} %join.1), channel_id=1, source_target_pairs={{0,4},{1,5},{2,6},{3,7},{4,0},{5,1},{6,2},{7,3},{8,12},{9,13},{10,... | collective-permute-start | bytes 786440 | tf_op jit(solution)/shard_map/ppermute | solution.py:17
  20.7 0.5 stage.5.acts
  21.2 10.9 %collective-permute-done.2.refs_0_ = bf16[512,256]{1,0:T(8,128)(2,1)S(1)} collective-permute-done((bf16[512,256]{1,0:T(8,128)(2,1)S(1)}, bf16[512,256]{1,0:T(8,128)(2,1)S(1)}, u32[]{:S(2)}, u32[]{:S(2)}) %collective-permute-start.2) | collective-permute-done | bytes 262176 | tf_op jit(solution)/shard_map/ppermute | solution.py:17
  32.2 0.7 collective-permute-start.14
  32.8 8.1 %collective-permute-done.14.refs_1_ = bf16[512,256]{1,0:T(8,128)(2,1)S(1)} collective-permute-done((bf16[512,256]{1,0:T(8,128)(2,1)S(1)}, bf16[512,256]{1,0:T(8,128)(2,1)S(1)}, u32[]{:S(2)}, u32[]{:S(2)}) %collective-permute-start.14) | collective-permute-done | bytes 262176 | tf_op jit(solution)/shard_map/ppermute | solution.py:17
  40.9 1.5 %collective-permute-start.15 = (bf16[512,256]{1,0:T(8,128)(2,1)S(1)}, bf16[512,256]{1,0:T(8,128)(2,1)S(1)}, u32[]{:S(2)}, u32[]{:S(2)}) collective-permute-start(bf16[512,256]{1,0:T(8,128)(2,1)S(1)} %collective-permute-done.13.refs_0_), channel_id=1, source_target_pairs={{0,16},{8,24},{16,0},{24,8},{1,17},{9,25},{17,1},{25,9},{2,18},{10... | collective-permute-start | bytes 786440 | tf_op jit(solution)/shard_map/ppermute | solution.py:17
  42.4 6.3 %collective-permute-done.15.refs_2_ = bf16[512,256]{1,0:T(8,128)(2,1)S(1)} collective-permute-done((bf16[512,256]{1,0:T(8,128)(2,1)S(1)}, bf16[512,256]{1,0:T(8,128)(2,1)S(1)}, u32[]{:S(2)}, u32[]{:S(2)}) %collective-permute-start.15) | collective-permute-done | bytes 262176 | tf_op jit(solution)/shard_map/ppermute | solution.py:17
  48.7 1.5 %collective-permute-start.16 = (bf16[512,256]{1,0:T(8,128)(2,1)S(1)}, bf16[512,256]{1,0:T(8,128)(2,1)S(1)}, u32[]{:S(2)}, u32[]{:S(2)}) collective-permute-start(bf16[512,256]{1,0:T(8,128)(2,1)S(1)} %collective-permute-done.13.refs_0_), channel_id=1, source_target_pairs={{0,24},{8,16},{16,8},{24,0},{1,25},{9,17},{17,9},{25,1},{2,26},{10... | collective-permute-start | bytes 786440 | tf_op jit(solution)/shard_map/ppermute | solution.py:17
  50.2 6.4 %collective-permute-done.16.refs_3_ = bf16[512,256]{1,0:T(8,128)(2,1)S(1)} collective-permute-done((bf16[512,256]{1,0:T(8,128)(2,1)S(1)}, bf16[512,256]{1,0:T(8,128)(2,1)S(1)}, u32[]{:S(2)}, u32[]{:S(2)}) %collective-permute-start.16) | collective-permute-done | bytes 262176 | tf_op jit(solution)/shard_map/ppermute | solution.py:17
  56.6 0.6 collective-permute-start.3
  57.3 5.7 %collective-permute-done.3.refs_0_ = bf16[512,256]{1,0:T(8,128)(2,1)S(1)} collective-permute-done((bf16[512,256]{1,0:T(8,128)(2,1)S(1)}, bf16[512,256]{1,0:T(8,128)(2,1)S(1)}, u32[]{:S(2)}, u32[]{:S(2)}) %collective-permute-start.3) | collective-permute-done | bytes 262176 | tf_op jit(solution)/shard_map/ppermute | solution.py:17
  63.0 0.7 collective-permute-start.10
  63.7 5.7 %collective-permute-done.10.refs_1_ = bf16[512,256]{1,0:T(8,128)(2,1)S(1)} collective-permute-done((bf16[512,256]{1,0:T(8,128)(2,1)S(1)}, bf16[512,256]{1,0:T(8,128)(2,1)S(1)}, u32[]{:S(2)}, u32[]{:S(2)}) %collective-permute-start.10) | collective-permute-done | bytes 262176 | tf_op jit(solution)/shard_map/ppermute | solution.py:17
  69.4 1.5 %collective-permute-start.11 = (bf16[512,256]{1,0:T(8,128)(2,1)S(1)}, bf16[512,256]{1,0:T(8,128)(2,1)S(1)}, u32[]{:S(2)}, u32[]{:S(2)}) collective-permute-start(bf16[512,256]{1,0:T(8,128)(2,1)S(1)} %collective-permute-done.3.refs_0_), channel_id=1, source_target_pairs={{0,16},{8,24},{16,0},{24,8},{1,17},{9,25},{17,1},{25,9},{2,18},{10... | collective-permute-start | bytes 786440 | tf_op jit(solution)/shard_map/ppermute | solution.py:17
  70.9 9.2 %collective-permute-done.11.refs_2_ = bf16[512,256]{1,0:T(8,128)(2,1)S(1)} collective-permute-done((bf16[512,256]{1,0:T(8,128)(2,1)S(1)}, bf16[512,256]{1,0:T(8,128)(2,1)S(1)}, u32[]{:S(2)}, u32[]{:S(2)}) %collective-permute-start.11) | collective-permute-done | bytes 262176 | tf_op jit(solution)/shard_map/ppermute | solution.py:17
  80.1 2.6 %collective-permute-start.7 = (bf16[512,256]{1,0:T(8,128)(2,1)S(1)}, bf16[512,256]{1,0:T(8,128)(2,1)S(1)}, u32[]{:S(2)}, u32[]{:S(2)}) collective-permute-start(bf16[512,256]{1,0:T(8,128)(2,1)S(1)} %collective-permute-done.2.refs_0_), channel_id=1, source_target_pairs={{0,16},{8,24},{16,0},{24,8},{1,17},{9,25},{17,1},{25,9},{2,18},{10... | collective-permute-start | bytes 786440 | tf_op jit(solution)/shard_map/ppermute | solution.py:17
  82.7 1.5 %collective-permute-start.9 = (bf16[512,256]{1,0:T(8,128)(2,1)S(1)}, bf16[512,256]{1,0:T(8,128)(2,1)S(1)}, u32[]{:S(2)}, u32[]{:S(2)}) collective-permute-start(bf16[512,256]{1,0:T(8,128)(2,1)S(1)} %pick.1), channel_id=1, source_target_pairs={{0,4},{1,5},{2,6},{3,7},{4,0},{5,1},{6,2},{7,3},{8,12},{9,13},{10,... | collective-permute-start | bytes 786440 | tf_op jit(solution)/shard_map/ppermute | solution.py:17
  84.2 1.2 project.5.refs_4_
  85.5 2.0 %collective-permute-start.4 = (bf16[512,256]{1,0:T(8,128)(2,1)S(1)}, bf16[512,256]{1,0:T(8,128)(2,1)S(1)}, u32[]{:S(2)}, u32[]{:S(2)}) collective-permute-start(bf16[512,256]{1,0:T(8,128)(2,1)S(1)} %collective-permute-done.3.refs_0_), channel_id=1, source_target_pairs={{0,24},{8,16},{16,8},{24,0},{1,25},{9,17},{17,9},{25,1},{2,26},{10... | collective-permute-start | bytes 786440 | tf_op jit(solution)/shard_map/ppermute | solution.py:17
  87.5 1.3 project.6.refs_3_
  88.8 1.0 project.7.refs_4_
  89.8 3.0 %collective-permute-done.9.refs_3_ = bf16[512,256]{1,0:T(8,128)(2,1)S(1)} collective-permute-done((bf16[512,256]{1,0:T(8,128)(2,1)S(1)}, bf16[512,256]{1,0:T(8,128)(2,1)S(1)}, u32[]{:S(2)}, u32[]{:S(2)}) %collective-permute-start.9) | collective-permute-done | bytes 262176 | tf_op jit(solution)/shard_map/ppermute | solution.py:17
  92.8 1.3 project.8.refs_1_
  94.1 0.7 project.9
  95.4 2.2 %collective-permute-done.19.oth_sums = f32[8,256]{1,0:T(8,128)S(1)} collective-permute-done((f32[8,256]{1,0:T(8,128)S(1)}, f32[8,256]{1,0:T(8,128)S(1)}, u32[]{:S(2)}, u32[]{:S(2)}) %collective-permute-start.19) | collective-permute-done | bytes 8224 | tf_op jit(solution)/shard_map/ppermute | solution.py:17
  97.5 1.3 gram.1
  98.9 2.5 %collective-permute-start.20 = (f16[144,512]{1,0:T(8,128)(2,1)S(1)}, f16[144,512]{1,0:T(8,128)(2,1)S(1)}, u32[]{:S(2)}, u32[]{:S(2)}) collective-permute-start(f16[144,512]{1,0:T(8,128)(2,1)S(1)} %convert_element_type.18), channel_id=1, source_target_pairs={{0,6},{1,7},{2,4},{3,5},{4,2},{5,3},{6,0},{7,1},{8,14},{9,15},{10,... | collective-permute-start | bytes 442376 | tf_op jit(solution)/shard_map/ppermute | solution.py:17
  101.8 1.7 %collective-permute-start.22 = (f16[144,512]{1,0:T(8,128)(2,1)S(1)}, f16[144,512]{1,0:T(8,128)(2,1)S(1)}, u32[]{:S(2)}, u32[]{:S(2)}) collective-permute-start(f16[144,512]{1,0:T(8,128)(2,1)S(1)} %convert_element_type.22), channel_id=1, source_target_pairs={{0,2},{1,3},{2,0},{3,1},{4,6},{5,7},{6,4},{7,5},{8,10},{9,11},{10,... | collective-permute-start | bytes 442376 | tf_op jit(solution)/shard_map/ppermute | solution.py:17
  103.5 4.1 %collective-permute-done.20 = f16[144,512]{1,0:T(8,128)(2,1)S(1)} collective-permute-done((f16[144,512]{1,0:T(8,128)(2,1)S(1)}, f16[144,512]{1,0:T(8,128)(2,1)S(1)}, u32[]{:S(2)}, u32[]{:S(2)}) %collective-permute-start.20) | collective-permute-done | bytes 147488 | tf_op jit(solution)/shard_map/ppermute | solution.py:17
  107.7 7.4 %collective-permute-done.21 = f16[144,512]{1,0:T(8,128)(2,1)S(1)} collective-permute-done((f16[144,512]{1,0:T(8,128)(2,1)S(1)}, f16[144,512]{1,0:T(8,128)(2,1)S(1)}, u32[]{:S(2)}, u32[]{:S(2)}) %collective-permute-start.21) | collective-permute-done | bytes 147488 | tf_op jit(solution)/shard_map/ppermute | solution.py:17
  115.6 2.1 %collective-permute-start.23 = (bf16[64,512]{1,0:T(8,128)(2,1)S(1)}, bf16[64,512]{1,0:T(8,128)(2,1)S(1)}, u32[]{:S(2)}, u32[]{:S(2)}) collective-permute-start(bf16[64,512]{1,0:T(8,128)(2,1)S(1)} %get-tuple-element.28), channel_id=1, source_target_pairs={{0,8},{8,0},{16,24},{24,16},{1,9},{9,1},{17,25},{25,17},{2,10},{10... | collective-permute-start | bytes 196616 | tf_op jit(solution)/shard_map/ppermute | solution.py:17
  117.6 1.9 %collective-permute-start.24 = (bf16[64,512]{1,0:T(8,128)(2,1)S(1)}, bf16[64,512]{1,0:T(8,128)(2,1)S(1)}, u32[]{:S(2)}, u32[]{:S(2)}) collective-permute-start(bf16[64,512]{1,0:T(8,128)(2,1)S(1)} %get-tuple-element.29), channel_id=1, source_target_pairs={{8,16},{16,8},{9,17},{17,9},{10,18},{18,10},{11,19},{19,11},{12,20... | collective-permute-start | bytes 196616 | tf_op jit(solution)/shard_map/ppermute | solution.py:426
  119.9 4.8 %collective-permute-done.24.two = bf16[64,512]{1,0:T(8,128)(2,1)S(1)} collective-permute-done((bf16[64,512]{1,0:T(8,128)(2,1)S(1)}, bf16[64,512]{1,0:T(8,128)(2,1)S(1)}, u32[]{:S(2)}, u32[]{:S(2)}) %collective-permute-start.24) | collective-permute-done | bytes 65568 | tf_op jit(solution)/shard_map/ppermute | solution.py:426
  125.0 1.2 collective-permute-done.25
  126.2 3.6 %collective-permute-done.26 = f32[8,128]{1,0:T(8,128)S(1)} collective-permute-done((f32[8,128]{1,0:T(8,128)S(1)}, f32[8,128]{1,0:T(8,128)S(1)}, u32[]{:S(2)}, u32[]{:S(2)}) %collective-permute-start.26) | collective-permute-done | bytes 4128 | tf_op jit(solution)/shard_map/ppermute | solution.py:17
  129.8 0.9 copy.4
  130.7 3.6 %collective-permute-done.27.two = f32[8,128]{1,0:T(8,128)S(1)} collective-permute-done((f32[8,128]{1,0:T(8,128)S(1)}, f32[8,128]{1,0:T(8,128)S(1)}, u32[]{:S(2)}, u32[]{:S(2)}) %collective-permute-start.27) | collective-permute-done | bytes 4128 | tf_op jit(solution)/shard_map/ppermute | solution.py:17
  134.3 0.6 ratios.1
  (40 shorter events, 3.5 us)
Async XLA Ops:
  0.6 3.4 %copy-start.1 = (bf16[2,256,8192]{2,1,0:T(8,128)(2,1)S(1)}, bf16[2,256,8192]{2,1,0:T(8,128)(2,1)}, u32[]{:S(2)}) copy-start(bf16[2,256,8192]{2,1,0:T(8,128)(2,1)} %param.2) | copy-start | bytes 25165828
  4.0 1.2 copy-start
  4.0 3.7 %copy-start.2 = (bf16[2,256,8192]{2,1,0:T(8,128)(2,1)S(1)}, bf16[2,256,8192]{2,1,0:T(8,128)(2,1)}, u32[]{:S(2)}) copy-start(bf16[2,256,8192]{2,1,0:T(8,128)(2,1)} %param.2) | copy-start | bytes 25165828
  4.5 75.6 %collective-permute-start.17 = (bf16[512,2048]{1,0:T(8,128)(2,1)S(1)}, bf16[512,2048]{1,0:T(8,128)(2,1)S(1)}, u32[]{:S(2)}, u32[]{:S(2)}) collective-permute-start(bf16[512,2048]{1,0:T(8,128)(2,1)S(1)} %stage.7.acts), channel_id=1, source_target_pairs={{0,1},{1,0},{2,3},{3,2},{4,5},{5,4},{6,7},{7,6},{8,9},{9,8},{10,11... | collective-permute-start | bytes 6291464 | tf_op jit(solution)/shard_map/ppermute | solution.py:17
  6.2 26.0 %collective-permute-start.8 = (bf16[1024,256]{1,0:T(8,128)(2,1)S(1)}, bf16[1024,256]{1,0:T(8,128)(2,1)S(1)}, u32[]{:S(2)}, u32[]{:S(2)}) collective-permute-start(bf16[1024,256]{1,0:T(8,128)(2,1)S(1)} %get-tuple-element.19), channel_id=1, source_target_pairs={{0,1},{1,0},{2,3},{3,2},{4,5},{5,4},{6,7},{7,6},{8,9},{9,8},{10,11... | collective-permute-start | bytes 1572872 | tf_op jit(solution)/shard_map/ppermute | solution.py:17
  6.8 2.9 %collective-permute-start.1 = (bf16[256,256]{1,0:T(8,128)(2,1)S(1)}, bf16[256,256]{1,0:T(8,128)(2,1)S(1)}, u32[]{:S(2)}, u32[]{:S(2)}) collective-permute-start(bf16[256,256]{1,0:T(8,128)(2,1)S(1)} %get-tuple-element.17), channel_id=1, source_target_pairs={{0,1},{1,0},{2,3},{3,2},{4,5},{5,4},{6,7},{7,6},{8,9},{9,8},{10,11... | collective-permute-start | bytes 393224 | tf_op jit(solution)/shard_map/ppermute | solution.py:17
  8.3 74.5 %collective-permute-start.12 = (bf16[512,2048]{1,0:T(8,128)(2,1)S(1)}, bf16[512,2048]{1,0:T(8,128)(2,1)S(1)}, u32[]{:S(2)}, u32[]{:S(2)}) collective-permute-start(bf16[512,2048]{1,0:T(8,128)(2,1)S(1)} %stage.6.acts), channel_id=1, source_target_pairs={{0,1},{1,0},{2,3},{3,2},{4,5},{5,4},{6,7},{7,6},{8,9},{9,8},{10,11... | collective-permute-start | bytes 6291464 | tf_op jit(solution)/shard_map/ppermute | solution.py:17
  9.7 8.4 %collective-permute-start.13 = (bf16[512,256]{1,0:T(8,128)(2,1)S(1)}, bf16[512,256]{1,0:T(8,128)(2,1)S(1)}, u32[]{:S(2)}, u32[]{:S(2)}) collective-permute-start(bf16[512,256]{1,0:T(8,128)(2,1)S(1)} %join.1), channel_id=1, source_target_pairs={{0,2},{1,3},{2,0},{3,1},{4,6},{5,7},{6,4},{7,5},{8,10},{9,11},{10,... | collective-permute-start | bytes 786440 | tf_op jit(solution)/shard_map/ppermute | solution.py:17
  11.9 73.6 %collective-permute-start = (bf16[512,2048]{1,0:T(8,128)(2,1)S(1)}, bf16[512,2048]{1,0:T(8,128)(2,1)S(1)}, u32[]{:S(2)}, u32[]{:S(2)}) collective-permute-start(bf16[512,2048]{1,0:T(8,128)(2,1)S(1)} %stage.4.acts), channel_id=1, source_target_pairs={{0,1},{1,0},{2,3},{3,2},{4,5},{5,4},{6,7},{7,6},{8,9},{9,8},{10,11... | collective-permute-start | bytes 6291464 | tf_op jit(solution)/shard_map/ppermute | solution.py:17
  18.1 14.0 %collective-permute-start.2 = (bf16[512,256]{1,0:T(8,128)(2,1)S(1)}, bf16[512,256]{1,0:T(8,128)(2,1)S(1)}, u32[]{:S(2)}, u32[]{:S(2)}) collective-permute-start(bf16[512,256]{1,0:T(8,128)(2,1)S(1)} %join.1), channel_id=1, source_target_pairs={{0,4},{1,5},{2,6},{3,7},{4,0},{5,1},{6,2},{7,3},{8,12},{9,13},{10,... | collective-permute-start | bytes 786440 | tf_op jit(solution)/shard_map/ppermute | solution.py:17
  32.1 60.7 %collective-permute-start.5 = (bf16[512,2048]{1,0:T(8,128)(2,1)S(1)}, bf16[512,2048]{1,0:T(8,128)(2,1)S(1)}, u32[]{:S(2)}, u32[]{:S(2)}) collective-permute-start(bf16[512,2048]{1,0:T(8,128)(2,1)S(1)} %stage.5.acts), channel_id=1, source_target_pairs={{0,1},{1,0},{2,3},{3,2},{4,5},{5,4},{6,7},{7,6},{8,9},{9,8},{10,11... | collective-permute-start | bytes 6291464 | tf_op jit(solution)/shard_map/ppermute | solution.py:17
  32.2 8.7 %collective-permute-start.14 = (bf16[512,256]{1,0:T(8,128)(2,1)S(1)}, bf16[512,256]{1,0:T(8,128)(2,1)S(1)}, u32[]{:S(2)}, u32[]{:S(2)}) collective-permute-start(bf16[512,256]{1,0:T(8,128)(2,1)S(1)} %collective-permute-done.13.refs_0_), channel_id=1, source_target_pairs={{0,8},{8,0},{16,24},{24,16},{1,9},{9,1},{17,25},{25,17},{2,10},{10... | collective-permute-start | bytes 786440 | tf_op jit(solution)/shard_map/ppermute | solution.py:17
  40.9 7.9 %collective-permute-start.15 = (bf16[512,256]{1,0:T(8,128)(2,1)S(1)}, bf16[512,256]{1,0:T(8,128)(2,1)S(1)}, u32[]{:S(2)}, u32[]{:S(2)}) collective-permute-start(bf16[512,256]{1,0:T(8,128)(2,1)S(1)} %collective-permute-done.13.refs_0_), channel_id=1, source_target_pairs={{0,16},{8,24},{16,0},{24,8},{1,17},{9,25},{17,1},{25,9},{2,18},{10... | collective-permute-start | bytes 786440 | tf_op jit(solution)/shard_map/ppermute | solution.py:17
  48.7 7.9 %collective-permute-start.16 = (bf16[512,256]{1,0:T(8,128)(2,1)S(1)}, bf16[512,256]{1,0:T(8,128)(2,1)S(1)}, u32[]{:S(2)}, u32[]{:S(2)}) collective-permute-start(bf16[512,256]{1,0:T(8,128)(2,1)S(1)} %collective-permute-done.13.refs_0_), channel_id=1, source_target_pairs={{0,24},{8,16},{16,8},{24,0},{1,25},{9,17},{17,9},{25,1},{2,26},{10... | collective-permute-start | bytes 786440 | tf_op jit(solution)/shard_map/ppermute | solution.py:17
  56.6 6.4 %collective-permute-start.3 = (bf16[512,256]{1,0:T(8,128)(2,1)S(1)}, bf16[512,256]{1,0:T(8,128)(2,1)S(1)}, u32[]{:S(2)}, u32[]{:S(2)}) collective-permute-start(bf16[512,256]{1,0:T(8,128)(2,1)S(1)} %collective-permute-done.2.refs_0_), channel_id=1, source_target_pairs={{0,2},{1,3},{2,0},{3,1},{4,6},{5,7},{6,4},{7,5},{8,10},{9,11},{10,... | collective-permute-start | bytes 786440 | tf_op jit(solution)/shard_map/ppermute | solution.py:17
  63.0 6.4 %collective-permute-start.10 = (bf16[512,256]{1,0:T(8,128)(2,1)S(1)}, bf16[512,256]{1,0:T(8,128)(2,1)S(1)}, u32[]{:S(2)}, u32[]{:S(2)}) collective-permute-start(bf16[512,256]{1,0:T(8,128)(2,1)S(1)} %collective-permute-done.3.refs_0_), channel_id=1, source_target_pairs={{0,8},{8,0},{16,24},{24,16},{1,9},{9,1},{17,25},{25,17},{2,10},{10... | collective-permute-start | bytes 786440 | tf_op jit(solution)/shard_map/ppermute | solution.py:17
  69.4 10.7 %collective-permute-start.11 = (bf16[512,256]{1,0:T(8,128)(2,1)S(1)}, bf16[512,256]{1,0:T(8,128)(2,1)S(1)}, u32[]{:S(2)}, u32[]{:S(2)}) collective-permute-start(bf16[512,256]{1,0:T(8,128)(2,1)S(1)} %collective-permute-done.3.refs_0_), channel_id=1, source_target_pairs={{0,16},{8,24},{16,0},{24,8},{1,17},{9,25},{17,1},{25,9},{2,18},{10... | collective-permute-start | bytes 786440 | tf_op jit(solution)/shard_map/ppermute | solution.py:17
  80.1 9.7 %collective-permute-start.6 = (bf16[512,256]{1,0:T(8,128)(2,1)S(1)}, bf16[512,256]{1,0:T(8,128)(2,1)S(1)}, u32[]{:S(2)}, u32[]{:S(2)}) collective-permute-start(bf16[512,256]{1,0:T(8,128)(2,1)S(1)} %collective-permute-done.2.refs_0_), channel_id=1, source_target_pairs={{0,8},{8,0},{16,24},{24,16},{1,9},{9,1},{17,25},{25,17},{2,10},{10... | collective-permute-start | bytes 786440 | tf_op jit(solution)/shard_map/ppermute | solution.py:17
  80.1 9.7 %collective-permute-start.7 = (bf16[512,256]{1,0:T(8,128)(2,1)S(1)}, bf16[512,256]{1,0:T(8,128)(2,1)S(1)}, u32[]{:S(2)}, u32[]{:S(2)}) collective-permute-start(bf16[512,256]{1,0:T(8,128)(2,1)S(1)} %collective-permute-done.2.refs_0_), channel_id=1, source_target_pairs={{0,16},{8,24},{16,0},{24,8},{1,17},{9,25},{17,1},{25,9},{2,18},{10... | collective-permute-start | bytes 786440 | tf_op jit(solution)/shard_map/ppermute | solution.py:17
  82.7 10.1 %collective-permute-start.9 = (bf16[512,256]{1,0:T(8,128)(2,1)S(1)}, bf16[512,256]{1,0:T(8,128)(2,1)S(1)}, u32[]{:S(2)}, u32[]{:S(2)}) collective-permute-start(bf16[512,256]{1,0:T(8,128)(2,1)S(1)} %pick.1), channel_id=1, source_target_pairs={{0,4},{1,5},{2,6},{3,7},{4,0},{5,1},{6,2},{7,3},{8,12},{9,13},{10,... | collective-permute-start | bytes 786440 | tf_op jit(solution)/shard_map/ppermute | solution.py:17
  85.5 8.6 %collective-permute-start.4 = (bf16[512,256]{1,0:T(8,128)(2,1)S(1)}, bf16[512,256]{1,0:T(8,128)(2,1)S(1)}, u32[]{:S(2)}, u32[]{:S(2)}) collective-permute-start(bf16[512,256]{1,0:T(8,128)(2,1)S(1)} %collective-permute-done.3.refs_0_), channel_id=1, source_target_pairs={{0,24},{8,16},{16,8},{24,0},{1,25},{9,17},{17,9},{25,1},{2,26},{10... | collective-permute-start | bytes 786440 | tf_op jit(solution)/shard_map/ppermute | solution.py:17
  94.8 2.7 %collective-permute-start.18 = (bf16[2,2,512,256]{3,2,1,0:T(8,128)(2,1)S(1)}, bf16[2,2,512,256]{3,2,1,0:T(8,128)(2,1)S(1)}, u32[]{:S(2)}, u32[]{:S(2)}) collective-permute-start(bf16[2,2,512,256]{3,2,1,0:T(8,128)(2,1)S(1)} %get-tuple-element.20.own), channel_id=1, source_target_pairs={{0,1},{1,0},{2,3},{3,2},{4,5},{5,4},{6,7},{7,6},{8,9},{9,8},{10,11... | collective-permute-start | bytes 3145736 | tf_op jit(solution)/shard_map/ppermute | solution.py:17
  94.9 2.7 %collective-permute-start.19 = (f32[8,256]{1,0:T(8,128)S(1)}, f32[8,256]{1,0:T(8,128)S(1)}, u32[]{:S(2)}, u32[]{:S(2)}) collective-permute-start(f32[8,256]{1,0:T(8,128)S(1)} %get-tuple-element.21.own_sums), channel_id=1, source_target_pairs={{0,1},{1,0},{2,3},{3,2},{4,5},{5,4},{6,7},{7,6},{8,9},{9,8},{10,11... | collective-permute-start | bytes 24584 | tf_op jit(solution)/shard_map/ppermute | solution.py:17
  98.9 8.7 %collective-permute-start.20 = (f16[144,512]{1,0:T(8,128)(2,1)S(1)}, f16[144,512]{1,0:T(8,128)(2,1)S(1)}, u32[]{:S(2)}, u32[]{:S(2)}) collective-permute-start(f16[144,512]{1,0:T(8,128)(2,1)S(1)} %convert_element_type.18), channel_id=1, source_target_pairs={{0,6},{1,7},{2,4},{3,5},{4,2},{5,3},{6,0},{7,1},{8,14},{9,15},{10,... | collective-permute-start | bytes 442376 | tf_op jit(solution)/shard_map/ppermute | solution.py:17
  101.4 13.7 %collective-permute-start.21 = (f16[144,512]{1,0:T(8,128)(2,1)S(1)}, f16[144,512]{1,0:T(8,128)(2,1)S(1)}, u32[]{:S(2)}, u32[]{:S(2)}) collective-permute-start(f16[144,512]{1,0:T(8,128)(2,1)S(1)} %convert_element_type.20), channel_id=1, source_target_pairs={{0,4},{1,5},{2,6},{3,7},{4,0},{5,1},{6,2},{7,3},{8,12},{9,13},{10,... | collective-permute-start | bytes 442376 | tf_op jit(solution)/shard_map/ppermute | solution.py:17
  101.8 13.3 %collective-permute-start.22 = (f16[144,512]{1,0:T(8,128)(2,1)S(1)}, f16[144,512]{1,0:T(8,128)(2,1)S(1)}, u32[]{:S(2)}, u32[]{:S(2)}) collective-permute-start(f16[144,512]{1,0:T(8,128)(2,1)S(1)} %convert_element_type.22), channel_id=1, source_target_pairs={{0,2},{1,3},{2,0},{3,1},{4,6},{5,7},{6,4},{7,5},{8,10},{9,11},{10,... | collective-permute-start | bytes 442376 | tf_op jit(solution)/shard_map/ppermute | solution.py:17
  115.6 4.3 %collective-permute-start.23 = (bf16[64,512]{1,0:T(8,128)(2,1)S(1)}, bf16[64,512]{1,0:T(8,128)(2,1)S(1)}, u32[]{:S(2)}, u32[]{:S(2)}) collective-permute-start(bf16[64,512]{1,0:T(8,128)(2,1)S(1)} %get-tuple-element.28), channel_id=1, source_target_pairs={{0,8},{8,0},{16,24},{24,16},{1,9},{9,1},{17,25},{25,17},{2,10},{10... | collective-permute-start | bytes 196616 | tf_op jit(solution)/shard_map/ppermute | solution.py:17
  117.6 7.0 %collective-permute-start.24 = (bf16[64,512]{1,0:T(8,128)(2,1)S(1)}, bf16[64,512]{1,0:T(8,128)(2,1)S(1)}, u32[]{:S(2)}, u32[]{:S(2)}) collective-permute-start(bf16[64,512]{1,0:T(8,128)(2,1)S(1)} %get-tuple-element.29), channel_id=1, source_target_pairs={{8,16},{16,8},{9,17},{17,9},{10,18},{18,10},{11,19},{19,11},{12,20... | collective-permute-start | bytes 196616 | tf_op jit(solution)/shard_map/ppermute | solution.py:426
  124.9 1.2 collective-permute-start.25
  126.2 3.6 %collective-permute-start.26 = (f32[8,128]{1,0:T(8,128)S(1)}, f32[8,128]{1,0:T(8,128)S(1)}, u32[]{:S(2)}, u32[]{:S(2)}) collective-permute-start(f32[8,128]{1,0:T(8,128)S(1)} %add.6), channel_id=1, source_target_pairs={{0,2},{1,3},{2,0},{3,1},{4,6},{5,7},{6,4},{7,5},{8,10},{9,11},{10,... | collective-permute-start | bytes 12296 | tf_op jit(solution)/shard_map/ppermute | solution.py:17
  129.8 4.5 %collective-permute-start.27 = (f32[8,128]{1,0:T(8,128)S(1)}, f32[8,128]{1,0:T(8,128)S(1)}, u32[]{:S(2)}, u32[]{:S(2)}) collective-permute-start(f32[8,128]{1,0:T(8,128)S(1)} %add.7.one), channel_id=1, source_target_pairs={{0,4},{1,5},{2,6},{3,7},{4,0},{5,1},{6,2},{7,3},{8,12},{9,13},{10,... | collective-permute-start | bytes 12296 | tf_op jit(solution)/shard_map/ppermute | solution.py:17

commit v2 on v1

--- a/solution.py
+++ b/solution.py
@@ -399,15 +399,15 @@
     for k in order:
         pieces[k] = {0: fetched[k]}
         for j in range(1, parts):
-            if 1 < k == k & -k and j in far:
+            if k == 1 and j in far:
                 pieces[k][j] = swap(far[j], "tok", 2 * k)
             else:
                 pieces[k][j] = swap(fetched[k], "section", j)
 
     total = project([mine, got], (None, None), parts, None, *staged[0], layers, False)
     final, keys = order[-1], tuple(range(parts))
-    steps = [(k, keys) for k in order[:-2]]
-    steps += [(final, keys[:-1])] + [(k, keys) for k in order[-2:-1]] + [(final, keys[-1:])]
+    steps = [(k, keys) for k in reversed(order[:-1])]
+    steps += [(final, keys[: parts // 2]), (final, keys[parts // 2 :])]
     steps = [step for step in steps if step[1]]
     for k, js in steps:
         last = (k, js) == steps[-1]

time: 135 us -> 127 us (0.941)
  the two profiles are of different devices: /device:TPU:2 before, /device:TPU:5 now
where the time goes in v2:
time: 127 us; the launch traced here: 125 us
  waiting for transfers between devices  73.9 us (58%)
  starting transfers between devices  34.1 us (27%)
  Pallas kernels  11.6 us (9%)
  local copies, waits for them, and re-layouts  4.5 us (4%)
    ppermute x27, waiting for transfers between devices, swap(): lax.ppermute(block, axis, [(i, i ^ mask) for i in range(lax.axis_size(axi...  71.1 us
    ppermute x27, starting transfers between devices, swap(): lax.ppermute(block, axis, [(i, i ^ mask) for i in range(lax.axis_size(axi...  31.1 us
    pallas_call x5, Pallas kernels, project(): pl.pallas_call(functools.partial(project_kernel, keys, parts, len(started...  5.44 us
    unnamed x7, local copies, waits for them, and re-layouts  4.5 us
    ppermute x1, starting transfers between devices, local(): second = lax.ppermute(second, 'section', route + [(b, a) for a, b in route])  3.07 us
    ppermute x1, waiting for transfers between devices, local(): second = lax.ppermute(second, 'section', route + [(b, a) for a, b in route])  2.81 us
  transfers between devices with their start and end apart: 28, of which 17 were waited for; matrix products, arithmetic and copies ran while one was open for 1% of the time, Pallas kernels for 6%

profile of v2, /device:TPU:5, one launch (start us, length us, event | category | flops | bytes accessed | tf_op | source)
XLA Modules:
  0.0 125.2 jit_solution(17609896238228159872)
XLA Ops:
  0.6 3.4 %copy-done.1 = bf16[2,256,8192]{2,1,0:T(8,128)(2,1)S(1)} copy-done((bf16[2,256,8192]{2,1,0:T(8,128)(2,1)S(1)}, bf16[2,256,8192]{2,1,0:T(8,128)(2,1)}, u32[]{:S(2)}) %copy-start.1) | copy-done | bytes 8388632
  4.0 0.5 stage.7.acts
  4.5 0.7 collective-permute-start.17
  5.3 0.9 deal.3
  6.2 0.7 collective-permute-start.11
  7.7 0.5 stage.6.acts
  8.3 0.7 collective-permute-start.13
  9.0 1.0 collective-permute-done.1.lower
  10.0 2.4 %collective-permute-start.2 = (bf16[512,256]{1,0:T(8,128)(2,1)S(1)}, bf16[512,256]{1,0:T(8,128)(2,1)S(1)}, u32[]{:S(2)}, u32[]{:S(2)}) collective-permute-start(bf16[512,256]{1,0:T(8,128)(2,1)S(1)} %join.1), channel_id=1, source_target_pairs={{0,4},{1,5},{2,6},{3,7},{4,0},{5,1},{6,2},{7,3},{8,12},{9,13},{10,... | collective-permute-start | bytes 786440 | tf_op jit(solution)/shard_map/ppermute | solution.py:17
  12.4 1.3 %collective-permute-start.8 = (bf16[512,256]{1,0:T(8,128)(2,1)S(1)}, bf16[512,256]{1,0:T(8,128)(2,1)S(1)}, u32[]{:S(2)}, u32[]{:S(2)}) collective-permute-start(bf16[512,256]{1,0:T(8,128)(2,1)S(1)} %join.1), channel_id=1, source_target_pairs={{0,2},{1,3},{2,0},{3,1},{4,6},{5,7},{6,4},{7,5},{8,10},{9,11},{10,... | collective-permute-start | bytes 786440 | tf_op jit(solution)/shard_map/ppermute | solution.py:17
  13.7 0.5 stage.5.acts
  14.2 9.9 %collective-permute-done.2.refs_0_ = bf16[512,256]{1,0:T(8,128)(2,1)S(1)} collective-permute-done((bf16[512,256]{1,0:T(8,128)(2,1)S(1)}, bf16[512,256]{1,0:T(8,128)(2,1)S(1)}, u32[]{:S(2)}, u32[]{:S(2)}) %collective-permute-start.2) | collective-permute-done | bytes 262176 | tf_op jit(solution)/shard_map/ppermute | solution.py:17
  24.1 1.3 %collective-permute-start.7 = (bf16[512,2048]{1,0:T(8,128)(2,1)S(1)}, bf16[512,2048]{1,0:T(8,128)(2,1)S(1)}, u32[]{:S(2)}, u32[]{:S(2)}) collective-permute-start(bf16[512,2048]{1,0:T(8,128)(2,1)S(1)} %stage.5.acts), channel_id=1, source_target_pairs={{0,1},{1,0},{2,3},{3,2},{4,5},{5,4},{6,7},{7,6},{8,9},{9,8},{10,11... | collective-permute-start | bytes 6291464 | tf_op jit(solution)/shard_map/ppermute | solution.py:17
  25.4 1.2 collective-permute-start.14
  26.6 0.5 stage.4.acts
  27.2 0.5 collective-permute-start
  27.7 5.4 %collective-permute-done.14.refs_1_ = bf16[512,256]{1,0:T(8,128)(2,1)S(1)} collective-permute-done((bf16[512,256]{1,0:T(8,128)(2,1)S(1)}, bf16[512,256]{1,0:T(8,128)(2,1)S(1)}, u32[]{:S(2)}, u32[]{:S(2)}) %collective-permute-start.14) | collective-permute-done | bytes 262176 | tf_op jit(solution)/shard_map/ppermute | solution.py:17
  33.3 6.6 %collective-permute-done.15.refs_2_ = bf16[512,256]{1,0:T(8,128)(2,1)S(1)} collective-permute-done((bf16[512,256]{1,0:T(8,128)(2,1)S(1)}, bf16[512,256]{1,0:T(8,128)(2,1)S(1)}, u32[]{:S(2)}, u32[]{:S(2)}) %collective-permute-start.15) | collective-permute-done | bytes 262176 | tf_op jit(solution)/shard_map/ppermute | solution.py:17
  39.9 1.2 collective-permute-start.16
  41.1 5.7 %collective-permute-done.16.refs_3_ = bf16[512,256]{1,0:T(8,128)(2,1)S(1)} collective-permute-done((bf16[512,256]{1,0:T(8,128)(2,1)S(1)}, bf16[512,256]{1,0:T(8,128)(2,1)S(1)}, u32[]{:S(2)}, u32[]{:S(2)}) %collective-permute-start.16) | collective-permute-done | bytes 262176 | tf_op jit(solution)/shard_map/ppermute | solution.py:17
  46.9 5.0 %collective-permute-done.10.refs_2_ = bf16[512,256]{1,0:T(8,128)(2,1)S(1)} collective-permute-done((bf16[512,256]{1,0:T(8,128)(2,1)S(1)}, bf16[512,256]{1,0:T(8,128)(2,1)S(1)}, u32[]{:S(2)}, u32[]{:S(2)}) %collective-permute-start.10) | collective-permute-done | bytes 262176 | tf_op jit(solution)/shard_map/ppermute | solution.py:17
  52.0 1.2 collective-permute-start.9
  53.2 4.0 %collective-permute-done.9.refs_1_ = bf16[512,256]{1,0:T(8,128)(2,1)S(1)} collective-permute-done((bf16[512,256]{1,0:T(8,128)(2,1)S(1)}, bf16[512,256]{1,0:T(8,128)(2,1)S(1)}, u32[]{:S(2)}, u32[]{:S(2)}) %collective-permute-start.9) | collective-permute-done | bytes 262176 | tf_op jit(solution)/shard_map/ppermute | solution.py:17
  57.2 5.2 %collective-permute-done.3.refs_0_ = bf16[512,256]{1,0:T(8,128)(2,1)S(1)} collective-permute-done((bf16[512,256]{1,0:T(8,128)(2,1)S(1)}, bf16[512,256]{1,0:T(8,128)(2,1)S(1)}, u32[]{:S(2)}, u32[]{:S(2)}) %collective-permute-start.3) | collective-permute-done | bytes 262176 | tf_op jit(solution)/shard_map/ppermute | solution.py:17
  62.4 8.0 %collective-permute-done.12.refs_3_ = bf16[512,256]{1,0:T(8,128)(2,1)S(1)} collective-permute-done((bf16[512,256]{1,0:T(8,128)(2,1)S(1)}, bf16[512,256]{1,0:T(8,128)(2,1)S(1)}, u32[]{:S(2)}, u32[]{:S(2)}) %collective-permute-start.12) | collective-permute-done | bytes 262176 | tf_op jit(solution)/shard_map/ppermute | solution.py:17
  70.5 1.2 collective-permute-start.6
  71.9 1.2 collective-permute-start.5
  73.1 1.2 project.5.refs_4_
  74.4 1.3 %project.6.refs_4_ = f32[2,512,256]{2,1,0:T(8,128)S(1)} custom-call(bf16[512,2048]{1,0:T(8,128)(2,1)S(1)} %stage.6.acts, bf16[512,2048]{1,0:T(8,128)(2,1)S(1)} %collective-permute-done.13.other, bf16[512,256]{1,0:T(8,128)(2,1)S(1)} %collective-permute-done.2.refs_0_, bf16[512,256]{1,0:T(8,128)(2,1)S(1)} %collective-permute-done.14.refs_1_, ...), custom_call_target="tpu_custom_call" | custom-call | flops 1073741824 | bytes 4194304 | tf_op jit(solution)/shard_map/project/pallas_call | solution.py:187
  75.6 1.3 %project.7.refs_2_ = f32[2,512,256]{2,1,0:T(8,128)S(1)} custom-call(bf16[512,2048]{1,0:T(8,128)(2,1)S(1)} %stage.5.acts, bf16[512,2048]{1,0:T(8,128)(2,1)S(1)} %collective-permute-done.7.other, bf16[512,256]{1,0:T(8,128)(2,1)S(1)} %collective-permute-done.8.refs_0_, bf16[512,256]{1,0:T(8,128)(2,1)S(1)} %collective-permute-done.9.refs_1_, ...), custom_call_target="tpu_custom_call" | custom-call | flops 1073741824 | bytes 4194304 | tf_op jit(solution)/shard_map/project/pallas_call | solution.py:187
  76.9 0.7 project.8.refs_2_
  77.7 2.0 %collective-permute-done.4.refs_0_ = bf16[512,256]{1,0:T(8,128)(2,1)S(1)} collective-permute-done((bf16[512,256]{1,0:T(8,128)(2,1)S(1)}, bf16[512,256]{1,0:T(8,128)(2,1)S(1)}, u32[]{:S(2)}, u32[]{:S(2)}) %collective-permute-start.4) | collective-permute-done | bytes 262176 | tf_op jit(solution)/shard_map/ppermute | solution.py:17
  79.7 0.9 project.9
  80.7 8.6 %collective-permute-start.18 = (bf16[2,2,512,256]{3,2,1,0:T(8,128)(2,1)S(1)}, bf16[2,2,512,256]{3,2,1,0:T(8,128)(2,1)S(1)}, u32[]{:S(2)}, u32[]{:S(2)}) collective-permute-start(bf16[2,2,512,256]{3,2,1,0:T(8,128)(2,1)S(1)} %get-tuple-element.20.own), channel_id=1, source_target_pairs={{0,1},{1,0},{2,3},{3,2},{4,5},{5,4},{6,7},{7,6},{8,9},{9,8},{10,11... | collective-permute-start | bytes 3145736 | tf_op jit(solution)/shard_map/ppermute | solution.py:17
  89.3 2.2 %collective-permute-done.19.oth_sums = f32[8,256]{1,0:T(8,128)S(1)} collective-permute-done((f32[8,256]{1,0:T(8,128)S(1)}, f32[8,256]{1,0:T(8,128)S(1)}, u32[]{:S(2)}, u32[]{:S(2)}) %collective-permute-start.19) | collective-permute-done | bytes 8224 | tf_op jit(solution)/shard_map/ppermute | solution.py:17
  91.5 1.3 %gram.1 = (f32[144,512]{1,0:T(8,128)S(1)}, f32[144,512]{1,0:T(8,128)S(1)}, f32[144,512]{1,0:T(8,128)S(1)}, f32[144,512]{1,0:T(8,128)S(1)}) custom-call(bf16[2,2,512,256]{3,2,1,0:T(8,128)(2,1)S(1)} %get-tuple-element.20.own, bf16[2,2,512,256]{3,2,1,0:T(8,128)(2,1)S(1)} %collective-permute-done.18.oth, f32[8,256]{1,0:T(8,128)S(1)} %get-tuple-element.21.own_sums, ...), custom_call_target="tpu_custom_call" | custom-call | flops 805306368 | bytes 2097152 | tf_op jit(solution)/shard_map/gram/pallas_call | solution.py:252
  92.9 3.7 %collective-permute-start.20 = (f16[144,512]{1,0:T(8,128)(2,1)S(1)}, f16[144,512]{1,0:T(8,128)(2,1)S(1)}, u32[]{:S(2)}, u32[]{:S(2)}) collective-permute-start(f16[144,512]{1,0:T(8,128)(2,1)S(1)} %convert_element_type.18), channel_id=1, source_target_pairs={{0,6},{1,7},{2,4},{3,5},{4,2},{5,3},{6,0},{7,1},{8,14},{9,15},{10,... | collective-permute-start | bytes 442376 | tf_op jit(solution)/shard_map/ppermute | solution.py:17
  97.0 3.4 %collective-permute-done.20 = f16[144,512]{1,0:T(8,128)(2,1)S(1)} collective-permute-done((f16[144,512]{1,0:T(8,128)(2,1)S(1)}, f16[144,512]{1,0:T(8,128)(2,1)S(1)}, u32[]{:S(2)}, u32[]{:S(2)}) %collective-permute-start.20) | collective-permute-done | bytes 147488 | tf_op jit(solution)/shard_map/ppermute | solution.py:17
  100.5 8.0 %collective-permute-done.21 = f16[144,512]{1,0:T(8,128)(2,1)S(1)} collective-permute-done((f16[144,512]{1,0:T(8,128)(2,1)S(1)}, f16[144,512]{1,0:T(8,128)(2,1)S(1)}, u32[]{:S(2)}, u32[]{:S(2)}) %collective-permute-start.21) | collective-permute-done | bytes 147488 | tf_op jit(solution)/shard_map/ppermute | solution.py:17
  109.3 3.1 %collective-permute-start.24 = (bf16[64,512]{1,0:T(8,128)(2,1)S(1)}, bf16[64,512]{1,0:T(8,128)(2,1)S(1)}, u32[]{:S(2)}, u32[]{:S(2)}) collective-permute-start(bf16[64,512]{1,0:T(8,128)(2,1)S(1)} %get-tuple-element.29), channel_id=1, source_target_pairs={{8,16},{16,8},{9,17},{17,9},{10,18},{18,10},{11,19},{19,11},{12,20... | collective-permute-start | bytes 196616 | tf_op jit(solution)/shard_map/ppermute | solution.py:426
  112.3 2.8 %collective-permute-done.24.two = bf16[64,512]{1,0:T(8,128)(2,1)S(1)} collective-permute-done((bf16[64,512]{1,0:T(8,128)(2,1)S(1)}, bf16[64,512]{1,0:T(8,128)(2,1)S(1)}, u32[]{:S(2)}, u32[]{:S(2)}) %collective-permute-start.24) | collective-permute-done | bytes 65568 | tf_op jit(solution)/shard_map/ppermute | solution.py:426
  115.4 2.4 %collective-permute-start.25 = (f32[8,128]{1,0:T(8,128)S(1)}, f32[8,128]{1,0:T(8,128)S(1)}, u32[]{:S(2)}, u32[]{:S(2)}) collective-permute-start(f32[8,128]{1,0:T(8,128)S(1)} %products.1), channel_id=1, source_target_pairs={{0,1},{1,0},{2,3},{3,2},{4,5},{5,4},{6,7},{7,6},{8,9},{9,8},{10,11... | collective-permute-start | bytes 12296 | tf_op jit(solution)/shard_map/ppermute | solution.py:17
  117.9 0.8 collective-permute-done.25
  118.7 2.5 %collective-permute-done.26 = f32[8,128]{1,0:T(8,128)S(1)} collective-permute-done((f32[8,128]{1,0:T(8,128)S(1)}, f32[8,128]{1,0:T(8,128)S(1)}, u32[]{:S(2)}, u32[]{:S(2)}) %collective-permute-start.26) | collective-permute-done | bytes 4128 | tf_op jit(solution)/shard_map/ppermute | solution.py:17
  121.1 1.2 collective-permute-start.27
  122.4 0.9 copy.4
  123.3 1.3 %collective-permute-done.27.two = f32[8,128]{1,0:T(8,128)S(1)} collective-permute-done((f32[8,128]{1,0:T(8,128)S(1)}, f32[8,128]{1,0:T(8,128)S(1)}, u32[]{:S(2)}, u32[]{:S(2)}) %collective-permute-start.27) | collective-permute-done | bytes 4128 | tf_op jit(solution)/shard_map/ppermute | solution.py:17
  124.5 0.6 ratios.1
  (40 shorter events, 3.1 us)
Async XLA Ops:
  0.6 3.4 %copy-start.1 = (bf16[2,256,8192]{2,1,0:T(8,128)(2,1)S(1)}, bf16[2,256,8192]{2,1,0:T(8,128)(2,1)}, u32[]{:S(2)}) copy-start(bf16[2,256,8192]{2,1,0:T(8,128)(2,1)} %param.2) | copy-start | bytes 25165828
  4.0 1.3 %copy-start = (bf16[1024,512]{1,0:T(8,128)(2,1)S(1)}, bf16[1024,512]{1,0:T(8,128)(2,1)}, u32[]{:S(2)}) copy-start(bf16[1024,512]{1,0:T(8,128)(2,1)} %proj.3) | copy-start | bytes 3145732
  4.0 3.7 %copy-start.2 = (bf16[2,256,8192]{2,1,0:T(8,128)(2,1)S(1)}, bf16[2,256,8192]{2,1,0:T(8,128)(2,1)}, u32[]{:S(2)}) copy-start(bf16[2,256,8192]{2,1,0:T(8,128)(2,1)} %param.2) | copy-start | bytes 25165828
  4.5 67.1 %collective-permute-start.17 = (bf16[512,2048]{1,0:T(8,128)(2,1)S(1)}, bf16[512,2048]{1,0:T(8,128)(2,1)S(1)}, u32[]{:S(2)}, u32[]{:S(2)}) collective-permute-start(bf16[512,2048]{1,0:T(8,128)(2,1)S(1)} %stage.7.acts), channel_id=1, source_target_pairs={{0,1},{1,0},{2,3},{3,2},{4,5},{5,4},{6,7},{7,6},{8,9},{9,8},{10,11... | collective-permute-start | bytes 6291464 | tf_op jit(solution)/shard_map/ppermute | solution.py:17
  6.2 20.9 %collective-permute-start.11 = (bf16[1024,256]{1,0:T(8,128)(2,1)S(1)}, bf16[1024,256]{1,0:T(8,128)(2,1)S(1)}, u32[]{:S(2)}, u32[]{:S(2)}) collective-permute-start(bf16[1024,256]{1,0:T(8,128)(2,1)S(1)} %get-tuple-element.19), channel_id=1, source_target_pairs={{0,1},{1,0},{2,3},{3,2},{4,5},{5,4},{6,7},{7,6},{8,9},{9,8},{10,11... | collective-permute-start | bytes 1572872 | tf_op jit(solution)/shard_map/ppermute | solution.py:17
  7.4 2.6 %collective-permute-start.1 = (bf16[256,256]{1,0:T(8,128)(2,1)S(1)}, bf16[256,256]{1,0:T(8,128)(2,1)S(1)}, u32[]{:S(2)}, u32[]{:S(2)}) collective-permute-start(bf16[256,256]{1,0:T(8,128)(2,1)S(1)} %get-tuple-element.17), channel_id=1, source_target_pairs={{0,1},{1,0},{2,3},{3,2},{4,5},{5,4},{6,7},{7,6},{8,9},{9,8},{10,11... | collective-permute-start | bytes 393224 | tf_op jit(solution)/shard_map/ppermute | solution.py:17
  8.3 63.7 %collective-permute-start.13 = (bf16[512,2048]{1,0:T(8,128)(2,1)S(1)}, bf16[512,2048]{1,0:T(8,128)(2,1)S(1)}, u32[]{:S(2)}, u32[]{:S(2)}) collective-permute-start(bf16[512,2048]{1,0:T(8,128)(2,1)S(1)} %stage.6.acts), channel_id=1, source_target_pairs={{0,1},{1,0},{2,3},{3,2},{4,5},{5,4},{6,7},{7,6},{8,9},{9,8},{10,11... | collective-permute-start | bytes 6291464 | tf_op jit(solution)/shard_map/ppermute | solution.py:17
  10.0 14.1 %collective-permute-start.2 = (bf16[512,256]{1,0:T(8,128)(2,1)S(1)}, bf16[512,256]{1,0:T(8,128)(2,1)S(1)}, u32[]{:S(2)}, u32[]{:S(2)}) collective-permute-start(bf16[512,256]{1,0:T(8,128)(2,1)S(1)} %join.1), channel_id=1, source_target_pairs={{0,4},{1,5},{2,6},{3,7},{4,0},{5,1},{6,2},{7,3},{8,12},{9,13},{10,... | collective-permute-start | bytes 786440 | tf_op jit(solution)/shard_map/ppermute | solution.py:17
  12.4 13.0 %collective-permute-start.8 = (bf16[512,256]{1,0:T(8,128)(2,1)S(1)}, bf16[512,256]{1,0:T(8,128)(2,1)S(1)}, u32[]{:S(2)}, u32[]{:S(2)}) collective-permute-start(bf16[512,256]{1,0:T(8,128)(2,1)S(1)} %join.1), channel_id=1, source_target_pairs={{0,2},{1,3},{2,0},{3,1},{4,6},{5,7},{6,4},{7,5},{8,10},{9,11},{10,... | collective-permute-start | bytes 786440 | tf_op jit(solution)/shard_map/ppermute | solution.py:17
  24.1 51.5 %collective-permute-start.7 = (bf16[512,2048]{1,0:T(8,128)(2,1)S(1)}, bf16[512,2048]{1,0:T(8,128)(2,1)S(1)}, u32[]{:S(2)}, u32[]{:S(2)}) collective-permute-start(bf16[512,2048]{1,0:T(8,128)(2,1)S(1)} %stage.5.acts), channel_id=1, source_target_pairs={{0,1},{1,0},{2,3},{3,2},{4,5},{5,4},{6,7},{7,6},{8,9},{9,8},{10,11... | collective-permute-start | bytes 6291464 | tf_op jit(solution)/shard_map/ppermute | solution.py:17
  25.4 7.7 %collective-permute-start.14 = (bf16[512,256]{1,0:T(8,128)(2,1)S(1)}, bf16[512,256]{1,0:T(8,128)(2,1)S(1)}, u32[]{:S(2)}, u32[]{:S(2)}) collective-permute-start(bf16[512,256]{1,0:T(8,128)(2,1)S(1)} %collective-permute-done.2.refs_0_), channel_id=1, source_target_pairs={{0,8},{8,0},{16,24},{24,16},{1,9},{9,1},{17,25},{25,17},{2,10},{10... | collective-permute-start | bytes 786440 | tf_op jit(solution)/shard_map/ppermute | solution.py:17
  27.2 49.8 %collective-permute-start = (bf16[512,2048]{1,0:T(8,128)(2,1)S(1)}, bf16[512,2048]{1,0:T(8,128)(2,1)S(1)}, u32[]{:S(2)}, u32[]{:S(2)}) collective-permute-start(bf16[512,2048]{1,0:T(8,128)(2,1)S(1)} %stage.4.acts), channel_id=1, source_target_pairs={{0,1},{1,0},{2,3},{3,2},{4,5},{5,4},{6,7},{7,6},{8,9},{9,8},{10,11... | collective-permute-start | bytes 6291464 | tf_op jit(solution)/shard_map/ppermute | solution.py:17
  33.1 6.8 %collective-permute-start.15 = (bf16[512,256]{1,0:T(8,128)(2,1)S(1)}, bf16[512,256]{1,0:T(8,128)(2,1)S(1)}, u32[]{:S(2)}, u32[]{:S(2)}) collective-permute-start(bf16[512,256]{1,0:T(8,128)(2,1)S(1)} %collective-permute-done.2.refs_0_), channel_id=1, source_target_pairs={{0,16},{8,24},{16,0},{24,8},{1,17},{9,25},{17,1},{25,9},{2,18},{10... | collective-permute-start | bytes 786440 | tf_op jit(solution)/shard_map/ppermute | solution.py:17
  39.9 6.9 %collective-permute-start.16 = (bf16[512,256]{1,0:T(8,128)(2,1)S(1)}, bf16[512,256]{1,0:T(8,128)(2,1)S(1)}, u32[]{:S(2)}, u32[]{:S(2)}) collective-permute-start(bf16[512,256]{1,0:T(8,128)(2,1)S(1)} %collective-permute-done.2.refs_0_), channel_id=1, source_target_pairs={{0,24},{8,16},{16,8},{24,0},{1,25},{9,17},{17,9},{25,1},{2,26},{10... | collective-permute-start | bytes 786440 | tf_op jit(solution)/shard_map/ppermute | solution.py:17
  46.8 5.2 %collective-permute-start.10 = (bf16[512,256]{1,0:T(8,128)(2,1)S(1)}, bf16[512,256]{1,0:T(8,128)(2,1)S(1)}, u32[]{:S(2)}, u32[]{:S(2)}) collective-permute-start(bf16[512,256]{1,0:T(8,128)(2,1)S(1)} %collective-permute-done.8.refs_0_), channel_id=1, source_target_pairs={{0,16},{8,24},{16,0},{24,8},{1,17},{9,25},{17,1},{25,9},{2,18},{10... | collective-permute-start | bytes 786440 | tf_op jit(solution)/shard_map/ppermute | solution.py:17
  52.0 5.2 %collective-permute-start.9 = (bf16[512,256]{1,0:T(8,128)(2,1)S(1)}, bf16[512,256]{1,0:T(8,128)(2,1)S(1)}, u32[]{:S(2)}, u32[]{:S(2)}) collective-permute-start(bf16[512,256]{1,0:T(8,128)(2,1)S(1)} %collective-permute-done.8.refs_0_), channel_id=1, source_target_pairs={{0,8},{8,0},{16,24},{24,16},{1,9},{9,1},{17,25},{25,17},{2,10},{10... | collective-permute-start | bytes 786440 | tf_op jit(solution)/shard_map/ppermute | solution.py:17
  57.2 5.2 %collective-permute-start.3 = (bf16[512,256]{1,0:T(8,128)(2,1)S(1)}, bf16[512,256]{1,0:T(8,128)(2,1)S(1)}, u32[]{:S(2)}, u32[]{:S(2)}) collective-permute-start(bf16[512,256]{1,0:T(8,128)(2,1)S(1)} %collective-permute-done.2.refs_0_), channel_id=1, source_target_pairs={{0,2},{1,3},{2,0},{3,1},{4,6},{5,7},{6,4},{7,5},{8,10},{9,11},{10,... | collective-permute-start | bytes 786440 | tf_op jit(solution)/shard_map/ppermute | solution.py:17
  62.4 8.0 %collective-permute-start.12 = (bf16[512,256]{1,0:T(8,128)(2,1)S(1)}, bf16[512,256]{1,0:T(8,128)(2,1)S(1)}, u32[]{:S(2)}, u32[]{:S(2)}) collective-permute-start(bf16[512,256]{1,0:T(8,128)(2,1)S(1)} %pick.1), channel_id=1, source_target_pairs={{0,2},{1,3},{2,0},{3,1},{4,6},{5,7},{6,4},{7,5},{8,10},{9,11},{10,... | collective-permute-start | bytes 786440 | tf_op jit(solution)/shard_map/ppermute | solution.py:17
  70.5 6.5 %collective-permute-start.6 = (bf16[512,256]{1,0:T(8,128)(2,1)S(1)}, bf16[512,256]{1,0:T(8,128)(2,1)S(1)}, u32[]{:S(2)}, u32[]{:S(2)}) collective-permute-start(bf16[512,256]{1,0:T(8,128)(2,1)S(1)} %collective-permute-done.3.refs_0_), channel_id=1, source_target_pairs={{0,8},{8,0},{16,24},{24,16},{1,9},{9,1},{17,25},{25,17},{2,10},{10... | collective-permute-start | bytes 786440 | tf_op jit(solution)/shard_map/ppermute | solution.py:17
  71.7 8.0 %collective-permute-start.4 = (bf16[512,256]{1,0:T(8,128)(2,1)S(1)}, bf16[512,256]{1,0:T(8,128)(2,1)S(1)}, u32[]{:S(2)}, u32[]{:S(2)}) collective-permute-start(bf16[512,256]{1,0:T(8,128)(2,1)S(1)} %collective-permute-done.3.refs_0_), channel_id=1, source_target_pairs={{0,16},{8,24},{16,0},{24,8},{1,17},{9,25},{17,1},{25,9},{2,18},{10... | collective-permute-start | bytes 786440 | tf_op jit(solution)/shard_map/ppermute | solution.py:17
  71.9 7.8 %collective-permute-start.5 = (bf16[512,256]{1,0:T(8,128)(2,1)S(1)}, bf16[512,256]{1,0:T(8,128)(2,1)S(1)}, u32[]{:S(2)}, u32[]{:S(2)}) collective-permute-start(bf16[512,256]{1,0:T(8,128)(2,1)S(1)} %collective-permute-done.3.refs_0_), channel_id=1, source_target_pairs={{0,24},{8,16},{16,8},{24,0},{1,25},{9,17},{17,9},{25,1},{2,26},{10... | collective-permute-start | bytes 786440 | tf_op jit(solution)/shard_map/ppermute | solution.py:17
  80.7 10.9 %collective-permute-start.18 = (bf16[2,2,512,256]{3,2,1,0:T(8,128)(2,1)S(1)}, bf16[2,2,512,256]{3,2,1,0:T(8,128)(2,1)S(1)}, u32[]{:S(2)}, u32[]{:S(2)}) collective-permute-start(bf16[2,2,512,256]{3,2,1,0:T(8,128)(2,1)S(1)} %get-tuple-element.20.own), channel_id=1, source_target_pairs={{0,1},{1,0},{2,3},{3,2},{4,5},{5,4},{6,7},{7,6},{8,9},{9,8},{10,11... | collective-permute-start | bytes 3145736 | tf_op jit(solution)/shard_map/ppermute | solution.py:17
  89.2 2.3 %collective-permute-start.19 = (f32[8,256]{1,0:T(8,128)S(1)}, f32[8,256]{1,0:T(8,128)S(1)}, u32[]{:S(2)}, u32[]{:S(2)}) collective-permute-start(f32[8,256]{1,0:T(8,128)S(1)} %get-tuple-element.21.own_sums), channel_id=1, source_target_pairs={{0,1},{1,0},{2,3},{3,2},{4,5},{5,4},{6,7},{7,6},{8,9},{9,8},{10,11... | collective-permute-start | bytes 24584 | tf_op jit(solution)/shard_map/ppermute | solution.py:17
  92.9 7.6 %collective-permute-start.20 = (f16[144,512]{1,0:T(8,128)(2,1)S(1)}, f16[144,512]{1,0:T(8,128)(2,1)S(1)}, u32[]{:S(2)}, u32[]{:S(2)}) collective-permute-start(f16[144,512]{1,0:T(8,128)(2,1)S(1)} %convert_element_type.18), channel_id=1, source_target_pairs={{0,6},{1,7},{2,4},{3,5},{4,2},{5,3},{6,0},{7,1},{8,14},{9,15},{10,... | collective-permute-start | bytes 442376 | tf_op jit(solution)/shard_map/ppermute | solution.py:17
  96.6 11.9 %collective-permute-start.21 = (f16[144,512]{1,0:T(8,128)(2,1)S(1)}, f16[144,512]{1,0:T(8,128)(2,1)S(1)}, u32[]{:S(2)}, u32[]{:S(2)}) collective-permute-start(f16[144,512]{1,0:T(8,128)(2,1)S(1)} %convert_element_type.20), channel_id=1, source_target_pairs={{0,4},{1,5},{2,6},{3,7},{4,0},{5,1},{6,2},{7,3},{8,12},{9,13},{10,... | collective-permute-start | bytes 442376 | tf_op jit(solution)/shard_map/ppermute | solution.py:17
  96.7 11.8 %collective-permute-start.22 = (f16[144,512]{1,0:T(8,128)(2,1)S(1)}, f16[144,512]{1,0:T(8,128)(2,1)S(1)}, u32[]{:S(2)}, u32[]{:S(2)}) collective-permute-start(f16[144,512]{1,0:T(8,128)(2,1)S(1)} %convert_element_type.22), channel_id=1, source_target_pairs={{0,2},{1,3},{2,0},{3,1},{4,6},{5,7},{6,4},{7,5},{8,10},{9,11},{10,... | collective-permute-start | bytes 442376 | tf_op jit(solution)/shard_map/ppermute | solution.py:17
  108.9 3.4 %collective-permute-start.23 = (bf16[64,512]{1,0:T(8,128)(2,1)S(1)}, bf16[64,512]{1,0:T(8,128)(2,1)S(1)}, u32[]{:S(2)}, u32[]{:S(2)}) collective-permute-start(bf16[64,512]{1,0:T(8,128)(2,1)S(1)} %get-tuple-element.28), channel_id=1, source_target_pairs={{0,8},{8,0},{16,24},{24,16},{1,9},{9,1},{17,25},{25,17},{2,10},{10... | collective-permute-start | bytes 196616 | tf_op jit(solution)/shard_map/ppermute | solution.py:17
  109.3 5.9 %collective-permute-start.24 = (bf16[64,512]{1,0:T(8,128)(2,1)S(1)}, bf16[64,512]{1,0:T(8,128)(2,1)S(1)}, u32[]{:S(2)}, u32[]{:S(2)}) collective-permute-start(bf16[64,512]{1,0:T(8,128)(2,1)S(1)} %get-tuple-element.29), channel_id=1, source_target_pairs={{8,16},{16,8},{9,17},{17,9},{10,18},{18,10},{11,19},{19,11},{12,20... | collective-permute-start | bytes 196616 | tf_op jit(solution)/shard_map/ppermute | solution.py:426
  115.4 3.3 %collective-permute-start.25 = (f32[8,128]{1,0:T(8,128)S(1)}, f32[8,128]{1,0:T(8,128)S(1)}, u32[]{:S(2)}, u32[]{:S(2)}) collective-permute-start(f32[8,128]{1,0:T(8,128)S(1)} %products.1), channel_id=1, source_target_pairs={{0,1},{1,0},{2,3},{3,2},{4,5},{5,4},{6,7},{7,6},{8,9},{9,8},{10,11... | collective-permute-start | bytes 12296 | tf_op jit(solution)/shard_map/ppermute | solution.py:17
  118.7 2.5 %collective-permute-start.26 = (f32[8,128]{1,0:T(8,128)S(1)}, f32[8,128]{1,0:T(8,128)S(1)}, u32[]{:S(2)}, u32[]{:S(2)}) collective-permute-start(f32[8,128]{1,0:T(8,128)S(1)} %add.6), channel_id=1, source_target_pairs={{0,2},{1,3},{2,0},{3,1},{4,6},{5,7},{6,4},{7,5},{8,10},{9,11},{10,... | collective-permute-start | bytes 12296 | tf_op jit(solution)/shard_map/ppermute | solution.py:17
  121.1 3.4 %collective-permute-start.27 = (f32[8,128]{1,0:T(8,128)S(1)}, f32[8,128]{1,0:T(8,128)S(1)}, u32[]{:S(2)}, u32[]{:S(2)}) collective-permute-start(f32[8,128]{1,0:T(8,128)S(1)} %add.7.one), channel_id=1, source_target_pairs={{0,4},{1,5},{2,6},{3,7},{4,0},{5,1},{6,2},{7,3},{8,12},{9,13},{10,... | collective-permute-start | bytes 12296 | tf_op jit(solution)/shard_map/ppermute | solution.py:17

commit v3 on v2

--- a/solution.py
+++ b/solution.py
@@ -200,26 +200,52 @@
     return jnp.ceil(jnp.log2(jnp.maximum(top, 1e-30))) - 14.0
 
 
-def gram_kernel(layers, chips, own, oth, own_sums, oth_sums, *outs):
+ALONG_TOKENS = (((0,), (0,)), ((), ()))
+
+
+def halves(ref, layer, rows, swapped):
+    span = pl.ds(layer * rows, rows)
+    sides = (1, 0) if swapped else (0, 1)
+    return [jnp.concatenate([ref[part, n, span, :] for n in sides], axis=0) for part in range(2)]
+
+
+def outer(left, right):
+    return sum(
+        lax.dot_general(left[i], right[j], ALONG_TOKENS, preferred_element_type=F32)
+        for i, j in ((0, 0), (0, 1), (1, 0))
+    )
+
+
+def inner_gram_kernel(layers, own, out):
+    rows = own.shape[2] // layers
+    for layer in range(layers):
+        here = halves(own, layer, rows, False)
+        out[layer] = outer(here, here)
+
+
+def inner_gram(own, layers):
+    rows, half = own.shape[2:]
+    return pl.pallas_call(
+        functools.partial(inner_gram_kernel, layers),
+        out_shape=jax.ShapeDtypeStruct((layers, half, half), F32),
+        in_specs=[VMEM],
+        out_specs=VMEM,
+        compiler_params=params(6),
+        cost_estimate=cost(12 * rows * half * half, 16 * rows * half),
+        name="inner_gram",
+    )(own)
+
+
+def gram_kernel(layers, chips, inner, own, oth, own_sums, oth_sums, *outs):
     chip = place()[0]
     half = own.shape[3]
     rows = own.shape[2] // layers
     width = half // chips
-    along_tokens = (((0,), (0,)), ((), ()))
     sums = jnp.concatenate([own_sums[...], oth_sums[...]], axis=1)
     tail = []
     for layer in range(layers):
-        span = pl.ds(layer * rows, rows)
-        left, right = [], []
-        for part in range(2):
-            here = jnp.concatenate([own[part, 0, span, :], own[part, 1, span, :]], axis=0)
-            there = jnp.concatenate([oth[part, 1, span, :], oth[part, 0, span, :]], axis=0)
-            left.append(here)
-            right.append(jnp.concatenate([here, there], axis=1))
-        gram = sum(
-            lax.dot_general(left[i], right[j], along_tokens, preferred_element_type=F32)
-            for i, j in ((0, 0), (0, 1), (1, 0))
-        )
+        cross = outer(halves(own, layer, rows, False), halves(oth, layer, rows, True))
+        gram = jnp.concatenate([inner[layer], cross], axis=1)
         power = exponent(gram)
         gram = gram * jnp.exp2(-power)
         blocks = [gram[i * width : (i + 1) * width] for i in range(chips)]
@@ -233,31 +259,33 @@
         column = column * jnp.exp2(-lift)
         high = column.astype(BF16).astype(F32)
         middle = (column - high).astype(BF16).astype(F32)
-        line = jnp.zeros_like(column)
-        tail += [high, middle, column - high - middle, line + power, line + lift]
+        line = jnp.zeros((1, half), F32)
+        powers = jnp.concatenate([line + power, line + lift], axis=1)
+        tail += [high, middle, column - high - middle, powers]
     for out in outs:
-        out[layers * width :, :] = jnp.zeros_like(out[layers * width :, :])
+        if len(tail) < tail_rows(layers):
+            out[layers * width :, :] = jnp.zeros_like(out[layers * width :, :])
         for n, line in enumerate(tail):
             out[layers * width + n : layers * width + n + 1, :] = line
 
 
 def tail_rows(layers):
-    return -(-5 * layers // 16) * 16
-
-
-def gram(own, oth, own_sums, oth_sums, layers, chips):
+    return -(-4 * layers // 8) * 8
+
+
+def gram(inner, own, oth, own_sums, oth_sums, layers, chips):
     rows, half = own.shape[2:]
     height = layers * (half // chips) + tail_rows(layers)
     message = jax.ShapeDtypeStruct((height, 2 * half), F32)
     return pl.pallas_call(
         functools.partial(gram_kernel, layers, chips),
         out_shape=(message,) * chips,
-        in_specs=[VMEM] * 4,
+        in_specs=[VMEM] * 5,
         out_specs=(VMEM,) * chips,
         compiler_params=params(10),
-        cost_estimate=cost(24 * rows * half * half, 16 * rows * half),
+        cost_estimate=cost(12 * rows * half * half, 16 * rows * half),
         name="gram",
-    )(own, oth, own_sums, oth_sums)
+    )(inner, own, oth, own_sums, oth_sums)
 
 
 def finish_kernel(layers, tokens, *refs):
@@ -272,12 +300,13 @@
     kept = []
     for layer in range(layers):
         span = slice(layer * width, (layer + 1) * width)
-        at = layers * width + 5 * layer
+        at = layers * width + 4 * layer
         value, sums = 0.0, []
         for message in messages:
-            line = [message[at + n : at + n + 1, :] for n in range(5)]
-            value = value + message[span, :] * jnp.exp2(line[3])
-            sums.append((line[0] + line[1] + line[2]) * jnp.exp2(line[4]))
+            line = [message[at + n : at + n + 1, :] for n in range(4)]
+            scale = jnp.exp2(line[3])
+            value = value + message[span, :] * scale[:, :1]
+            sums.append((line[0] + line[1] + line[2]) * scale[:, rank - 1 :])
         mean = sum(sums) / tokens
         for total in sums:
             drift = total / (tokens // chips) - mean
@@ -399,15 +428,16 @@
     for k in order:
         pieces[k] = {0: fetched[k]}
         for j in range(1, parts):
-            if k == 1 and j in far:
+            if j in far and k in (1, order[-1]):
                 pieces[k][j] = swap(far[j], "tok", 2 * k)
             else:
                 pieces[k][j] = swap(fetched[k], "section", j)
 
     total = project([mine, got], (None, None), parts, None, *staged[0], layers, False)
     final, keys = order[-1], tuple(range(parts))
+    late = tuple(j for j in keys[1:] if j not in far)
     steps = [(k, keys) for k in reversed(order[:-1])]
-    steps += [(final, keys[: parts // 2]), (final, keys[parts // 2 :])]
+    steps += [(final, tuple(j for j in keys if j not in late)), (final, late)]
     steps = [step for step in steps if step[1]]
     for k, js in steps:
         last = (k, js) == steps[-1]
@@ -415,15 +445,18 @@
         total = project(chosen, js, parts, total, *staged[k], layers, last)
     split, sums = total
 
-    messages = gram(split, swap(split, "tok", 1), sums, swap(sums, "tok", 1), layers, chips)
+    split_oth = swap(split, "tok", 1)
+    sums_oth = swap(sums, "tok", 1)
+    inner = inner_gram(split, layers)
+    messages = gram(inner, split, split_oth, sums, sums_oth, layers, chips)
     arrived = [messages[0]]
     for k in reversed(range(1, chips)):
         arrived.append(swap(messages[k].astype(jnp.float16), "tok", 2 * k).astype(F32))
     sketch, turned, first, second = finish(arrived, layers, tok_rows * groups)
 
-    first = swap(first, "section", 1)
     route = [(i, i + 1) for i in range(1, sections - 1, 2)]
     second = lax.ppermute(second, "section", route + [(b, a) for a, b in route])
+    first = swap(first, "section", 1)
     value = products(turned, first, second, sections)
     mask = 1
     while 2 * mask < groups:

time: 127 us -> 129 us (1.016)
  starting transfers between devices: 34.1 us -> 37.7 us
  waiting for transfers between devices: 73.9 us -> 71.3 us
    ppermute x27, starting transfers between devices: 31.1 us -> 35 us  [swap(): lax.ppermute(block, axis, [(i, i ^ mask) for i in range(lax.axis_size(axi...]
    ppermute x27, waiting for transfers between devices: 71.1 us -> 68.2 us  [swap(): lax.ppermute(block, axis, [(i, i ^ mask) for i in range(lax.axis_size(axi...]
where the time goes in v3:
time: 129 us; the launch traced here: 127 us
  waiting for transfers between devices  71.3 us (55%)
  starting transfers between devices  37.7 us (29%)
  Pallas kernels  12 us (9%)
  local copies, waits for them, and re-layouts  4.5 us (3%)
    ppermute x27, waiting for transfers between devices, swap(): lax.ppermute(block, axis, [(i, i ^ mask) for i in range(lax.axis_size(axi...  68.2 us
    ppermute x27, starting transfers between devices, swap(): lax.ppermute(block, axis, [(i, i ^ mask) for i in range(lax.axis_size(axi...  35 us
    pallas_call x5, Pallas kernels, project(): pl.pallas_call(functools.partial(project_kernel, keys, parts, len(started...  5.45 us
    unnamed x7, local copies, waits for them, and re-layouts  4.5 us
    ppermute x1, waiting for transfers between devices, local(): second = lax.ppermute(second, 'section', route + [(b, a) for a, b in route])  3.12 us
    ppermute x1, starting transfers between devices, local(): second = lax.ppermute(second, 'section', route + [(b, a) for a, b in route])  2.76 us
  transfers between devices with their start and end apart: 28, of which 17 were waited for; matrix products, arithmetic and copies ran while one was open for 1% of the time, Pallas kernels for 6%

profile of v3, /device:TPU:5, one launch (start us, length us, event | category | flops | bytes accessed | tf_op | source)
XLA Modules:
  0.0 126.5 jit_solution(4452019712104689609)
XLA Ops:
  0.6 3.4 %copy-done.1 = bf16[2,256,8192]{2,1,0:T(8,128)(2,1)S(1)} copy-done((bf16[2,256,8192]{2,1,0:T(8,128)(2,1)S(1)}, bf16[2,256,8192]{2,1,0:T(8,128)(2,1)}, u32[]{:S(2)}) %copy-start.1) | copy-done | bytes 8388632
  4.0 0.5 stage.7.acts
  4.5 0.7 collective-permute-start.17
  5.3 0.9 deal.3
  6.2 0.7 collective-permute-start.6
  8.3 0.7 collective-permute-start.13
  9.0 1.0 collective-permute-done.1.lower
  10.0 2.4 %collective-permute-start.2 = (bf16[512,256]{1,0:T(8,128)(2,1)S(1)}, bf16[512,256]{1,0:T(8,128)(2,1)S(1)}, u32[]{:S(2)}, u32[]{:S(2)}) collective-permute-start(bf16[512,256]{1,0:T(8,128)(2,1)S(1)} %join.1), channel_id=1, source_target_pairs={{0,4},{1,5},{2,6},{3,7},{4,0},{5,1},{6,2},{7,3},{8,12},{9,13},{10,... | collective-permute-start | bytes 786440 | tf_op jit(solution)/shard_map/ppermute | solution.py:17
  12.4 1.3 %collective-permute-start.9 = (bf16[512,256]{1,0:T(8,128)(2,1)S(1)}, bf16[512,256]{1,0:T(8,128)(2,1)S(1)}, u32[]{:S(2)}, u32[]{:S(2)}) collective-permute-start(bf16[512,256]{1,0:T(8,128)(2,1)S(1)} %join.1), channel_id=1, source_target_pairs={{0,2},{1,3},{2,0},{3,1},{4,6},{5,7},{6,4},{7,5},{8,10},{9,11},{10,... | collective-permute-start | bytes 786440 | tf_op jit(solution)/shard_map/ppermute | solution.py:17
  14.2 9.9 %collective-permute-done.2.refs_0_ = bf16[512,256]{1,0:T(8,128)(2,1)S(1)} collective-permute-done((bf16[512,256]{1,0:T(8,128)(2,1)S(1)}, bf16[512,256]{1,0:T(8,128)(2,1)S(1)}, u32[]{:S(2)}, u32[]{:S(2)}) %collective-permute-start.2) | collective-permute-done | bytes 262176 | tf_op jit(solution)/shard_map/ppermute | solution.py:17
  24.1 1.3 %collective-permute-start.8 = (bf16[512,2048]{1,0:T(8,128)(2,1)S(1)}, bf16[512,2048]{1,0:T(8,128)(2,1)S(1)}, u32[]{:S(2)}, u32[]{:S(2)}) collective-permute-start(bf16[512,2048]{1,0:T(8,128)(2,1)S(1)} %stage.5.acts), channel_id=1, source_target_pairs={{0,1},{1,0},{2,3},{3,2},{4,5},{5,4},{6,7},{7,6},{8,9},{9,8},{10,11... | collective-permute-start | bytes 6291464 | tf_op jit(solution)/shard_map/ppermute | solution.py:17
  25.4 1.2 collective-permute-start.14
  27.2 0.5 collective-permute-start
  27.7 5.4 %collective-permute-done.14.refs_1_ = bf16[512,256]{1,0:T(8,128)(2,1)S(1)} collective-permute-done((bf16[512,256]{1,0:T(8,128)(2,1)S(1)}, bf16[512,256]{1,0:T(8,128)(2,1)S(1)}, u32[]{:S(2)}, u32[]{:S(2)}) %collective-permute-start.14) | collective-permute-done | bytes 262176 | tf_op jit(solution)/shard_map/ppermute | solution.py:17
  33.3 6.6 %collective-permute-done.15.refs_2_ = bf16[512,256]{1,0:T(8,128)(2,1)S(1)} collective-permute-done((bf16[512,256]{1,0:T(8,128)(2,1)S(1)}, bf16[512,256]{1,0:T(8,128)(2,1)S(1)}, u32[]{:S(2)}, u32[]{:S(2)}) %collective-permute-start.15) | collective-permute-done | bytes 262176 | tf_op jit(solution)/shard_map/ppermute | solution.py:17
  39.9 1.2 collective-permute-start.16
  41.1 5.7 %collective-permute-done.16.refs_3_ = bf16[512,256]{1,0:T(8,128)(2,1)S(1)} collective-permute-done((bf16[512,256]{1,0:T(8,128)(2,1)S(1)}, bf16[512,256]{1,0:T(8,128)(2,1)S(1)}, u32[]{:S(2)}, u32[]{:S(2)}) %collective-permute-start.16) | collective-permute-done | bytes 262176 | tf_op jit(solution)/shard_map/ppermute | solution.py:17
  46.8 1.2 collective-permute-start.10
  48.0 4.0 %collective-permute-done.10.refs_1_ = bf16[512,256]{1,0:T(8,128)(2,1)S(1)} collective-permute-done((bf16[512,256]{1,0:T(8,128)(2,1)S(1)}, bf16[512,256]{1,0:T(8,128)(2,1)S(1)}, u32[]{:S(2)}, u32[]{:S(2)}) %collective-permute-start.10) | collective-permute-done | bytes 262176 | tf_op jit(solution)/shard_map/ppermute | solution.py:17
  52.2 5.0 %collective-permute-done.11.refs_2_ = bf16[512,256]{1,0:T(8,128)(2,1)S(1)} collective-permute-done((bf16[512,256]{1,0:T(8,128)(2,1)S(1)}, bf16[512,256]{1,0:T(8,128)(2,1)S(1)}, u32[]{:S(2)}, u32[]{:S(2)}) %collective-permute-start.11) | collective-permute-done | bytes 262176 | tf_op jit(solution)/shard_map/ppermute | solution.py:17
  57.2 5.2 %collective-permute-done.3.refs_0_ = bf16[512,256]{1,0:T(8,128)(2,1)S(1)} collective-permute-done((bf16[512,256]{1,0:T(8,128)(2,1)S(1)}, bf16[512,256]{1,0:T(8,128)(2,1)S(1)}, u32[]{:S(2)}, u32[]{:S(2)}) %collective-permute-start.3) | collective-permute-done | bytes 262176 | tf_op jit(solution)/shard_map/ppermute | solution.py:17
  62.4 8.0 %collective-permute-done.12.refs_3_ = bf16[512,256]{1,0:T(8,128)(2,1)S(1)} collective-permute-done((bf16[512,256]{1,0:T(8,128)(2,1)S(1)}, bf16[512,256]{1,0:T(8,128)(2,1)S(1)}, u32[]{:S(2)}, u32[]{:S(2)}) %collective-permute-start.12) | collective-permute-done | bytes 262176 | tf_op jit(solution)/shard_map/ppermute | solution.py:17
  70.5 3.8 %collective-permute-start.7 = (bf16[512,256]{1,0:T(8,128)(2,1)S(1)}, bf16[512,256]{1,0:T(8,128)(2,1)S(1)}, u32[]{:S(2)}, u32[]{:S(2)}) collective-permute-start(bf16[512,256]{1,0:T(8,128)(2,1)S(1)} %pick.1), channel_id=1, source_target_pairs={{0,6},{1,7},{2,4},{3,5},{4,2},{5,3},{6,0},{7,1},{8,14},{9,15},{10,... | collective-permute-start | bytes 786440 | tf_op jit(solution)/shard_map/ppermute | solution.py:17
  74.2 1.2 collective-permute-start.4
  75.7 1.2 project.5.refs_4_
  76.9 1.3 %project.6.refs_4_ = f32[2,512,256]{2,1,0:T(8,128)S(1)} custom-call(bf16[512,2048]{1,0:T(8,128)(2,1)S(1)} %stage.6.acts, bf16[512,2048]{1,0:T(8,128)(2,1)S(1)} %collective-permute-done.13.other, bf16[512,256]{1,0:T(8,128)(2,1)S(1)} %collective-permute-done.2.refs_0_, bf16[512,256]{1,0:T(8,128)(2,1)S(1)} %collective-permute-done.14.refs_1_, ...), custom_call_target="tpu_custom_call" | custom-call | flops 1073741824 | bytes 4194304 | tf_op jit(solution)/shard_map/project/pallas_call | solution.py:187
  78.2 1.3 %project.7.refs_2_ = f32[2,512,256]{2,1,0:T(8,128)S(1)} custom-call(bf16[512,2048]{1,0:T(8,128)(2,1)S(1)} %stage.5.acts, bf16[512,2048]{1,0:T(8,128)(2,1)S(1)} %collective-permute-done.8.other, bf16[512,256]{1,0:T(8,128)(2,1)S(1)} %collective-permute-done.9.refs_0_, bf16[512,256]{1,0:T(8,128)(2,1)S(1)} %collective-permute-done.10.refs_1_, ...), custom_call_target="tpu_custom_call" | custom-call | flops 1073741824 | bytes 4194304 | tf_op jit(solution)/shard_map/project/pallas_call | solution.py:187
  79.5 0.6 collective-permute-done.7.refs_1_
  80.1 0.7 project.8.refs_2_
  80.8 0.9 project.9
  81.8 11.3 %collective-permute-start.18 = (bf16[2,2,512,256]{3,2,1,0:T(8,128)(2,1)S(1)}, bf16[2,2,512,256]{3,2,1,0:T(8,128)(2,1)S(1)}, u32[]{:S(2)}, u32[]{:S(2)}) collective-permute-start(bf16[2,2,512,256]{3,2,1,0:T(8,128)(2,1)S(1)} %get-tuple-element.20.own), channel_id=1, source_target_pairs={{0,1},{1,0},{2,3},{3,2},{4,5},{5,4},{6,7},{7,6},{8,9},{9,8},{10,11... | collective-permute-start | bytes 3145736 | tf_op jit(solution)/shard_map/ppermute | solution.py:17
  93.2 0.6 inner_gram.1.inner
  93.8 1.6 %collective-permute-done.19.oth_sums = f32[8,256]{1,0:T(8,128)S(1)} collective-permute-done((f32[8,256]{1,0:T(8,128)S(1)}, f32[8,256]{1,0:T(8,128)S(1)}, u32[]{:S(2)}, u32[]{:S(2)}) %collective-permute-start.19) | collective-permute-done | bytes 8224 | tf_op jit(solution)/shard_map/ppermute | solution.py:17
  95.4 1.0 gram.1
  96.5 0.8 collective-permute-start.20
  97.4 2.8 %collective-permute-start.22 = (f16[136,512]{1,0:T(8,128)(2,1)S(1)}, f16[136,512]{1,0:T(8,128)(2,1)S(1)}, u32[]{:S(2)}, u32[]{:S(2)}) collective-permute-start(f16[136,512]{1,0:T(8,128)(2,1)S(1)} %convert_element_type.22), channel_id=1, source_target_pairs={{0,2},{1,3},{2,0},{3,1},{4,6},{5,7},{6,4},{7,5},{8,10},{9,11},{10,... | collective-permute-start | bytes 417800 | tf_op jit(solution)/shard_map/ppermute | solution.py:17
  100.2 3.0 %collective-permute-done.20 = f16[136,512]{1,0:T(8,128)(2,1)S(1)} collective-permute-done((f16[136,512]{1,0:T(8,128)(2,1)S(1)}, f16[136,512]{1,0:T(8,128)(2,1)S(1)}, u32[]{:S(2)}, u32[]{:S(2)}) %collective-permute-start.20) | collective-permute-done | bytes 139296 | tf_op jit(solution)/shard_map/ppermute | solution.py:17
  103.2 6.6 %collective-permute-done.21 = f16[136,512]{1,0:T(8,128)(2,1)S(1)} collective-permute-done((f16[136,512]{1,0:T(8,128)(2,1)S(1)}, f16[136,512]{1,0:T(8,128)(2,1)S(1)}, u32[]{:S(2)}, u32[]{:S(2)}) %collective-permute-start.21) | collective-permute-done | bytes 139296 | tf_op jit(solution)/shard_map/ppermute | solution.py:17
  109.9 0.5 finish.1
  110.4 0.6 collective-permute-start.23
  111.0 2.8 %collective-permute-start.24 = (bf16[64,512]{1,0:T(8,128)(2,1)S(1)}, bf16[64,512]{1,0:T(8,128)(2,1)S(1)}, u32[]{:S(2)}, u32[]{:S(2)}) collective-permute-start(bf16[64,512]{1,0:T(8,128)(2,1)S(1)} %get-tuple-element.29), channel_id=1, source_target_pairs={{8,16},{16,8},{9,17},{17,9},{10,18},{18,10},{11,19},{19,11},{12,20... | collective-permute-start | bytes 196616 | tf_op jit(solution)/shard_map/ppermute | solution.py:458
  113.8 3.1 %collective-permute-done.24.two = bf16[64,512]{1,0:T(8,128)(2,1)S(1)} collective-permute-done((bf16[64,512]{1,0:T(8,128)(2,1)S(1)}, bf16[64,512]{1,0:T(8,128)(2,1)S(1)}, u32[]{:S(2)}, u32[]{:S(2)}) %collective-permute-start.24) | collective-permute-done | bytes 65568 | tf_op jit(solution)/shard_map/ppermute | solution.py:458
  117.2 2.1 %collective-permute-start.25 = (f32[8,128]{1,0:T(8,128)S(1)}, f32[8,128]{1,0:T(8,128)S(1)}, u32[]{:S(2)}, u32[]{:S(2)}) collective-permute-start(f32[8,128]{1,0:T(8,128)S(1)} %products.1), channel_id=1, source_target_pairs={{0,1},{1,0},{2,3},{3,2},{4,5},{5,4},{6,7},{7,6},{8,9},{9,8},{10,11... | collective-permute-start | bytes 12296 | tf_op jit(solution)/shard_map/ppermute | solution.py:17
  119.2 0.8 collective-permute-done.25
  120.1 2.5 %collective-permute-done.26 = f32[8,128]{1,0:T(8,128)S(1)} collective-permute-done((f32[8,128]{1,0:T(8,128)S(1)}, f32[8,128]{1,0:T(8,128)S(1)}, u32[]{:S(2)}, u32[]{:S(2)}) %collective-permute-start.26) | collective-permute-done | bytes 4128 | tf_op jit(solution)/shard_map/ppermute | solution.py:17
  122.8 0.9 copy.4
  123.7 2.2 %collective-permute-done.27.two = f32[8,128]{1,0:T(8,128)S(1)} collective-permute-done((f32[8,128]{1,0:T(8,128)S(1)}, f32[8,128]{1,0:T(8,128)S(1)}, u32[]{:S(2)}, u32[]{:S(2)}) %collective-permute-start.27) | collective-permute-done | bytes 4128 | tf_op jit(solution)/shard_map/ppermute | solution.py:17
  125.9 0.6 ratios.1
  (41 shorter events, 3.8 us)
Async XLA Ops:
  0.6 3.4 %copy-start.1 = (bf16[2,256,8192]{2,1,0:T(8,128)(2,1)S(1)}, bf16[2,256,8192]{2,1,0:T(8,128)(2,1)}, u32[]{:S(2)}) copy-start(bf16[2,256,8192]{2,1,0:T(8,128)(2,1)} %param.2) | copy-start | bytes 25165828
  4.0 1.3 %copy-start = (bf16[1024,512]{1,0:T(8,128)(2,1)S(1)}, bf16[1024,512]{1,0:T(8,128)(2,1)}, u32[]{:S(2)}) copy-start(bf16[1024,512]{1,0:T(8,128)(2,1)} %proj.3) | copy-start | bytes 3145732
  4.0 3.7 %copy-start.2 = (bf16[2,256,8192]{2,1,0:T(8,128)(2,1)S(1)}, bf16[2,256,8192]{2,1,0:T(8,128)(2,1)}, u32[]{:S(2)}) copy-start(bf16[2,256,8192]{2,1,0:T(8,128)(2,1)} %param.2) | copy-start | bytes 25165828
  4.5 69.7 %collective-permute-start.17 = (bf16[512,2048]{1,0:T(8,128)(2,1)S(1)}, bf16[512,2048]{1,0:T(8,128)(2,1)S(1)}, u32[]{:S(2)}, u32[]{:S(2)}) collective-permute-start(bf16[512,2048]{1,0:T(8,128)(2,1)S(1)} %stage.7.acts), channel_id=1, source_target_pairs={{0,1},{1,0},{2,3},{3,2},{4,5},{5,4},{6,7},{7,6},{8,9},{9,8},{10,11... | collective-permute-start | bytes 6291464 | tf_op jit(solution)/shard_map/ppermute | solution.py:17
  6.2 20.9 %collective-permute-start.6 = (bf16[1024,256]{1,0:T(8,128)(2,1)S(1)}, bf16[1024,256]{1,0:T(8,128)(2,1)S(1)}, u32[]{:S(2)}, u32[]{:S(2)}) collective-permute-start(bf16[1024,256]{1,0:T(8,128)(2,1)S(1)} %get-tuple-element.19), channel_id=1, source_target_pairs={{0,1},{1,0},{2,3},{3,2},{4,5},{5,4},{6,7},{7,6},{8,9},{9,8},{10,11... | collective-permute-start | bytes 1572872 | tf_op jit(solution)/shard_map/ppermute | solution.py:17
  7.4 2.6 %collective-permute-start.1 = (bf16[256,256]{1,0:T(8,128)(2,1)S(1)}, bf16[256,256]{1,0:T(8,128)(2,1)S(1)}, u32[]{:S(2)}, u32[]{:S(2)}) collective-permute-start(bf16[256,256]{1,0:T(8,128)(2,1)S(1)} %get-tuple-element.17), channel_id=1, source_target_pairs={{0,1},{1,0},{2,3},{3,2},{4,5},{5,4},{6,7},{7,6},{8,9},{9,8},{10,11... | collective-permute-start | bytes 393224 | tf_op jit(solution)/shard_map/ppermute | solution.py:17
  8.3 67.2 %collective-permute-start.13 = (bf16[512,2048]{1,0:T(8,128)(2,1)S(1)}, bf16[512,2048]{1,0:T(8,128)(2,1)S(1)}, u32[]{:S(2)}, u32[]{:S(2)}) collective-permute-start(bf16[512,2048]{1,0:T(8,128)(2,1)S(1)} %stage.6.acts), channel_id=1, source_target_pairs={{0,1},{1,0},{2,3},{3,2},{4,5},{5,4},{6,7},{7,6},{8,9},{9,8},{10,11... | collective-permute-start | bytes 6291464 | tf_op jit(solution)/shard_map/ppermute | solution.py:17
  10.0 14.1 %collective-permute-start.2 = (bf16[512,256]{1,0:T(8,128)(2,1)S(1)}, bf16[512,256]{1,0:T(8,128)(2,1)S(1)}, u32[]{:S(2)}, u32[]{:S(2)}) collective-permute-start(bf16[512,256]{1,0:T(8,128)(2,1)S(1)} %join.1), channel_id=1, source_target_pairs={{0,4},{1,5},{2,6},{3,7},{4,0},{5,1},{6,2},{7,3},{8,12},{9,13},{10,... | collective-permute-start | bytes 786440 | tf_op jit(solution)/shard_map/ppermute | solution.py:17
  12.4 13.0 %collective-permute-start.9 = (bf16[512,256]{1,0:T(8,128)(2,1)S(1)}, bf16[512,256]{1,0:T(8,128)(2,1)S(1)}, u32[]{:S(2)}, u32[]{:S(2)}) collective-permute-start(bf16[512,256]{1,0:T(8,128)(2,1)S(1)} %join.1), channel_id=1, source_target_pairs={{0,2},{1,3},{2,0},{3,1},{4,6},{5,7},{6,4},{7,5},{8,10},{9,11},{10,... | collective-permute-start | bytes 786440 | tf_op jit(solution)/shard_map/ppermute | solution.py:17
  24.1 54.1 %collective-permute-start.8 = (bf16[512,2048]{1,0:T(8,128)(2,1)S(1)}, bf16[512,2048]{1,0:T(8,128)(2,1)S(1)}, u32[]{:S(2)}, u32[]{:S(2)}) collective-permute-start(bf16[512,2048]{1,0:T(8,128)(2,1)S(1)} %stage.5.acts), channel_id=1, source_target_pairs={{0,1},{1,0},{2,3},{3,2},{4,5},{5,4},{6,7},{7,6},{8,9},{9,8},{10,11... | collective-permute-start | bytes 6291464 | tf_op jit(solution)/shard_map/ppermute | solution.py:17
  25.4 7.7 %collective-permute-start.14 = (bf16[512,256]{1,0:T(8,128)(2,1)S(1)}, bf16[512,256]{1,0:T(8,128)(2,1)S(1)}, u32[]{:S(2)}, u32[]{:S(2)}) collective-permute-start(bf16[512,256]{1,0:T(8,128)(2,1)S(1)} %collective-permute-done.2.refs_0_), channel_id=1, source_target_pairs={{0,8},{8,0},{16,24},{24,16},{1,9},{9,1},{17,25},{25,17},{2,10},{10... | collective-permute-start | bytes 786440 | tf_op jit(solution)/shard_map/ppermute | solution.py:17
  27.2 52.9 %collective-permute-start = (bf16[512,2048]{1,0:T(8,128)(2,1)S(1)}, bf16[512,2048]{1,0:T(8,128)(2,1)S(1)}, u32[]{:S(2)}, u32[]{:S(2)}) collective-permute-start(bf16[512,2048]{1,0:T(8,128)(2,1)S(1)} %stage.4.acts), channel_id=1, source_target_pairs={{0,1},{1,0},{2,3},{3,2},{4,5},{5,4},{6,7},{7,6},{8,9},{9,8},{10,11... | collective-permute-start | bytes 6291464 | tf_op jit(solution)/shard_map/ppermute | solution.py:17
  33.1 6.8 %collective-permute-start.15 = (bf16[512,256]{1,0:T(8,128)(2,1)S(1)}, bf16[512,256]{1,0:T(8,128)(2,1)S(1)}, u32[]{:S(2)}, u32[]{:S(2)}) collective-permute-start(bf16[512,256]{1,0:T(8,128)(2,1)S(1)} %collective-permute-done.2.refs_0_), channel_id=1, source_target_pairs={{0,16},{8,24},{16,0},{24,8},{1,17},{9,25},{17,1},{25,9},{2,18},{10... | collective-permute-start | bytes 786440 | tf_op jit(solution)/shard_map/ppermute | solution.py:17
  39.9 6.9 %collective-permute-start.16 = (bf16[512,256]{1,0:T(8,128)(2,1)S(1)}, bf16[512,256]{1,0:T(8,128)(2,1)S(1)}, u32[]{:S(2)}, u32[]{:S(2)}) collective-permute-start(bf16[512,256]{1,0:T(8,128)(2,1)S(1)} %collective-permute-done.2.refs_0_), channel_id=1, source_target_pairs={{0,24},{8,16},{16,8},{24,0},{1,25},{9,17},{17,9},{25,1},{2,26},{10... | collective-permute-start | bytes 786440 | tf_op jit(solution)/shard_map/ppermute | solution.py:17
  46.8 5.2 %collective-permute-start.10 = (bf16[512,256]{1,0:T(8,128)(2,1)S(1)}, bf16[512,256]{1,0:T(8,128)(2,1)S(1)}, u32[]{:S(2)}, u32[]{:S(2)}) collective-permute-start(bf16[512,256]{1,0:T(8,128)(2,1)S(1)} %collective-permute-done.9.refs_0_), channel_id=1, source_target_pairs={{0,8},{8,0},{16,24},{24,16},{1,9},{9,1},{17,25},{25,17},{2,10},{10... | collective-permute-start | bytes 786440 | tf_op jit(solution)/shard_map/ppermute | solution.py:17
  52.0 5.2 %collective-permute-start.11 = (bf16[512,256]{1,0:T(8,128)(2,1)S(1)}, bf16[512,256]{1,0:T(8,128)(2,1)S(1)}, u32[]{:S(2)}, u32[]{:S(2)}) collective-permute-start(bf16[512,256]{1,0:T(8,128)(2,1)S(1)} %collective-permute-done.9.refs_0_), channel_id=1, source_target_pairs={{0,16},{8,24},{16,0},{24,8},{1,17},{9,25},{17,1},{25,9},{2,18},{10... | collective-permute-start | bytes 786440 | tf_op jit(solution)/shard_map/ppermute | solution.py:17
  57.2 5.2 %collective-permute-start.3 = (bf16[512,256]{1,0:T(8,128)(2,1)S(1)}, bf16[512,256]{1,0:T(8,128)(2,1)S(1)}, u32[]{:S(2)}, u32[]{:S(2)}) collective-permute-start(bf16[512,256]{1,0:T(8,128)(2,1)S(1)} %collective-permute-done.2.refs_0_), channel_id=1, source_target_pairs={{0,2},{1,3},{2,0},{3,1},{4,6},{5,7},{6,4},{7,5},{8,10},{9,11},{10,... | collective-permute-start | bytes 786440 | tf_op jit(solution)/shard_map/ppermute | solution.py:17
  62.4 8.0 %collective-permute-start.12 = (bf16[512,256]{1,0:T(8,128)(2,1)S(1)}, bf16[512,256]{1,0:T(8,128)(2,1)S(1)}, u32[]{:S(2)}, u32[]{:S(2)}) collective-permute-start(bf16[512,256]{1,0:T(8,128)(2,1)S(1)} %pick.1), channel_id=1, source_target_pairs={{0,2},{1,3},{2,0},{3,1},{4,6},{5,7},{6,4},{7,5},{8,10},{9,11},{10,... | collective-permute-start | bytes 786440 | tf_op jit(solution)/shard_map/ppermute | solution.py:17
  70.5 9.6 %collective-permute-start.7 = (bf16[512,256]{1,0:T(8,128)(2,1)S(1)}, bf16[512,256]{1,0:T(8,128)(2,1)S(1)}, u32[]{:S(2)}, u32[]{:S(2)}) collective-permute-start(bf16[512,256]{1,0:T(8,128)(2,1)S(1)} %pick.1), channel_id=1, source_target_pairs={{0,6},{1,7},{2,4},{3,5},{4,2},{5,3},{6,0},{7,1},{8,14},{9,15},{10,... | collective-permute-start | bytes 786440 | tf_op jit(solution)/shard_map/ppermute | solution.py:17
  74.2 6.6 %collective-permute-start.4 = (bf16[512,256]{1,0:T(8,128)(2,1)S(1)}, bf16[512,256]{1,0:T(8,128)(2,1)S(1)}, u32[]{:S(2)}, u32[]{:S(2)}) collective-permute-start(bf16[512,256]{1,0:T(8,128)(2,1)S(1)} %collective-permute-done.3.refs_0_), channel_id=1, source_target_pairs={{0,8},{8,0},{16,24},{24,16},{1,9},{9,1},{17,25},{25,17},{2,10},{10... | collective-permute-start | bytes 786440 | tf_op jit(solution)/shard_map/ppermute | solution.py:17
  75.4 5.4 %collective-permute-start.5 = (bf16[512,256]{1,0:T(8,128)(2,1)S(1)}, bf16[512,256]{1,0:T(8,128)(2,1)S(1)}, u32[]{:S(2)}, u32[]{:S(2)}) collective-permute-start(bf16[512,256]{1,0:T(8,128)(2,1)S(1)} %collective-permute-done.3.refs_0_), channel_id=1, source_target_pairs={{0,16},{8,24},{16,0},{24,8},{1,17},{9,25},{17,1},{25,9},{2,18},{10... | collective-permute-start | bytes 786440 | tf_op jit(solution)/shard_map/ppermute | solution.py:17
  81.8 13.6 %collective-permute-start.18 = (bf16[2,2,512,256]{3,2,1,0:T(8,128)(2,1)S(1)}, bf16[2,2,512,256]{3,2,1,0:T(8,128)(2,1)S(1)}, u32[]{:S(2)}, u32[]{:S(2)}) collective-permute-start(bf16[2,2,512,256]{3,2,1,0:T(8,128)(2,1)S(1)} %get-tuple-element.20.own), channel_id=1, source_target_pairs={{0,1},{1,0},{2,3},{3,2},{4,5},{5,4},{6,7},{7,6},{8,9},{9,8},{10,11... | collective-permute-start | bytes 3145736 | tf_op jit(solution)/shard_map/ppermute | solution.py:17
  93.1 2.3 %collective-permute-start.19 = (f32[8,256]{1,0:T(8,128)S(1)}, f32[8,256]{1,0:T(8,128)S(1)}, u32[]{:S(2)}, u32[]{:S(2)}) collective-permute-start(f32[8,256]{1,0:T(8,128)S(1)} %get-tuple-element.21.own_sums), channel_id=1, source_target_pairs={{0,1},{1,0},{2,3},{3,2},{4,5},{5,4},{6,7},{7,6},{8,9},{9,8},{10,11... | collective-permute-start | bytes 24584 | tf_op jit(solution)/shard_map/ppermute | solution.py:17
  96.5 6.8 %collective-permute-start.20 = (f16[136,512]{1,0:T(8,128)(2,1)S(1)}, f16[136,512]{1,0:T(8,128)(2,1)S(1)}, u32[]{:S(2)}, u32[]{:S(2)}) collective-permute-start(f16[136,512]{1,0:T(8,128)(2,1)S(1)} %convert_element_type.18), channel_id=1, source_target_pairs={{0,6},{1,7},{2,4},{3,5},{4,2},{5,3},{6,0},{7,1},{8,14},{9,15},{10,... | collective-permute-start | bytes 417800 | tf_op jit(solution)/shard_map/ppermute | solution.py:17
  97.3 12.5 %collective-permute-start.21 = (f16[136,512]{1,0:T(8,128)(2,1)S(1)}, f16[136,512]{1,0:T(8,128)(2,1)S(1)}, u32[]{:S(2)}, u32[]{:S(2)}) collective-permute-start(f16[136,512]{1,0:T(8,128)(2,1)S(1)} %convert_element_type.20), channel_id=1, source_target_pairs={{0,4},{1,5},{2,6},{3,7},{4,0},{5,1},{6,2},{7,3},{8,12},{9,13},{10,... | collective-permute-start | bytes 417800 | tf_op jit(solution)/shard_map/ppermute | solution.py:17
  97.4 12.4 %collective-permute-start.22 = (f16[136,512]{1,0:T(8,128)(2,1)S(1)}, f16[136,512]{1,0:T(8,128)(2,1)S(1)}, u32[]{:S(2)}, u32[]{:S(2)}) collective-permute-start(f16[136,512]{1,0:T(8,128)(2,1)S(1)} %convert_element_type.22), channel_id=1, source_target_pairs={{0,2},{1,3},{2,0},{3,1},{4,6},{5,7},{6,4},{7,5},{8,10},{9,11},{10,... | collective-permute-start | bytes 417800 | tf_op jit(solution)/shard_map/ppermute | solution.py:17
  110.4 3.4 %collective-permute-start.23 = (bf16[64,512]{1,0:T(8,128)(2,1)S(1)}, bf16[64,512]{1,0:T(8,128)(2,1)S(1)}, u32[]{:S(2)}, u32[]{:S(2)}) collective-permute-start(bf16[64,512]{1,0:T(8,128)(2,1)S(1)} %get-tuple-element.28), channel_id=1, source_target_pairs={{0,8},{8,0},{16,24},{24,16},{1,9},{9,1},{17,25},{25,17},{2,10},{10... | collective-permute-start | bytes 196616 | tf_op jit(solution)/shard_map/ppermute | solution.py:17
  111.0 5.9 %collective-permute-start.24 = (bf16[64,512]{1,0:T(8,128)(2,1)S(1)}, bf16[64,512]{1,0:T(8,128)(2,1)S(1)}, u32[]{:S(2)}, u32[]{:S(2)}) collective-permute-start(bf16[64,512]{1,0:T(8,128)(2,1)S(1)} %get-tuple-element.29), channel_id=1, source_target_pairs={{8,16},{16,8},{9,17},{17,9},{10,18},{18,10},{11,19},{19,11},{12,20... | collective-permute-start | bytes 196616 | tf_op jit(solution)/shard_map/ppermute | solution.py:458
  117.2 2.9 %collective-permute-start.25 = (f32[8,128]{1,0:T(8,128)S(1)}, f32[8,128]{1,0:T(8,128)S(1)}, u32[]{:S(2)}, u32[]{:S(2)}) collective-permute-start(f32[8,128]{1,0:T(8,128)S(1)} %products.1), channel_id=1, source_target_pairs={{0,1},{1,0},{2,3},{3,2},{4,5},{5,4},{6,7},{7,6},{8,9},{9,8},{10,11... | collective-permute-start | bytes 12296 | tf_op jit(solution)/shard_map/ppermute | solution.py:17
  120.1 2.5 %collective-permute-start.26 = (f32[8,128]{1,0:T(8,128)S(1)}, f32[8,128]{1,0:T(8,128)S(1)}, u32[]{:S(2)}, u32[]{:S(2)}) collective-permute-start(f32[8,128]{1,0:T(8,128)S(1)} %add.6), channel_id=1, source_target_pairs={{0,2},{1,3},{2,0},{3,1},{4,6},{5,7},{6,4},{7,5},{8,10},{9,11},{10,... | collective-permute-start | bytes 12296 | tf_op jit(solution)/shard_map/ppermute | solution.py:17
  122.5 3.4 %collective-permute-start.27 = (f32[8,128]{1,0:T(8,128)S(1)}, f32[8,128]{1,0:T(8,128)S(1)}, u32[]{:S(2)}, u32[]{:S(2)}) collective-permute-start(f32[8,128]{1,0:T(8,128)S(1)} %add.7.one), channel_id=1, source_target_pairs={{0,4},{1,5},{2,6},{3,7},{4,0},{5,1},{6,2},{7,3},{8,12},{9,13},{10,... | collective-permute-start | bytes 12296 | tf_op jit(solution)/shard_map/ppermute | solution.py:17

commit v4 on v3

--- a/solution.py
+++ b/solution.py
@@ -30,13 +30,8 @@
     return pl.CostEstimate(flops=int(flops), bytes_accessed=int(moved), transcendentals=0)
 
 
-def deal_kernel(width, rows, proj, mine, give, block, sem):
-    _, core, section = place()
-    start = 0
-    if rows < proj.shape[0]:
-        start = pl.multiple_of((section % (proj.shape[0] // rows)) * rows, 16)
-    copy = pltpu.make_async_copy(proj.at[pl.ds(start, rows), :], block, sem)
-    copy.start()
+def deal_kernel(width, proj, mine, give):
+    core = place()[1]
     rank, half = proj.shape[1], mine.shape[1]
     row = lax.broadcasted_iota(jnp.int32, (rank, half), 0)
     col = lax.broadcasted_iota(jnp.int32, (rank, half), 1)
@@ -44,20 +39,18 @@
     picks = [
         jnp.where(row == first + side * width, 1.0, 0.0).astype(BF16) for side in (core, 1 - core)
     ]
-    copy.wait()
     for out, pick in zip((mine, give), picks):
-        out[...] = jnp.dot(block[...], pick, preferred_element_type=F32).astype(BF16)
-
-
-def deal(proj, width, rows):
-    rank = proj.shape[1]
+        out[...] = jnp.dot(proj[...], pick, preferred_element_type=F32).astype(BF16)
+
+
+def deal(proj, width):
+    rows, rank = proj.shape
     half = jax.ShapeDtypeStruct((rows, rank // 2), BF16)
     return pl.pallas_call(
-        functools.partial(deal_kernel, width, rows),
+        functools.partial(deal_kernel, width),
         out_shape=(half, half),
-        in_specs=[HBM],
+        in_specs=[VMEM],
         out_specs=(VMEM, VMEM),
-        scratch_shapes=[pltpu.VMEM((rows, rank), BF16), pltpu.SemaphoreType.DMA],
         compiler_params=params(4),
         cost_estimate=cost(2 * rows * rank * rank, 4 * rows * rank),
         name="deal",
@@ -375,8 +368,9 @@
     )(turned, one, two)
 
 
-def ratios_kernel(layers, one, two, out):
-    value = one[...] + two[...]
+def ratios_kernel(layers, *refs):
+    out = refs[-1]
+    value = sum(ref[...] for ref in refs[:-1])
     squares = value[: layers + 2]
     chained = value[layers + 2 : 2 * layers + 3]
     ratio = chained / jnp.sqrt(squares[:-1] * squares[1:])
@@ -384,16 +378,16 @@
     out[:, 1:2] = ratio[1:, 0:1]
 
 
-def ratios(one, two, layers):
+def ratios(shares, layers):
     return pl.pallas_call(
         functools.partial(ratios_kernel, layers),
         out_shape=jax.ShapeDtypeStruct((layers, 2), F32),
-        in_specs=[VMEM] * 2,
+        in_specs=[VMEM] * len(shares),
         out_specs=VMEM,
         compiler_params=params(4),
         cost_estimate=cost(1e4, 1e4),
         name="ratios",
-    )(one, two)
+    )(*shares)
 
 
 def local(activations, projection):
@@ -405,7 +399,9 @@
     deep = block // parts
 
     acts = activations.reshape(layers * tok_rows, model)
-    mine_part, give_part = deal(projection, width, deep)
+    start = (lax.axis_index("section") & (parts - 1)) * deep
+    part = lax.dynamic_slice_in_dim(projection, start, deep, 0)
+    mine_part, give_part = deal(part, width)
     got_part = swap(give_part, "tok", 1)
     own = join(mine_part, got_part)
 
@@ -414,7 +410,7 @@
         low = k & -k
         fetched[k] = swap(own if k == low else fetched[k ^ low], "tok", 2 * low)
 
-    mine, give = deal(projection, width, block)
+    mine, give = deal(projection, width)
     got = swap(give, "tok", 1)
 
     order = sorted(fetched, key=lambda k: (bin(k).count("1"), k))
@@ -436,8 +432,9 @@
     total = project([mine, got], (None, None), parts, None, *staged[0], layers, False)
     final, keys = order[-1], tuple(range(parts))
     late = tuple(j for j in keys[1:] if j not in far)
-    steps = [(k, keys) for k in reversed(order[:-1])]
-    steps += [(final, tuple(j for j in keys if j not in late)), (final, late)]
+    steps = [(k, keys) for k in reversed(order[1:-1])]
+    steps += [(final, tuple(j for j in keys if j not in late))]
+    steps += [(k, keys) for k in order[:-1][:1]] + [(final, late)]
     steps = [step for step in steps if step[1]]
     for k, js in steps:
         last = (k, js) == steps[-1]
@@ -458,11 +455,18 @@
     second = lax.ppermute(second, "section", route + [(b, a) for a, b in route])
     first = swap(first, "section", 1)
     value = products(turned, first, second, sections)
-    mask = 1
-    while 2 * mask < groups:
-        value = value + swap(value, "tok", mask)
-        mask *= 2
-    return sketch, ratios(value, swap(value, "tok", mask), layers)
+    value = value + swap(value, "tok", 1)
+    if chips <= 4:
+        others = []
+        for k in reversed(range(1, chips)):
+            others.append(swap(value, "tok", 2 * k))
+    else:
+        mask = 2
+        while 2 * mask < groups:
+            value = value + swap(value, "tok", mask)
+            mask *= 2
+        others = [swap(value, "tok", mask)]
+    return sketch, ratios([value] + others, layers)
 
 
 def solution(mesh):

time: 129 us -> 129 us (level)
  waiting for transfers between devices: 71.3 us -> 62.9 us
  starting transfers between devices: 37.7 us -> 43.4 us
  local copies, waits for them, and re-layouts: 4.5 us -> 7.55 us
    ppermute x27 -> x28, waiting for transfers between devices: 68.2 us -> 61.1 us  [swap(): lax.ppermute(block, axis, [(i, i ^ mask) for i in range(lax.axis_size(axi...]
    ppermute x27 -> x28, starting transfers between devices: 35 us -> 38.9 us  [swap(): lax.ppermute(block, axis, [(i, i ^ mask) for i in range(lax.axis_size(axi...]
    unnamed x7, local copies, waits for them, and re-layouts: 4.5 us -> 6.58 us
    ppermute x1, starting transfers between devices: 2.76 us -> 4.5 us  [local(): second = lax.ppermute(second, 'section', route + [(b, a) for a, b in route])]
  transfers between devices with their start and end apart: 28 -> 29, of which waited for: 17 -> 15; matrix products, arithmetic and copies ran while one was open for 1% -> 1% of each run, Pallas kernels for 6% -> 6%
where the time goes in v4:
time: 129 us; the launch traced here: 126 us
  waiting for transfers between devices  62.9 us (49%)
  starting transfers between devices  43.4 us (34%)
  Pallas kernels  11.6 us (9%)
  local copies, waits for them, and re-layouts  7.55 us (6%)
    ppermute x28, waiting for transfers between devices, swap(): lax.ppermute(block, axis, [(i, i ^ mask) for i in range(lax.axis_size(axi...  61.1 us
    ppermute x28, starting transfers between devices, swap(): lax.ppermute(block, axis, [(i, i ^ mask) for i in range(lax.axis_size(axi...  38.9 us
    unnamed x7, local copies, waits for them, and re-layouts  6.58 us
    pallas_call x5, Pallas kernels, project(): pl.pallas_call(functools.partial(project_kernel, keys, parts, len(started...  5.44 us
    ppermute x1, starting transfers between devices, local(): second = lax.ppermute(second, 'section', route + [(b, a) for a, b in route])  4.5 us
  transfers between devices with their start and end apart: 29, of which 15 were waited for; matrix products, arithmetic and copies ran while one was open for 1% of the time, Pallas kernels for 6%

profile of v4, /device:TPU:5, one launch (start us, length us, event | category | flops | bytes accessed | tf_op | source)
XLA Modules:
  0.0 126.5 jit_solution(6399511172947990502)
XLA Ops:
  0.6 1.0 constant_dynamic-slice_fusion.proj
  1.9 0.7 collective-permute-start.1
  2.7 3.4 %copy-done.1 = bf16[2,256,8192]{2,1,0:T(8,128)(2,1)S(1)} copy-done((bf16[2,256,8192]{2,1,0:T(8,128)(2,1)S(1)}, bf16[2,256,8192]{2,1,0:T(8,128)(2,1)}, u32[]{:S(2)}) %copy-start.1) | copy-done | bytes 8388632
  6.7 0.6 copy-done
  7.3 0.7 deal.3
  8.1 1.7 %copy-done.2 = bf16[2,256,8192]{2,1,0:T(8,128)(2,1)S(1)} copy-done((bf16[2,256,8192]{2,1,0:T(8,128)(2,1)S(1)}, bf16[2,256,8192]{2,1,0:T(8,128)(2,1)}, u32[]{:S(2)}) %copy-start.2) | copy-done | bytes 8388632
  10.4 2.4 %collective-permute-start.2 = (bf16[512,256]{1,0:T(8,128)(2,1)S(1)}, bf16[512,256]{1,0:T(8,128)(2,1)S(1)}, u32[]{:S(2)}, u32[]{:S(2)}) collective-permute-start(bf16[512,256]{1,0:T(8,128)(2,1)S(1)} %join.1), channel_id=1, source_target_pairs={{0,4},{1,5},{2,6},{3,7},{4,0},{5,1},{6,2},{7,3},{8,12},{9,13},{10,... | collective-permute-start | bytes 786440 | tf_op jit(solution)/shard_map/ppermute | solution.py:17
  13.3 0.8 collective-permute-start
  14.1 10.2 %collective-permute-done.2.refs_0_ = bf16[512,256]{1,0:T(8,128)(2,1)S(1)} collective-permute-done((bf16[512,256]{1,0:T(8,128)(2,1)S(1)}, bf16[512,256]{1,0:T(8,128)(2,1)S(1)}, u32[]{:S(2)}, u32[]{:S(2)}) %collective-permute-start.2) | collective-permute-done | bytes 262176 | tf_op jit(solution)/shard_map/ppermute | solution.py:17
  24.4 1.2 collective-permute-start.7
  26.1 4.8 %collective-permute-done.7.refs_0_ = bf16[512,256]{1,0:T(8,128)(2,1)S(1)} collective-permute-done((bf16[512,256]{1,0:T(8,128)(2,1)S(1)}, bf16[512,256]{1,0:T(8,128)(2,1)S(1)}, u32[]{:S(2)}, u32[]{:S(2)}) %collective-permute-start.7) | collective-permute-done | bytes 262176 | tf_op jit(solution)/shard_map/ppermute | solution.py:17
  30.9 2.2 %collective-permute-start.6 = (bf16[512,2048]{1,0:T(8,128)(2,1)S(1)}, bf16[512,2048]{1,0:T(8,128)(2,1)S(1)}, u32[]{:S(2)}, u32[]{:S(2)}) collective-permute-start(bf16[512,2048]{1,0:T(8,128)(2,1)S(1)} %stage.5.acts), channel_id=1, source_target_pairs={{0,1},{1,0},{2,3},{3,2},{4,5},{5,4},{6,7},{7,6},{8,9},{9,8},{10,11... | collective-permute-start | bytes 6291464 | tf_op jit(solution)/shard_map/ppermute | solution.py:17
  33.1 1.2 collective-permute-start.14
  34.3 6.7 %collective-permute-done.14.refs_1_ = bf16[512,256]{1,0:T(8,128)(2,1)S(1)} collective-permute-done((bf16[512,256]{1,0:T(8,128)(2,1)S(1)}, bf16[512,256]{1,0:T(8,128)(2,1)S(1)}, u32[]{:S(2)}, u32[]{:S(2)}) %collective-permute-start.14) | collective-permute-done | bytes 262176 | tf_op jit(solution)/shard_map/ppermute | solution.py:17
  41.4 6.6 %collective-permute-done.15.refs_2_ = bf16[512,256]{1,0:T(8,128)(2,1)S(1)} collective-permute-done((bf16[512,256]{1,0:T(8,128)(2,1)S(1)}, bf16[512,256]{1,0:T(8,128)(2,1)S(1)}, u32[]{:S(2)}, u32[]{:S(2)}) %collective-permute-start.15) | collective-permute-done | bytes 262176 | tf_op jit(solution)/shard_map/ppermute | solution.py:17
  48.0 1.2 collective-permute-start.16
  49.1 5.9 %collective-permute-done.16.refs_3_ = bf16[512,256]{1,0:T(8,128)(2,1)S(1)} collective-permute-done((bf16[512,256]{1,0:T(8,128)(2,1)S(1)}, bf16[512,256]{1,0:T(8,128)(2,1)S(1)}, u32[]{:S(2)}, u32[]{:S(2)}) %collective-permute-start.16) | collective-permute-done | bytes 262176 | tf_op jit(solution)/shard_map/ppermute | solution.py:17
  55.0 1.2 collective-permute-start.3
  56.3 4.0 %collective-permute-done.3.refs_0_ = bf16[512,256]{1,0:T(8,128)(2,1)S(1)} collective-permute-done((bf16[512,256]{1,0:T(8,128)(2,1)S(1)}, bf16[512,256]{1,0:T(8,128)(2,1)S(1)}, u32[]{:S(2)}, u32[]{:S(2)}) %collective-permute-start.3) | collective-permute-done | bytes 262176 | tf_op jit(solution)/shard_map/ppermute | solution.py:17
  60.2 1.2 collective-permute-start.8
  61.5 4.0 %collective-permute-done.8.refs_1_ = bf16[512,256]{1,0:T(8,128)(2,1)S(1)} collective-permute-done((bf16[512,256]{1,0:T(8,128)(2,1)S(1)}, bf16[512,256]{1,0:T(8,128)(2,1)S(1)}, u32[]{:S(2)}, u32[]{:S(2)}) %collective-permute-start.8) | collective-permute-done | bytes 262176 | tf_op jit(solution)/shard_map/ppermute | solution.py:17
  65.5 4.1 %collective-permute-start.12 = (bf16[512,256]{1,0:T(8,128)(2,1)S(1)}, bf16[512,256]{1,0:T(8,128)(2,1)S(1)}, u32[]{:S(2)}, u32[]{:S(2)}) collective-permute-start(bf16[512,256]{1,0:T(8,128)(2,1)S(1)} %pick.1), channel_id=1, source_target_pairs={{0,6},{1,7},{2,4},{3,5},{4,2},{5,3},{6,0},{7,1},{8,14},{9,15},{10,... | collective-permute-start | bytes 786440 | tf_op jit(solution)/shard_map/ppermute | solution.py:17
  69.5 3.9 %collective-permute-done.12.refs_1_ = bf16[512,256]{1,0:T(8,128)(2,1)S(1)} collective-permute-done((bf16[512,256]{1,0:T(8,128)(2,1)S(1)}, bf16[512,256]{1,0:T(8,128)(2,1)S(1)}, u32[]{:S(2)}, u32[]{:S(2)}) %collective-permute-start.12) | collective-permute-done | bytes 262176 | tf_op jit(solution)/shard_map/ppermute | solution.py:17
  73.6 2.7 %collective-permute-start.11 = (bf16[512,256]{1,0:T(8,128)(2,1)S(1)}, bf16[512,256]{1,0:T(8,128)(2,1)S(1)}, u32[]{:S(2)}, u32[]{:S(2)}) collective-permute-start(bf16[512,256]{1,0:T(8,128)(2,1)S(1)} %pick.1), channel_id=1, source_target_pairs={{0,2},{1,3},{2,0},{3,1},{4,6},{5,7},{6,4},{7,5},{8,10},{9,11},{10,... | collective-permute-start | bytes 786440 | tf_op jit(solution)/shard_map/ppermute | solution.py:17
  76.3 1.2 collective-permute-start.4
  77.5 1.2 collective-permute-start.5
  78.7 1.2 project.5.refs_4_
  80.0 1.3 %project.6.refs_2_ = f32[2,512,256]{2,1,0:T(8,128)S(1)} custom-call(bf16[512,2048]{1,0:T(8,128)(2,1)S(1)} %stage.6.acts, bf16[512,2048]{1,0:T(8,128)(2,1)S(1)} %collective-permute-done.13.other, bf16[512,256]{1,0:T(8,128)(2,1)S(1)} %collective-permute-done.2.refs_0_, bf16[512,256]{1,0:T(8,128)(2,1)S(1)} %collective-permute-done.14.refs_1_, ...), custom_call_target="tpu_custom_call" | custom-call | flops 1073741824 | bytes 4194304 | tf_op jit(solution)/shard_map/project/pallas_call | solution.py:180
  81.3 0.7 project.7.refs_4_
  82.0 1.3 %project.8.refs_2_ = f32[2,512,256]{2,1,0:T(8,128)S(1)} custom-call(bf16[512,2048]{1,0:T(8,128)(2,1)S(1)} %stage.5.acts, bf16[512,2048]{1,0:T(8,128)(2,1)S(1)} %collective-permute-done.6.other, bf16[512,256]{1,0:T(8,128)(2,1)S(1)} %collective-permute-done.7.refs_0_, bf16[512,256]{1,0:T(8,128)(2,1)S(1)} %collective-permute-done.8.refs_1_, ...), custom_call_target="tpu_custom_call" | custom-call | flops 1073741824 | bytes 4194304 | tf_op jit(solution)/shard_map/project/pallas_call | solution.py:180
  83.4 0.9 project.9
  84.3 6.8 %collective-permute-start.18 = (bf16[2,2,512,256]{3,2,1,0:T(8,128)(2,1)S(1)}, bf16[2,2,512,256]{3,2,1,0:T(8,128)(2,1)S(1)}, u32[]{:S(2)}, u32[]{:S(2)}) collective-permute-start(bf16[2,2,512,256]{3,2,1,0:T(8,128)(2,1)S(1)} %get-tuple-element.20.own), channel_id=1, source_target_pairs={{0,1},{1,0},{2,3},{3,2},{4,5},{5,4},{6,7},{7,6},{8,9},{9,8},{10,11... | collective-permute-start | bytes 3145736 | tf_op jit(solution)/shard_map/ppermute | solution.py:17
  91.3 0.6 inner_gram.1.inner
  91.9 1.6 %collective-permute-done.19.oth_sums = f32[8,256]{1,0:T(8,128)S(1)} collective-permute-done((f32[8,256]{1,0:T(8,128)S(1)}, f32[8,256]{1,0:T(8,128)S(1)}, u32[]{:S(2)}, u32[]{:S(2)}) %collective-permute-start.19) | collective-permute-done | bytes 8224 | tf_op jit(solution)/shard_map/ppermute | solution.py:17
  93.5 1.0 gram.1
  94.5 3.1 %collective-permute-start.20 = (f16[136,512]{1,0:T(8,128)(2,1)S(1)}, f16[136,512]{1,0:T(8,128)(2,1)S(1)}, u32[]{:S(2)}, u32[]{:S(2)}) collective-permute-start(f16[136,512]{1,0:T(8,128)(2,1)S(1)} %convert_element_type.18), channel_id=1, source_target_pairs={{0,6},{1,7},{2,4},{3,5},{4,2},{5,3},{6,0},{7,1},{8,14},{9,15},{10,... | collective-permute-start | bytes 417800 | tf_op jit(solution)/shard_map/ppermute | solution.py:17
  97.8 0.5 collective-permute-start.22
  98.3 3.0 %collective-permute-done.20 = f16[136,512]{1,0:T(8,128)(2,1)S(1)} collective-permute-done((f16[136,512]{1,0:T(8,128)(2,1)S(1)}, f16[136,512]{1,0:T(8,128)(2,1)S(1)}, u32[]{:S(2)}, u32[]{:S(2)}) %collective-permute-start.20) | collective-permute-done | bytes 139296 | tf_op jit(solution)/shard_map/ppermute | solution.py:17
  101.3 8.4 %collective-permute-done.21 = f16[136,512]{1,0:T(8,128)(2,1)S(1)} collective-permute-done((f16[136,512]{1,0:T(8,128)(2,1)S(1)}, f16[136,512]{1,0:T(8,128)(2,1)S(1)}, u32[]{:S(2)}, u32[]{:S(2)}) %collective-permute-start.21) | collective-permute-done | bytes 139296 | tf_op jit(solution)/shard_map/ppermute | solution.py:17
  110.5 4.5 %collective-permute-start.24 = (bf16[64,512]{1,0:T(8,128)(2,1)S(1)}, bf16[64,512]{1,0:T(8,128)(2,1)S(1)}, u32[]{:S(2)}, u32[]{:S(2)}) collective-permute-start(bf16[64,512]{1,0:T(8,128)(2,1)S(1)} %get-tuple-element.29), channel_id=1, source_target_pairs={{8,16},{16,8},{9,17},{17,9},{10,18},{18,10},{11,19},{19,11},{12,20... | collective-permute-start | bytes 196616 | tf_op jit(solution)/shard_map/ppermute | solution.py:455
  115.0 1.8 %collective-permute-done.24.two = bf16[64,512]{1,0:T(8,128)(2,1)S(1)} collective-permute-done((bf16[64,512]{1,0:T(8,128)(2,1)S(1)}, bf16[64,512]{1,0:T(8,128)(2,1)S(1)}, u32[]{:S(2)}, u32[]{:S(2)}) %collective-permute-start.24) | collective-permute-done | bytes 65568 | tf_op jit(solution)/shard_map/ppermute | solution.py:455
  117.1 2.3 %collective-permute-start.25 = (f32[8,128]{1,0:T(8,128)S(1)}, f32[8,128]{1,0:T(8,128)S(1)}, u32[]{:S(2)}, u32[]{:S(2)}) collective-permute-start(f32[8,128]{1,0:T(8,128)S(1)} %products.1), channel_id=1, source_target_pairs={{0,1},{1,0},{2,3},{3,2},{4,5},{5,4},{6,7},{7,6},{8,9},{9,8},{10,11... | collective-permute-start | bytes 12296 | tf_op jit(solution)/shard_map/ppermute | solution.py:17
  119.4 0.8 collective-permute-done.25
  120.2 2.3 %collective-permute-start.26 = (f32[8,128]{1,0:T(8,128)S(1)}, f32[8,128]{1,0:T(8,128)S(1)}, u32[]{:S(2)}, u32[]{:S(2)}) collective-permute-start(f32[8,128]{1,0:T(8,128)S(1)} %add.7.refs_0_), channel_id=1, source_target_pairs={{0,6},{1,7},{2,4},{3,5},{4,2},{5,3},{6,0},{7,1},{8,14},{9,15},{10,... | collective-permute-start | bytes 12296 | tf_op jit(solution)/shard_map/ppermute | solution.py:17
  122.5 1.3 %collective-permute-start.28 = (f32[8,128]{1,0:T(8,128)S(1)}, f32[8,128]{1,0:T(8,128)S(1)}, u32[]{:S(2)}, u32[]{:S(2)}) collective-permute-start(f32[8,128]{1,0:T(8,128)S(1)} %add.7.refs_0_), channel_id=1, source_target_pairs={{0,2},{1,3},{2,0},{3,1},{4,6},{5,7},{6,4},{7,5},{8,10},{9,11},{10,... | collective-permute-start | bytes 12296 | tf_op jit(solution)/shard_map/ppermute | solution.py:17
  123.8 0.9 copy.4
  124.7 1.2 collective-permute-done.27.refs_2_
  125.8 0.7 ratios.1
  (43 shorter events, 4.6 us)
Async XLA Ops:
  1.9 8.4 %collective-permute-start.1 = (bf16[256,256]{1,0:T(8,128)(2,1)S(1)}, bf16[256,256]{1,0:T(8,128)(2,1)S(1)}, u32[]{:S(2)}, u32[]{:S(2)}) collective-permute-start(bf16[256,256]{1,0:T(8,128)(2,1)S(1)} %get-tuple-element.17), channel_id=1, source_target_pairs={{0,1},{1,0},{2,3},{3,2},{4,5},{5,4},{6,7},{7,6},{8,9},{9,8},{10,11... | collective-permute-start | bytes 393224 | tf_op jit(solution)/shard_map/ppermute | solution.py:17
  2.7 3.4 %copy-start.1 = (bf16[2,256,8192]{2,1,0:T(8,128)(2,1)S(1)}, bf16[2,256,8192]{2,1,0:T(8,128)(2,1)}, u32[]{:S(2)}) copy-start(bf16[2,256,8192]{2,1,0:T(8,128)(2,1)} %param.2) | copy-start | bytes 25165828
  6.1 1.2 copy-start
  6.1 3.7 %copy-start.2 = (bf16[2,256,8192]{2,1,0:T(8,128)(2,1)S(1)}, bf16[2,256,8192]{2,1,0:T(8,128)(2,1)}, u32[]{:S(2)}) copy-start(bf16[2,256,8192]{2,1,0:T(8,128)(2,1)} %param.2) | copy-start | bytes 25165828
  6.6 67.0 %collective-permute-start.17 = (bf16[512,2048]{1,0:T(8,128)(2,1)S(1)}, bf16[512,2048]{1,0:T(8,128)(2,1)S(1)}, u32[]{:S(2)}, u32[]{:S(2)}) collective-permute-start(bf16[512,2048]{1,0:T(8,128)(2,1)S(1)} %stage.7.acts), channel_id=1, source_target_pairs={{0,1},{1,0},{2,3},{3,2},{4,5},{5,4},{6,7},{7,6},{8,9},{9,8},{10,11... | collective-permute-start | bytes 6291464 | tf_op jit(solution)/shard_map/ppermute | solution.py:17
  8.0 25.1 %collective-permute-start.10 = (bf16[1024,256]{1,0:T(8,128)(2,1)S(1)}, bf16[1024,256]{1,0:T(8,128)(2,1)S(1)}, u32[]{:S(2)}, u32[]{:S(2)}) collective-permute-start(bf16[1024,256]{1,0:T(8,128)(2,1)S(1)} %get-tuple-element.19), channel_id=1, source_target_pairs={{0,1},{1,0},{2,3},{3,2},{4,5},{5,4},{6,7},{7,6},{8,9},{9,8},{10,11... | collective-permute-start | bytes 1572872 | tf_op jit(solution)/shard_map/ppermute | solution.py:17
  10.3 66.0 %collective-permute-start.13 = (bf16[512,2048]{1,0:T(8,128)(2,1)S(1)}, bf16[512,2048]{1,0:T(8,128)(2,1)S(1)}, u32[]{:S(2)}, u32[]{:S(2)}) collective-permute-start(bf16[512,2048]{1,0:T(8,128)(2,1)S(1)} %stage.6.acts), channel_id=1, source_target_pairs={{0,1},{1,0},{2,3},{3,2},{4,5},{5,4},{6,7},{7,6},{8,9},{9,8},{10,11... | collective-permute-start | bytes 6291464 | tf_op jit(solution)/shard_map/ppermute | solution.py:17
  10.4 14.0 %collective-permute-start.2 = (bf16[512,256]{1,0:T(8,128)(2,1)S(1)}, bf16[512,256]{1,0:T(8,128)(2,1)S(1)}, u32[]{:S(2)}, u32[]{:S(2)}) collective-permute-start(bf16[512,256]{1,0:T(8,128)(2,1)S(1)} %join.1), channel_id=1, source_target_pairs={{0,4},{1,5},{2,6},{3,7},{4,0},{5,1},{6,2},{7,3},{8,12},{9,13},{10,... | collective-permute-start | bytes 786440 | tf_op jit(solution)/shard_map/ppermute | solution.py:17
  13.3 64.2 %collective-permute-start = (bf16[512,2048]{1,0:T(8,128)(2,1)S(1)}, bf16[512,2048]{1,0:T(8,128)(2,1)S(1)}, u32[]{:S(2)}, u32[]{:S(2)}) collective-permute-start(bf16[512,2048]{1,0:T(8,128)(2,1)S(1)} %stage.4.acts), channel_id=1, source_target_pairs={{0,1},{1,0},{2,3},{3,2},{4,5},{5,4},{6,7},{7,6},{8,9},{9,8},{10,11... | collective-permute-start | bytes 6291464 | tf_op jit(solution)/shard_map/ppermute | solution.py:17
  24.4 6.5 %collective-permute-start.7 = (bf16[512,256]{1,0:T(8,128)(2,1)S(1)}, bf16[512,256]{1,0:T(8,128)(2,1)S(1)}, u32[]{:S(2)}, u32[]{:S(2)}) collective-permute-start(bf16[512,256]{1,0:T(8,128)(2,1)S(1)} %join.1), channel_id=1, source_target_pairs={{0,2},{1,3},{2,0},{3,1},{4,6},{5,7},{6,4},{7,5},{8,10},{9,11},{10,... | collective-permute-start | bytes 786440 | tf_op jit(solution)/shard_map/ppermute | solution.py:17
  30.9 51.1 %collective-permute-start.6 = (bf16[512,2048]{1,0:T(8,128)(2,1)S(1)}, bf16[512,2048]{1,0:T(8,128)(2,1)S(1)}, u32[]{:S(2)}, u32[]{:S(2)}) collective-permute-start(bf16[512,2048]{1,0:T(8,128)(2,1)S(1)} %stage.5.acts), channel_id=1, source_target_pairs={{0,1},{1,0},{2,3},{3,2},{4,5},{5,4},{6,7},{7,6},{8,9},{9,8},{10,11... | collective-permute-start | bytes 6291464 | tf_op jit(solution)/shard_map/ppermute | solution.py:17
  33.1 7.9 %collective-permute-start.14 = (bf16[512,256]{1,0:T(8,128)(2,1)S(1)}, bf16[512,256]{1,0:T(8,128)(2,1)S(1)}, u32[]{:S(2)}, u32[]{:S(2)}) collective-permute-start(bf16[512,256]{1,0:T(8,128)(2,1)S(1)} %collective-permute-done.2.refs_0_), channel_id=1, source_target_pairs={{0,8},{8,0},{16,24},{24,16},{1,9},{9,1},{17,25},{25,17},{2,10},{10... | collective-permute-start | bytes 786440 | tf_op jit(solution)/shard_map/ppermute | solution.py:17
  41.0 7.0 %collective-permute-start.15 = (bf16[512,256]{1,0:T(8,128)(2,1)S(1)}, bf16[512,256]{1,0:T(8,128)(2,1)S(1)}, u32[]{:S(2)}, u32[]{:S(2)}) collective-permute-start(bf16[512,256]{1,0:T(8,128)(2,1)S(1)} %collective-permute-done.2.refs_0_), channel_id=1, source_target_pairs={{0,16},{8,24},{16,0},{24,8},{1,17},{9,25},{17,1},{25,9},{2,18},{10... | collective-permute-start | bytes 786440 | tf_op jit(solution)/shard_map/ppermute | solution.py:17
  48.0 7.0 %collective-permute-start.16 = (bf16[512,256]{1,0:T(8,128)(2,1)S(1)}, bf16[512,256]{1,0:T(8,128)(2,1)S(1)}, u32[]{:S(2)}, u32[]{:S(2)}) collective-permute-start(bf16[512,256]{1,0:T(8,128)(2,1)S(1)} %collective-permute-done.2.refs_0_), channel_id=1, source_target_pairs={{0,24},{8,16},{16,8},{24,0},{1,25},{9,17},{17,9},{25,1},{2,26},{10... | collective-permute-start | bytes 786440 | tf_op jit(solution)/shard_map/ppermute | solution.py:17
  55.0 5.2 %collective-permute-start.3 = (bf16[512,256]{1,0:T(8,128)(2,1)S(1)}, bf16[512,256]{1,0:T(8,128)(2,1)S(1)}, u32[]{:S(2)}, u32[]{:S(2)}) collective-permute-start(bf16[512,256]{1,0:T(8,128)(2,1)S(1)} %collective-permute-done.2.refs_0_), channel_id=1, source_target_pairs={{0,2},{1,3},{2,0},{3,1},{4,6},{5,7},{6,4},{7,5},{8,10},{9,11},{10,... | collective-permute-start | bytes 786440 | tf_op jit(solution)/shard_map/ppermute | solution.py:17
  60.2 5.2 %collective-permute-start.8 = (bf16[512,256]{1,0:T(8,128)(2,1)S(1)}, bf16[512,256]{1,0:T(8,128)(2,1)S(1)}, u32[]{:S(2)}, u32[]{:S(2)}) collective-permute-start(bf16[512,256]{1,0:T(8,128)(2,1)S(1)} %collective-permute-done.7.refs_0_), channel_id=1, source_target_pairs={{0,8},{8,0},{16,24},{24,16},{1,9},{9,1},{17,25},{25,17},{2,10},{10... | collective-permute-start | bytes 786440 | tf_op jit(solution)/shard_map/ppermute | solution.py:17
  65.5 7.9 %collective-permute-start.12 = (bf16[512,256]{1,0:T(8,128)(2,1)S(1)}, bf16[512,256]{1,0:T(8,128)(2,1)S(1)}, u32[]{:S(2)}, u32[]{:S(2)}) collective-permute-start(bf16[512,256]{1,0:T(8,128)(2,1)S(1)} %pick.1), channel_id=1, source_target_pairs={{0,6},{1,7},{2,4},{3,5},{4,2},{5,3},{6,0},{7,1},{8,14},{9,15},{10,... | collective-permute-start | bytes 786440 | tf_op jit(solution)/shard_map/ppermute | solution.py:17
  73.4 8.6 %collective-permute-start.9 = (bf16[512,256]{1,0:T(8,128)(2,1)S(1)}, bf16[512,256]{1,0:T(8,128)(2,1)S(1)}, u32[]{:S(2)}, u32[]{:S(2)}) collective-permute-start(bf16[512,256]{1,0:T(8,128)(2,1)S(1)} %collective-permute-done.7.refs_0_), channel_id=1, source_target_pairs={{0,16},{8,24},{16,0},{24,8},{1,17},{9,25},{17,1},{25,9},{2,18},{10... | collective-permute-start | bytes 786440 | tf_op jit(solution)/shard_map/ppermute | solution.py:17
  73.6 8.4 %collective-permute-start.11 = (bf16[512,256]{1,0:T(8,128)(2,1)S(1)}, bf16[512,256]{1,0:T(8,128)(2,1)S(1)}, u32[]{:S(2)}, u32[]{:S(2)}) collective-permute-start(bf16[512,256]{1,0:T(8,128)(2,1)S(1)} %pick.1), channel_id=1, source_target_pairs={{0,2},{1,3},{2,0},{3,1},{4,6},{5,7},{6,4},{7,5},{8,10},{9,11},{10,... | collective-permute-start | bytes 786440 | tf_op jit(solution)/shard_map/ppermute | solution.py:17
  76.3 7.0 %collective-permute-start.4 = (bf16[512,256]{1,0:T(8,128)(2,1)S(1)}, bf16[512,256]{1,0:T(8,128)(2,1)S(1)}, u32[]{:S(2)}, u32[]{:S(2)}) collective-permute-start(bf16[512,256]{1,0:T(8,128)(2,1)S(1)} %collective-permute-done.3.refs_0_), channel_id=1, source_target_pairs={{0,8},{8,0},{16,24},{24,16},{1,9},{9,1},{17,25},{25,17},{2,10},{10... | collective-permute-start | bytes 786440 | tf_op jit(solution)/shard_map/ppermute | solution.py:17
  77.5 5.9 %collective-permute-start.5 = (bf16[512,256]{1,0:T(8,128)(2,1)S(1)}, bf16[512,256]{1,0:T(8,128)(2,1)S(1)}, u32[]{:S(2)}, u32[]{:S(2)}) collective-permute-start(bf16[512,256]{1,0:T(8,128)(2,1)S(1)} %collective-permute-done.3.refs_0_), channel_id=1, source_target_pairs={{0,16},{8,24},{16,0},{24,8},{1,17},{9,25},{17,1},{25,9},{2,18},{10... | collective-permute-start | bytes 786440 | tf_op jit(solution)/shard_map/ppermute | solution.py:17
  84.3 9.1 %collective-permute-start.18 = (bf16[2,2,512,256]{3,2,1,0:T(8,128)(2,1)S(1)}, bf16[2,2,512,256]{3,2,1,0:T(8,128)(2,1)S(1)}, u32[]{:S(2)}, u32[]{:S(2)}) collective-permute-start(bf16[2,2,512,256]{3,2,1,0:T(8,128)(2,1)S(1)} %get-tuple-element.20.own), channel_id=1, source_target_pairs={{0,1},{1,0},{2,3},{3,2},{4,5},{5,4},{6,7},{7,6},{8,9},{9,8},{10,11... | collective-permute-start | bytes 3145736 | tf_op jit(solution)/shard_map/ppermute | solution.py:17
  91.2 2.3 %collective-permute-start.19 = (f32[8,256]{1,0:T(8,128)S(1)}, f32[8,256]{1,0:T(8,128)S(1)}, u32[]{:S(2)}, u32[]{:S(2)}) collective-permute-start(f32[8,256]{1,0:T(8,128)S(1)} %get-tuple-element.21.own_sums), channel_id=1, source_target_pairs={{0,1},{1,0},{2,3},{3,2},{4,5},{5,4},{6,7},{7,6},{8,9},{9,8},{10,11... | collective-permute-start | bytes 24584 | tf_op jit(solution)/shard_map/ppermute | solution.py:17
  94.5 6.8 %collective-permute-start.20 = (f16[136,512]{1,0:T(8,128)(2,1)S(1)}, f16[136,512]{1,0:T(8,128)(2,1)S(1)}, u32[]{:S(2)}, u32[]{:S(2)}) collective-permute-start(f16[136,512]{1,0:T(8,128)(2,1)S(1)} %convert_element_type.18), channel_id=1, source_target_pairs={{0,6},{1,7},{2,4},{3,5},{4,2},{5,3},{6,0},{7,1},{8,14},{9,15},{10,... | collective-permute-start | bytes 417800 | tf_op jit(solution)/shard_map/ppermute | solution.py:17
  97.7 12.1 %collective-permute-start.21 = (f16[136,512]{1,0:T(8,128)(2,1)S(1)}, f16[136,512]{1,0:T(8,128)(2,1)S(1)}, u32[]{:S(2)}, u32[]{:S(2)}) collective-permute-start(f16[136,512]{1,0:T(8,128)(2,1)S(1)} %convert_element_type.20), channel_id=1, source_target_pairs={{0,4},{1,5},{2,6},{3,7},{4,0},{5,1},{6,2},{7,3},{8,12},{9,13},{10,... | collective-permute-start | bytes 417800 | tf_op jit(solution)/shard_map/ppermute | solution.py:17
  97.8 12.0 %collective-permute-start.22 = (f16[136,512]{1,0:T(8,128)(2,1)S(1)}, f16[136,512]{1,0:T(8,128)(2,1)S(1)}, u32[]{:S(2)}, u32[]{:S(2)}) collective-permute-start(f16[136,512]{1,0:T(8,128)(2,1)S(1)} %convert_element_type.22), channel_id=1, source_target_pairs={{0,2},{1,3},{2,0},{3,1},{4,6},{5,7},{6,4},{7,5},{8,10},{9,11},{10,... | collective-permute-start | bytes 417800 | tf_op jit(solution)/shard_map/ppermute | solution.py:17
  110.4 4.7 %collective-permute-start.23 = (bf16[64,512]{1,0:T(8,128)(2,1)S(1)}, bf16[64,512]{1,0:T(8,128)(2,1)S(1)}, u32[]{:S(2)}, u32[]{:S(2)}) collective-permute-start(bf16[64,512]{1,0:T(8,128)(2,1)S(1)} %get-tuple-element.28), channel_id=1, source_target_pairs={{0,8},{8,0},{16,24},{24,16},{1,9},{9,1},{17,25},{25,17},{2,10},{10... | collective-permute-start | bytes 196616 | tf_op jit(solution)/shard_map/ppermute | solution.py:17
  110.5 6.4 %collective-permute-start.24 = (bf16[64,512]{1,0:T(8,128)(2,1)S(1)}, bf16[64,512]{1,0:T(8,128)(2,1)S(1)}, u32[]{:S(2)}, u32[]{:S(2)}) collective-permute-start(bf16[64,512]{1,0:T(8,128)(2,1)S(1)} %get-tuple-element.29), channel_id=1, source_target_pairs={{8,16},{16,8},{9,17},{17,9},{10,18},{18,10},{11,19},{19,11},{12,20... | collective-permute-start | bytes 196616 | tf_op jit(solution)/shard_map/ppermute | solution.py:455
  117.1 3.1 %collective-permute-start.25 = (f32[8,128]{1,0:T(8,128)S(1)}, f32[8,128]{1,0:T(8,128)S(1)}, u32[]{:S(2)}, u32[]{:S(2)}) collective-permute-start(f32[8,128]{1,0:T(8,128)S(1)} %products.1), channel_id=1, source_target_pairs={{0,1},{1,0},{2,3},{3,2},{4,5},{5,4},{6,7},{7,6},{8,9},{9,8},{10,11... | collective-permute-start | bytes 12296 | tf_op jit(solution)/shard_map/ppermute | solution.py:17
  120.2 4.4 %collective-permute-start.26 = (f32[8,128]{1,0:T(8,128)S(1)}, f32[8,128]{1,0:T(8,128)S(1)}, u32[]{:S(2)}, u32[]{:S(2)}) collective-permute-start(f32[8,128]{1,0:T(8,128)S(1)} %add.7.refs_0_), channel_id=1, source_target_pairs={{0,6},{1,7},{2,4},{3,5},{4,2},{5,3},{6,0},{7,1},{8,14},{9,15},{10,... | collective-permute-start | bytes 12296 | tf_op jit(solution)/shard_map/ppermute | solution.py:17
  122.5 3.4 %collective-permute-start.27 = (f32[8,128]{1,0:T(8,128)S(1)}, f32[8,128]{1,0:T(8,128)S(1)}, u32[]{:S(2)}, u32[]{:S(2)}) collective-permute-start(f32[8,128]{1,0:T(8,128)S(1)} %add.7.refs_0_), channel_id=1, source_target_pairs={{0,4},{1,5},{2,6},{3,7},{4,0},{5,1},{6,2},{7,3},{8,12},{9,13},{10,... | collective-permute-start | bytes 12296 | tf_op jit(solution)/shard_map/ppermute | solution.py:17
  122.5 3.4 %collective-permute-start.28 = (f32[8,128]{1,0:T(8,128)S(1)}, f32[8,128]{1,0:T(8,128)S(1)}, u32[]{:S(2)}, u32[]{:S(2)}) collective-permute-start(f32[8,128]{1,0:T(8,128)S(1)} %add.7.refs_0_), channel_id=1, source_target_pairs={{0,2},{1,3},{2,0},{3,1},{4,6},{5,7},{6,4},{7,5},{8,10},{9,11},{10,... | collective-permute-start | bytes 12296 | tf_op jit(solution)/shard_map/ppermute | solution.py:17

commit v5 on v4

--- a/solution.py
+++ b/solution.py
@@ -118,28 +118,34 @@
     )(upper, lower)
 
 
-def project_kernel(keys, parts, started, last, layers, acts, other, *refs):
-    pieces, refs = refs[: len(keys)], refs[len(keys) :]
+def project_kernel(groups, parts, started, last, layers, *refs):
+    arrays, refs = refs[: 2 * len(groups)], refs[2 * len(groups) :]
+    count = sum(len(keys) for keys in groups)
+    pieces, refs = refs[:count], refs[count:]
     total = refs[0] if started else None
     outs = refs[started:]
     _, core, section = place()
     part = section % parts
-    block = acts.shape[1] // 2
-    offs = []
-    for j, piece in zip(keys, pieces):
-        if j is None:
-            offs += [(core * block, block)] if not offs else [((1 - core) * block, block)]
-        else:
-            deep = block // parts
-            offs += [(side * block + (part ^ j) * deep, deep) for side in (core, 1 - core)]
-    offs = [pl.ds(pl.multiple_of(at, 128), deep) for at, deep in offs]
+    block = arrays[0].shape[1] // 2
+    sides = (core, 1 - core)
+    spots = []
+    for n, keys in enumerate(groups):
+        for j, which in keys:
+            for side in which:
+                if j is None:
+                    spots.append((n, sides[side] * block, block))
+                else:
+                    at = sides[side] * block + (part ^ j) * (block // parts)
+                    spots.append((n, at, block // parts))
+    spots = [(n, pl.ds(pl.multiple_of(at, 128), deep)) for n, at, deep in spots]
     weights = jnp.concatenate([piece[...] for piece in pieces], axis=0)
-    rows = acts.shape[0] // layers
+    rows = arrays[0].shape[0] // layers
     kept = []
-    for side, source in enumerate((acts, other)):
+    for side in range(2):
         for layer in range(layers):
             span = pl.ds(layer * rows, rows)
-            left = jnp.concatenate([source[span, columns] for columns in offs], axis=1)
+            left = [arrays[2 * n + side][span, columns] for n, columns in spots]
+            left = jnp.concatenate(left, axis=1)
             value = jnp.dot(left, weights, preferred_element_type=F32)
             if started:
                 value = value + total[side, span, :]
@@ -164,8 +170,11 @@
             split[1, side, span, :] = (value - high.astype(F32)).astype(BF16)
 
 
-def project(pieces, keys, parts, total, acts, other, layers, last):
-    rows, half = acts.shape[0], pieces[0].shape[1]
+def project(groups, parts, total, layers, last):
+    arrays = [array for acts, _ in groups for array in acts]
+    pieces = [piece for _, held in groups for piece in held.values()]
+    keys = tuple(tuple(held) for _, held in groups)
+    rows, half = arrays[0].shape[0], pieces[0].shape[1]
     deep = sum(piece.shape[0] for piece in pieces)
     if last:
         out_shape = (
@@ -180,12 +189,12 @@
     return pl.pallas_call(
         functools.partial(project_kernel, keys, parts, len(started), last, layers),
         out_shape=out_shape,
-        in_specs=[VMEM] * (2 + len(pieces) + len(started)),
+        in_specs=[VMEM] * (len(arrays) + len(pieces) + len(started)),
         out_specs=out_specs,
-        compiler_params=params(10),
+        compiler_params=params(14 if len(groups) > 1 else 10),
         cost_estimate=cost(4 * rows * deep * half, 4 * rows * deep),
         name="project",
-    )(acts, other, *pieces, *started)
+    )(*arrays, *pieces, *started)
 
 
 def exponent(value):
@@ -420,26 +429,40 @@
         staged[k] = (staged[k], swap(staged[k], "tok", 1))
 
     far = {j: pick(mine, got, parts, j) for j in range(1, parts) if j & (j - 1)}
-    pieces = {0: {}}
+    both, final = (0, 1), order[-1]
+    pieces = {}
     for k in order:
-        pieces[k] = {0: fetched[k]}
+        held = {(0, both): fetched[k]}
         for j in range(1, parts):
-            if j in far and k in (1, order[-1]):
-                pieces[k][j] = swap(far[j], "tok", 2 * k)
+            near = j & -j
+            if j in far and k in (1, final):
+                held[j, both] = swap(far[j], "tok", 2 * k)
+            elif j in far and (j ^ near) not in far:
+                upper = swap(held[j ^ near, both][:deep], "section", near)
+                lower = swap(held[near, both][deep:], "section", j ^ near)
+                held[j, (0,)], held[j, (1,)] = upper, lower
             else:
-                pieces[k][j] = swap(fetched[k], "section", j)
-
-    total = project([mine, got], (None, None), parts, None, *staged[0], layers, False)
-    final, keys = order[-1], tuple(range(parts))
-    late = tuple(j for j in keys[1:] if j not in far)
-    steps = [(k, keys) for k in reversed(order[1:-1])]
-    steps += [(final, tuple(j for j in keys if j not in late))]
-    steps += [(k, keys) for k in order[:-1][:1]] + [(final, late)]
-    steps = [step for step in steps if step[1]]
-    for k, js in steps:
-        last = (k, js) == steps[-1]
-        chosen = [pieces[k][j] for j in js]
-        total = project(chosen, js, parts, total, *staged[k], layers, last)
+                held[j, both] = swap(fetched[k], "section", j)
+        pieces[k] = held
+
+    own_rows = {(None, (0,)): mine, (None, (1,)): got}
+    total = project([(staged[0], own_rows)], parts, None, layers, False)
+
+    def is_late(k, key):
+        return len(key[1]) == 1 or (k == final and key[0] != 0 and key[0] not in far)
+
+    late, early = [], {}
+    for k in order:
+        early[k] = {key: piece for key, piece in pieces[k].items() if not is_late(k, key)}
+        held = {key: piece for key, piece in pieces[k].items() if is_late(k, key)}
+        if held:
+            late.append((staged[k], held))
+    steps = [(k, [(staged[k], early[k])]) for k in order[-2::-1] + order[-1:]]
+    if late:
+        steps.append((None, late))
+    for n, (k, groups_of) in enumerate(steps):
+        last = n == len(steps) - 1
+        total = project(groups_of, parts, total, layers, last)
     split, sums = total
 
     split_oth = swap(split, "tok", 1)

time: 129 us -> 134 us (1.039); the launches traced: 126 us -> 133 us
  waiting for transfers between devices: 62.9 us -> 70.8 us
    ppermute x28 -> x29, waiting for transfers between devices: 61.1 us -> 67.9 us  [swap(): lax.ppermute(block, axis, [(i, i ^ mask) for i in range(lax.axis_size(axi...]
    ppermute x1, starting transfers between devices: 4.5 us -> 3.06 us  [local(): second = lax.ppermute(second, 'section', route + [(b, a) for a, b in route])]
    ppermute x28 -> x29, starting transfers between devices: 38.9 us -> 39.1 us  [swap(): lax.ppermute(block, axis, [(i, i ^ mask) for i in range(lax.axis_size(axi...]
  transfers between devices with their start and end apart: 29 -> 30, of which waited for: 15 -> 17; matrix products, arithmetic and copies ran while one was open for 1% -> 1% of each run, Pallas kernels for 6% -> 6%
where the time goes in v5:
time: 134 us; the launch traced here: 133 us
  waiting for transfers between devices  70.8 us (53%)
  starting transfers between devices  42.2 us (31%)
  Pallas kernels  11.3 us (8%)
  local copies, waits for them, and re-layouts  7.57 us (6%)
    ppermute x29, waiting for transfers between devices, swap(): lax.ppermute(block, axis, [(i, i ^ mask) for i in range(lax.axis_size(axi...  67.9 us
    ppermute x29, starting transfers between devices, swap(): lax.ppermute(block, axis, [(i, i ^ mask) for i in range(lax.axis_size(axi...  39.1 us
    unnamed x7, local copies, waits for them, and re-layouts  6.58 us
    pallas_call x5, Pallas kernels, project(): pl.pallas_call(functools.partial(project_kernel, keys, parts, len(started...  5.41 us
    ppermute x1, starting transfers between devices, local(): second = lax.ppermute(second, 'section', route + [(b, a) for a, b in route])  3.06 us
    ppermute x1, waiting for transfers between devices, local(): second = lax.ppermute(second, 'section', route + [(b, a) for a, b in route])  2.82 us
  transfers between devices with their start and end apart: 30, of which 17 were waited for; matrix products, arithmetic and copies ran while one was open for 1% of the time, Pallas kernels for 6%

profile of v5, /device:TPU:5, one launch (start us, length us, event | category | flops | bytes accessed | tf_op | source)
XLA Modules:
  0.0 132.9 jit_solution(12924321732288612902)
XLA Ops:
  0.6 1.0 constant_dynamic-slice_fusion.proj
  1.9 0.7 collective-permute-start.2
  2.7 3.4 %copy-done.1 = bf16[2,256,8192]{2,1,0:T(8,128)(2,1)S(1)} copy-done((bf16[2,256,8192]{2,1,0:T(8,128)(2,1)S(1)}, bf16[2,256,8192]{2,1,0:T(8,128)(2,1)}, u32[]{:S(2)}) %copy-start.1) | copy-done | bytes 8388632
  6.7 0.6 copy-done
  7.3 0.7 deal.3
  8.1 1.7 %copy-done.2 = bf16[2,256,8192]{2,1,0:T(8,128)(2,1)S(1)} copy-done((bf16[2,256,8192]{2,1,0:T(8,128)(2,1)S(1)}, bf16[2,256,8192]{2,1,0:T(8,128)(2,1)}, u32[]{:S(2)}) %copy-start.2) | copy-done | bytes 8388632
  10.4 2.4 %collective-permute-start.3 = (bf16[512,256]{1,0:T(8,128)(2,1)S(1)}, bf16[512,256]{1,0:T(8,128)(2,1)S(1)}, u32[]{:S(2)}, u32[]{:S(2)}) collective-permute-start(bf16[512,256]{1,0:T(8,128)(2,1)S(1)} %join.1), channel_id=1, source_target_pairs={{0,4},{1,5},{2,6},{3,7},{4,0},{5,1},{6,2},{7,3},{8,12},{9,13},{10,... | collective-permute-start | bytes 786440 | tf_op jit(solution)/shard_map/ppermute | solution.py:17
  13.3 0.8 collective-permute-start.13
  14.1 10.2 %collective-permute-done.3.refs_2_ = bf16[512,256]{1,0:T(8,128)(2,1)S(1)} collective-permute-done((bf16[512,256]{1,0:T(8,128)(2,1)S(1)}, bf16[512,256]{1,0:T(8,128)(2,1)S(1)}, u32[]{:S(2)}, u32[]{:S(2)}) %collective-permute-start.3) | collective-permute-done | bytes 262176 | tf_op jit(solution)/shard_map/ppermute | solution.py:17
  24.4 1.2 collective-permute-start.14
  25.9 5.0 %collective-permute-done.14.refs_2_ = bf16[512,256]{1,0:T(8,128)(2,1)S(1)} collective-permute-done((bf16[512,256]{1,0:T(8,128)(2,1)S(1)}, bf16[512,256]{1,0:T(8,128)(2,1)S(1)}, u32[]{:S(2)}, u32[]{:S(2)}) %collective-permute-start.14) | collective-permute-done | bytes 262176 | tf_op jit(solution)/shard_map/ppermute | solution.py:17
  30.9 2.2 %collective-permute-start.1 = (bf16[512,2048]{1,0:T(8,128)(2,1)S(1)}, bf16[512,2048]{1,0:T(8,128)(2,1)S(1)}, u32[]{:S(2)}, u32[]{:S(2)}) collective-permute-start(bf16[512,2048]{1,0:T(8,128)(2,1)S(1)} %stage.5.refs_0_.refs_2_), channel_id=1, source_target_pairs={{0,1},{1,0},{2,3},{3,2},{4,5},{5,4},{6,7},{7,6},{8,9},{9,8},{10,11... | collective-permute-start | bytes 6291464 | tf_op jit(solution)/shard_map/ppermute | solution.py:17
  33.5 7.4 %collective-permute-done.4.refs_4_ = bf16[512,256]{1,0:T(8,128)(2,1)S(1)} collective-permute-done((bf16[512,256]{1,0:T(8,128)(2,1)S(1)}, bf16[512,256]{1,0:T(8,128)(2,1)S(1)}, u32[]{:S(2)}, u32[]{:S(2)}) %collective-permute-start.4) | collective-permute-done | bytes 262176 | tf_op jit(solution)/shard_map/ppermute | solution.py:17
  41.0 1.2 collective-permute-start.6
  42.2 5.8 %collective-permute-done.6.refs_3_ = bf16[512,256]{1,0:T(8,128)(2,1)S(1)} collective-permute-done((bf16[512,256]{1,0:T(8,128)(2,1)S(1)}, bf16[512,256]{1,0:T(8,128)(2,1)S(1)}, u32[]{:S(2)}, u32[]{:S(2)}) %collective-permute-start.6) | collective-permute-done | bytes 262176 | tf_op jit(solution)/shard_map/ppermute | solution.py:17
  48.0 1.2 collective-permute-start.15
  49.2 4.9 %collective-permute-done.15.refs_3_ = bf16[512,256]{1,0:T(8,128)(2,1)S(1)} collective-permute-done((bf16[512,256]{1,0:T(8,128)(2,1)S(1)}, bf16[512,256]{1,0:T(8,128)(2,1)S(1)}, u32[]{:S(2)}, u32[]{:S(2)}) %collective-permute-start.15) | collective-permute-done | bytes 262176 | tf_op jit(solution)/shard_map/ppermute | solution.py:17
  54.6 4.8 %collective-permute-done.16.refs_4_ = bf16[512,256]{1,0:T(8,128)(2,1)S(1)} collective-permute-done((bf16[512,256]{1,0:T(8,128)(2,1)S(1)}, bf16[512,256]{1,0:T(8,128)(2,1)S(1)}, u32[]{:S(2)}, u32[]{:S(2)}) %collective-permute-start.16) | collective-permute-done | bytes 262176 | tf_op jit(solution)/shard_map/ppermute | solution.py:17
  59.3 1.2 collective-permute-start.8
  60.6 4.0 %collective-permute-done.8.refs_2_ = bf16[512,256]{1,0:T(8,128)(2,1)S(1)} collective-permute-done((bf16[512,256]{1,0:T(8,128)(2,1)S(1)}, bf16[512,256]{1,0:T(8,128)(2,1)S(1)}, u32[]{:S(2)}, u32[]{:S(2)}) %collective-permute-start.8) | collective-permute-done | bytes 262176 | tf_op jit(solution)/shard_map/ppermute | solution.py:17
  64.6 1.2 collective-permute-start.17
  65.8 5.7 %collective-permute-done.17.refs_5_ = bf16[512,256]{1,0:T(8,128)(2,1)S(1)} collective-permute-done((bf16[512,256]{1,0:T(8,128)(2,1)S(1)}, bf16[512,256]{1,0:T(8,128)(2,1)S(1)}, u32[]{:S(2)}, u32[]{:S(2)}) %collective-permute-start.17) | collective-permute-done | bytes 262176 | tf_op jit(solution)/shard_map/ppermute | solution.py:17
  71.5 4.1 %collective-permute-start.12 = (bf16[512,256]{1,0:T(8,128)(2,1)S(1)}, bf16[512,256]{1,0:T(8,128)(2,1)S(1)}, u32[]{:S(2)}, u32[]{:S(2)}) collective-permute-start(bf16[512,256]{1,0:T(8,128)(2,1)S(1)} %pick.1), channel_id=1, source_target_pairs={{0,6},{1,7},{2,4},{3,5},{4,2},{5,3},{6,0},{7,1},{8,14},{9,15},{10,... | collective-permute-start | bytes 786440 | tf_op jit(solution)/shard_map/ppermute | solution.py:17
  75.9 1.2 collective-permute-start.9
  77.2 1.2 project.5.refs_5_
  78.4 1.0 project.6.refs_6_
  79.4 2.7 %collective-permute-done.12.refs_3_ = bf16[512,256]{1,0:T(8,128)(2,1)S(1)} collective-permute-done((bf16[512,256]{1,0:T(8,128)(2,1)S(1)}, bf16[512,256]{1,0:T(8,128)(2,1)S(1)}, u32[]{:S(2)}, u32[]{:S(2)}) %collective-permute-start.12) | collective-permute-done | bytes 262176 | tf_op jit(solution)/shard_map/ppermute | solution.py:17
  82.1 1.2 collective-permute-start.5
  83.5 1.3 project.7.refs_4_
  84.8 0.7 project.8.refs_8_
  85.5 0.7 collective-permute-done.5.refs_4_
  86.2 1.2 collective-permute-done.7.refs_5_
  87.4 1.2 project.9
  88.6 8.3 %collective-permute-start.19 = (bf16[2,2,512,256]{3,2,1,0:T(8,128)(2,1)S(1)}, bf16[2,2,512,256]{3,2,1,0:T(8,128)(2,1)S(1)}, u32[]{:S(2)}, u32[]{:S(2)}) collective-permute-start(bf16[2,2,512,256]{3,2,1,0:T(8,128)(2,1)S(1)} %get-tuple-element.20.own), channel_id=1, source_target_pairs={{0,1},{1,0},{2,3},{3,2},{4,5},{5,4},{6,7},{7,6},{8,9},{9,8},{10,11... | collective-permute-start | bytes 3145736 | tf_op jit(solution)/shard_map/ppermute | solution.py:17
  97.6 1.6 %collective-permute-done.20.oth_sums = f32[8,256]{1,0:T(8,128)S(1)} collective-permute-done((f32[8,256]{1,0:T(8,128)S(1)}, f32[8,256]{1,0:T(8,128)S(1)}, u32[]{:S(2)}, u32[]{:S(2)}) %collective-permute-start.20) | collective-permute-done | bytes 8224 | tf_op jit(solution)/shard_map/ppermute | solution.py:17
  99.2 1.0 gram.1
  100.3 3.6 %collective-permute-start.21 = (f16[136,512]{1,0:T(8,128)(2,1)S(1)}, f16[136,512]{1,0:T(8,128)(2,1)S(1)}, u32[]{:S(2)}, u32[]{:S(2)}) collective-permute-start(f16[136,512]{1,0:T(8,128)(2,1)S(1)} %convert_element_type.18), channel_id=1, source_target_pairs={{0,6},{1,7},{2,4},{3,5},{4,2},{5,3},{6,0},{7,1},{8,14},{9,15},{10,... | collective-permute-start | bytes 417800 | tf_op jit(solution)/shard_map/ppermute | solution.py:17
  104.4 3.2 %collective-permute-done.21 = f16[136,512]{1,0:T(8,128)(2,1)S(1)} collective-permute-done((f16[136,512]{1,0:T(8,128)(2,1)S(1)}, f16[136,512]{1,0:T(8,128)(2,1)S(1)}, u32[]{:S(2)}, u32[]{:S(2)}) %collective-permute-start.21) | collective-permute-done | bytes 139296 | tf_op jit(solution)/shard_map/ppermute | solution.py:17
  107.6 8.6 %collective-permute-done.22 = f16[136,512]{1,0:T(8,128)(2,1)S(1)} collective-permute-done((f16[136,512]{1,0:T(8,128)(2,1)S(1)}, f16[136,512]{1,0:T(8,128)(2,1)S(1)}, u32[]{:S(2)}, u32[]{:S(2)}) %collective-permute-start.22) | collective-permute-done | bytes 139296 | tf_op jit(solution)/shard_map/ppermute | solution.py:17
  117.1 3.1 %collective-permute-start.25 = (bf16[64,512]{1,0:T(8,128)(2,1)S(1)}, bf16[64,512]{1,0:T(8,128)(2,1)S(1)}, u32[]{:S(2)}, u32[]{:S(2)}) collective-permute-start(bf16[64,512]{1,0:T(8,128)(2,1)S(1)} %get-tuple-element.29), channel_id=1, source_target_pairs={{8,16},{16,8},{9,17},{17,9},{10,18},{18,10},{11,19},{19,11},{12,20... | collective-permute-start | bytes 196616 | tf_op jit(solution)/shard_map/ppermute | solution.py:478
  120.2 2.8 %collective-permute-done.25.two = bf16[64,512]{1,0:T(8,128)(2,1)S(1)} collective-permute-done((bf16[64,512]{1,0:T(8,128)(2,1)S(1)}, bf16[64,512]{1,0:T(8,128)(2,1)S(1)}, u32[]{:S(2)}, u32[]{:S(2)}) %collective-permute-start.25) | collective-permute-done | bytes 65568 | tf_op jit(solution)/shard_map/ppermute | solution.py:478
  123.3 2.4 %collective-permute-start.26 = (f32[8,128]{1,0:T(8,128)S(1)}, f32[8,128]{1,0:T(8,128)S(1)}, u32[]{:S(2)}, u32[]{:S(2)}) collective-permute-start(f32[8,128]{1,0:T(8,128)S(1)} %products.1), channel_id=1, source_target_pairs={{0,1},{1,0},{2,3},{3,2},{4,5},{5,4},{6,7},{7,6},{8,9},{9,8},{10,11... | collective-permute-start | bytes 12296 | tf_op jit(solution)/shard_map/ppermute | solution.py:17
  125.7 0.8 collective-permute-done.26
  126.5 2.4 %collective-permute-start.27 = (f32[8,128]{1,0:T(8,128)S(1)}, f32[8,128]{1,0:T(8,128)S(1)}, u32[]{:S(2)}, u32[]{:S(2)}) collective-permute-start(f32[8,128]{1,0:T(8,128)S(1)} %add.7.refs_0_), channel_id=1, source_target_pairs={{0,6},{1,7},{2,4},{3,5},{4,2},{5,3},{6,0},{7,1},{8,14},{9,15},{10,... | collective-permute-start | bytes 12296 | tf_op jit(solution)/shard_map/ppermute | solution.py:17
  128.8 1.2 collective-permute-start.29
  130.0 0.9 copy.4
  130.9 1.3 collective-permute-done.28.refs_2_
  132.2 0.7 ratios.1
  (47 shorter events, 6.2 us)
Async XLA Ops:
  1.9 8.4 %collective-permute-start.2 = (bf16[256,256]{1,0:T(8,128)(2,1)S(1)}, bf16[256,256]{1,0:T(8,128)(2,1)S(1)}, u32[]{:S(2)}, u32[]{:S(2)}) collective-permute-start(bf16[256,256]{1,0:T(8,128)(2,1)S(1)} %get-tuple-element.17), channel_id=1, source_target_pairs={{0,1},{1,0},{2,3},{3,2},{4,5},{5,4},{6,7},{7,6},{8,9},{9,8},{10,11... | collective-permute-start | bytes 393224 | tf_op jit(solution)/shard_map/ppermute | solution.py:17
  2.7 3.4 %copy-start.1 = (bf16[2,256,8192]{2,1,0:T(8,128)(2,1)S(1)}, bf16[2,256,8192]{2,1,0:T(8,128)(2,1)}, u32[]{:S(2)}) copy-start(bf16[2,256,8192]{2,1,0:T(8,128)(2,1)} %param.2) | copy-start | bytes 25165828
  6.1 1.2 copy-start
  6.1 3.7 %copy-start.2 = (bf16[2,256,8192]{2,1,0:T(8,128)(2,1)S(1)}, bf16[2,256,8192]{2,1,0:T(8,128)(2,1)}, u32[]{:S(2)}) copy-start(bf16[2,256,8192]{2,1,0:T(8,128)(2,1)} %param.2) | copy-start | bytes 25165828
  6.6 69.1 %collective-permute-start.18 = (bf16[512,2048]{1,0:T(8,128)(2,1)S(1)}, bf16[512,2048]{1,0:T(8,128)(2,1)S(1)}, u32[]{:S(2)}, u32[]{:S(2)}) collective-permute-start(bf16[512,2048]{1,0:T(8,128)(2,1)S(1)} %stage.7.refs_0_), channel_id=1, source_target_pairs={{0,1},{1,0},{2,3},{3,2},{4,5},{5,4},{6,7},{7,6},{8,9},{9,8},{10,11... | collective-permute-start | bytes 6291464 | tf_op jit(solution)/shard_map/ppermute | solution.py:17
  8.0 25.1 %collective-permute-start.11 = (bf16[1024,256]{1,0:T(8,128)(2,1)S(1)}, bf16[1024,256]{1,0:T(8,128)(2,1)S(1)}, u32[]{:S(2)}, u32[]{:S(2)}) collective-permute-start(bf16[1024,256]{1,0:T(8,128)(2,1)S(1)} %get-tuple-element.19), channel_id=1, source_target_pairs={{0,1},{1,0},{2,3},{3,2},{4,5},{5,4},{6,7},{7,6},{8,9},{9,8},{10,11... | collective-permute-start | bytes 1572872 | tf_op jit(solution)/shard_map/ppermute | solution.py:17
  10.3 65.6 %collective-permute-start = (bf16[512,2048]{1,0:T(8,128)(2,1)S(1)}, bf16[512,2048]{1,0:T(8,128)(2,1)S(1)}, u32[]{:S(2)}, u32[]{:S(2)}) collective-permute-start(bf16[512,2048]{1,0:T(8,128)(2,1)S(1)} %stage.4.refs_0_), channel_id=1, source_target_pairs={{0,1},{1,0},{2,3},{3,2},{4,5},{5,4},{6,7},{7,6},{8,9},{9,8},{10,11... | collective-permute-start | bytes 6291464 | tf_op jit(solution)/shard_map/ppermute | solution.py:17
  10.4 14.0 %collective-permute-start.3 = (bf16[512,256]{1,0:T(8,128)(2,1)S(1)}, bf16[512,256]{1,0:T(8,128)(2,1)S(1)}, u32[]{:S(2)}, u32[]{:S(2)}) collective-permute-start(bf16[512,256]{1,0:T(8,128)(2,1)S(1)} %join.1), channel_id=1, source_target_pairs={{0,4},{1,5},{2,6},{3,7},{4,0},{5,1},{6,2},{7,3},{8,12},{9,13},{10,... | collective-permute-start | bytes 786440 | tf_op jit(solution)/shard_map/ppermute | solution.py:17
  13.3 70.0 %collective-permute-start.13 = (bf16[512,2048]{1,0:T(8,128)(2,1)S(1)}, bf16[512,2048]{1,0:T(8,128)(2,1)S(1)}, u32[]{:S(2)}, u32[]{:S(2)}) collective-permute-start(bf16[512,2048]{1,0:T(8,128)(2,1)S(1)} %stage.6.refs_0_), channel_id=1, source_target_pairs={{0,1},{1,0},{2,3},{3,2},{4,5},{5,4},{6,7},{7,6},{8,9},{9,8},{10,11... | collective-permute-start | bytes 6291464 | tf_op jit(solution)/shard_map/ppermute | solution.py:17
  24.4 6.5 %collective-permute-start.14 = (bf16[512,256]{1,0:T(8,128)(2,1)S(1)}, bf16[512,256]{1,0:T(8,128)(2,1)S(1)}, u32[]{:S(2)}, u32[]{:S(2)}) collective-permute-start(bf16[512,256]{1,0:T(8,128)(2,1)S(1)} %join.1), channel_id=1, source_target_pairs={{0,2},{1,3},{2,0},{3,1},{4,6},{5,7},{6,4},{7,5},{8,10},{9,11},{10,... | collective-permute-start | bytes 786440 | tf_op jit(solution)/shard_map/ppermute | solution.py:17
  30.9 53.9 %collective-permute-start.1 = (bf16[512,2048]{1,0:T(8,128)(2,1)S(1)}, bf16[512,2048]{1,0:T(8,128)(2,1)S(1)}, u32[]{:S(2)}, u32[]{:S(2)}) collective-permute-start(bf16[512,2048]{1,0:T(8,128)(2,1)S(1)} %stage.5.refs_0_.refs_2_), channel_id=1, source_target_pairs={{0,1},{1,0},{2,3},{3,2},{4,5},{5,4},{6,7},{7,6},{8,9},{9,8},{10,11... | collective-permute-start | bytes 6291464 | tf_op jit(solution)/shard_map/ppermute | solution.py:17
  33.1 7.9 %collective-permute-start.4 = (bf16[512,256]{1,0:T(8,128)(2,1)S(1)}, bf16[512,256]{1,0:T(8,128)(2,1)S(1)}, u32[]{:S(2)}, u32[]{:S(2)}) collective-permute-start(bf16[512,256]{1,0:T(8,128)(2,1)S(1)} %collective-permute-done.3.refs_2_), channel_id=1, source_target_pairs={{0,16},{8,24},{16,0},{24,8},{1,17},{9,25},{17,1},{25,9},{2,18},{10... | collective-permute-start | bytes 786440 | tf_op jit(solution)/shard_map/ppermute | solution.py:17
  41.0 7.0 %collective-permute-start.6 = (bf16[512,256]{1,0:T(8,128)(2,1)S(1)}, bf16[512,256]{1,0:T(8,128)(2,1)S(1)}, u32[]{:S(2)}, u32[]{:S(2)}) collective-permute-start(bf16[512,256]{1,0:T(8,128)(2,1)S(1)} %collective-permute-done.3.refs_2_), channel_id=1, source_target_pairs={{0,8},{8,0},{16,24},{24,16},{1,9},{9,1},{17,25},{25,17},{2,10},{10... | collective-permute-start | bytes 786440 | tf_op jit(solution)/shard_map/ppermute | solution.py:17
  48.0 6.1 %collective-permute-start.15 = (bf16[512,256]{1,0:T(8,128)(2,1)S(1)}, bf16[512,256]{1,0:T(8,128)(2,1)S(1)}, u32[]{:S(2)}, u32[]{:S(2)}) collective-permute-start(bf16[512,256]{1,0:T(8,128)(2,1)S(1)} %collective-permute-done.14.refs_2_), channel_id=1, source_target_pairs={{0,8},{8,0},{16,24},{24,16},{1,9},{9,1},{17,25},{25,17},{2,10},{10... | collective-permute-start | bytes 786440 | tf_op jit(solution)/shard_map/ppermute | solution.py:17
  54.1 5.2 %collective-permute-start.16 = (bf16[512,256]{1,0:T(8,128)(2,1)S(1)}, bf16[512,256]{1,0:T(8,128)(2,1)S(1)}, u32[]{:S(2)}, u32[]{:S(2)}) collective-permute-start(bf16[512,256]{1,0:T(8,128)(2,1)S(1)} %collective-permute-done.14.refs_2_), channel_id=1, source_target_pairs={{0,16},{8,24},{16,0},{24,8},{1,17},{9,25},{17,1},{25,9},{2,18},{10... | collective-permute-start | bytes 786440 | tf_op jit(solution)/shard_map/ppermute | solution.py:17
  59.3 5.2 %collective-permute-start.8 = (bf16[512,256]{1,0:T(8,128)(2,1)S(1)}, bf16[512,256]{1,0:T(8,128)(2,1)S(1)}, u32[]{:S(2)}, u32[]{:S(2)}) collective-permute-start(bf16[512,256]{1,0:T(8,128)(2,1)S(1)} %collective-permute-done.3.refs_2_), channel_id=1, source_target_pairs={{0,2},{1,3},{2,0},{3,1},{4,6},{5,7},{6,4},{7,5},{8,10},{9,11},{10,... | collective-permute-start | bytes 786440 | tf_op jit(solution)/shard_map/ppermute | solution.py:17
  64.6 7.0 %collective-permute-start.17 = (bf16[512,256]{1,0:T(8,128)(2,1)S(1)}, bf16[512,256]{1,0:T(8,128)(2,1)S(1)}, u32[]{:S(2)}, u32[]{:S(2)}) collective-permute-start(bf16[512,256]{1,0:T(8,128)(2,1)S(1)} %pick.1), channel_id=1, source_target_pairs={{0,2},{1,3},{2,0},{3,1},{4,6},{5,7},{6,4},{7,5},{8,10},{9,11},{10,... | collective-permute-start | bytes 786440 | tf_op jit(solution)/shard_map/ppermute | solution.py:17
  71.5 10.5 %collective-permute-start.12 = (bf16[512,256]{1,0:T(8,128)(2,1)S(1)}, bf16[512,256]{1,0:T(8,128)(2,1)S(1)}, u32[]{:S(2)}, u32[]{:S(2)}) collective-permute-start(bf16[512,256]{1,0:T(8,128)(2,1)S(1)} %pick.1), channel_id=1, source_target_pairs={{0,6},{1,7},{2,4},{3,5},{4,2},{5,3},{6,0},{7,1},{8,14},{9,15},{10,... | collective-permute-start | bytes 786440 | tf_op jit(solution)/shard_map/ppermute | solution.py:17
  75.7 11.8 %collective-permute-start.10 = (bf16[512,256]{1,0:T(8,128)(2,1)S(1)}, bf16[512,256]{1,0:T(8,128)(2,1)S(1)}, u32[]{:S(2)}, u32[]{:S(2)}) collective-permute-start(bf16[512,256]{1,0:T(8,128)(2,1)S(1)} %collective-permute-done.8.refs_2_), channel_id=1, source_target_pairs={{0,16},{8,24},{16,0},{24,8},{1,17},{9,25},{17,1},{25,9},{2,18},{10... | collective-permute-start | bytes 786440 | tf_op jit(solution)/shard_map/ppermute | solution.py:17
  75.9 11.5 %collective-permute-start.9 = (bf16[512,256]{1,0:T(8,128)(2,1)S(1)}, bf16[512,256]{1,0:T(8,128)(2,1)S(1)}, u32[]{:S(2)}, u32[]{:S(2)}) collective-permute-start(bf16[512,256]{1,0:T(8,128)(2,1)S(1)} %collective-permute-done.8.refs_2_), channel_id=1, source_target_pairs={{0,8},{8,0},{16,24},{24,16},{1,9},{9,1},{17,25},{25,17},{2,10},{10... | collective-permute-start | bytes 786440 | tf_op jit(solution)/shard_map/ppermute | solution.py:17
  82.1 4.1 %collective-permute-start.5 = (bf16[256,256]{1,0:T(8,128)(2,1)S(1)}, bf16[256,256]{1,0:T(8,128)(2,1)S(1)}, u32[]{:S(2)}, u32[]{:S(2)}) collective-permute-start(bf16[256,256]{1,0:T(8,128)(2,1)S(1)} %slice.8), channel_id=1, source_target_pairs={{0,8},{8,0},{16,24},{24,16},{1,9},{9,1},{17,25},{25,17},{2,10},{10... | collective-permute-start | bytes 393224 | tf_op jit(solution)/shard_map/ppermute | solution.py:17
  83.3 4.1 %collective-permute-start.7 = (bf16[256,256]{1,0:T(8,128)(2,1)S(1)}, bf16[256,256]{1,0:T(8,128)(2,1)S(1)}, u32[]{:S(2)}, u32[]{:S(2)}) collective-permute-start(bf16[256,256]{1,0:T(8,128)(2,1)S(1)} %slice.9), channel_id=1, source_target_pairs={{0,16},{8,24},{16,0},{24,8},{1,17},{9,25},{17,1},{25,9},{2,18},{10... | collective-permute-start | bytes 393224 | tf_op jit(solution)/shard_map/ppermute | solution.py:17
  88.6 10.6 %collective-permute-start.19 = (bf16[2,2,512,256]{3,2,1,0:T(8,128)(2,1)S(1)}, bf16[2,2,512,256]{3,2,1,0:T(8,128)(2,1)S(1)}, u32[]{:S(2)}, u32[]{:S(2)}) collective-permute-start(bf16[2,2,512,256]{3,2,1,0:T(8,128)(2,1)S(1)} %get-tuple-element.20.own), channel_id=1, source_target_pairs={{0,1},{1,0},{2,3},{3,2},{4,5},{5,4},{6,7},{7,6},{8,9},{9,8},{10,11... | collective-permute-start | bytes 3145736 | tf_op jit(solution)/shard_map/ppermute | solution.py:17
  96.9 2.3 %collective-permute-start.20 = (f32[8,256]{1,0:T(8,128)S(1)}, f32[8,256]{1,0:T(8,128)S(1)}, u32[]{:S(2)}, u32[]{:S(2)}) collective-permute-start(f32[8,256]{1,0:T(8,128)S(1)} %get-tuple-element.21.own_sums), channel_id=1, source_target_pairs={{0,1},{1,0},{2,3},{3,2},{4,5},{5,4},{6,7},{7,6},{8,9},{9,8},{10,11... | collective-permute-start | bytes 24584 | tf_op jit(solution)/shard_map/ppermute | solution.py:17
  100.3 7.3 %collective-permute-start.21 = (f16[136,512]{1,0:T(8,128)(2,1)S(1)}, f16[136,512]{1,0:T(8,128)(2,1)S(1)}, u32[]{:S(2)}, u32[]{:S(2)}) collective-permute-start(f16[136,512]{1,0:T(8,128)(2,1)S(1)} %convert_element_type.18), channel_id=1, source_target_pairs={{0,6},{1,7},{2,4},{3,5},{4,2},{5,3},{6,0},{7,1},{8,14},{9,15},{10,... | collective-permute-start | bytes 417800 | tf_op jit(solution)/shard_map/ppermute | solution.py:17
  103.9 12.3 %collective-permute-start.22 = (f16[136,512]{1,0:T(8,128)(2,1)S(1)}, f16[136,512]{1,0:T(8,128)(2,1)S(1)}, u32[]{:S(2)}, u32[]{:S(2)}) collective-permute-start(f16[136,512]{1,0:T(8,128)(2,1)S(1)} %convert_element_type.20), channel_id=1, source_target_pairs={{0,4},{1,5},{2,6},{3,7},{4,0},{5,1},{6,2},{7,3},{8,12},{9,13},{10,... | collective-permute-start | bytes 417800 | tf_op jit(solution)/shard_map/ppermute | solution.py:17
  104.0 12.2 %collective-permute-start.23 = (f16[136,512]{1,0:T(8,128)(2,1)S(1)}, f16[136,512]{1,0:T(8,128)(2,1)S(1)}, u32[]{:S(2)}, u32[]{:S(2)}) collective-permute-start(f16[136,512]{1,0:T(8,128)(2,1)S(1)} %convert_element_type.22), channel_id=1, source_target_pairs={{0,2},{1,3},{2,0},{3,1},{4,6},{5,7},{6,4},{7,5},{8,10},{9,11},{10,... | collective-permute-start | bytes 417800 | tf_op jit(solution)/shard_map/ppermute | solution.py:17
  116.8 3.4 %collective-permute-start.24 = (bf16[64,512]{1,0:T(8,128)(2,1)S(1)}, bf16[64,512]{1,0:T(8,128)(2,1)S(1)}, u32[]{:S(2)}, u32[]{:S(2)}) collective-permute-start(bf16[64,512]{1,0:T(8,128)(2,1)S(1)} %get-tuple-element.28), channel_id=1, source_target_pairs={{0,8},{8,0},{16,24},{24,16},{1,9},{9,1},{17,25},{25,17},{2,10},{10... | collective-permute-start | bytes 196616 | tf_op jit(solution)/shard_map/ppermute | solution.py:17
  117.1 5.9 %collective-permute-start.25 = (bf16[64,512]{1,0:T(8,128)(2,1)S(1)}, bf16[64,512]{1,0:T(8,128)(2,1)S(1)}, u32[]{:S(2)}, u32[]{:S(2)}) collective-permute-start(bf16[64,512]{1,0:T(8,128)(2,1)S(1)} %get-tuple-element.29), channel_id=1, source_target_pairs={{8,16},{16,8},{9,17},{17,9},{10,18},{18,10},{11,19},{19,11},{12,20... | collective-permute-start | bytes 196616 | tf_op jit(solution)/shard_map/ppermute | solution.py:478
  123.3 3.2 %collective-permute-start.26 = (f32[8,128]{1,0:T(8,128)S(1)}, f32[8,128]{1,0:T(8,128)S(1)}, u32[]{:S(2)}, u32[]{:S(2)}) collective-permute-start(f32[8,128]{1,0:T(8,128)S(1)} %products.1), channel_id=1, source_target_pairs={{0,1},{1,0},{2,3},{3,2},{4,5},{5,4},{6,7},{7,6},{8,9},{9,8},{10,11... | collective-permute-start | bytes 12296 | tf_op jit(solution)/shard_map/ppermute | solution.py:17
  126.5 4.4 %collective-permute-start.27 = (f32[8,128]{1,0:T(8,128)S(1)}, f32[8,128]{1,0:T(8,128)S(1)}, u32[]{:S(2)}, u32[]{:S(2)}) collective-permute-start(f32[8,128]{1,0:T(8,128)S(1)} %add.7.refs_0_), channel_id=1, source_target_pairs={{0,6},{1,7},{2,4},{3,5},{4,2},{5,3},{6,0},{7,1},{8,14},{9,15},{10,... | collective-permute-start | bytes 12296 | tf_op jit(solution)/shard_map/ppermute | solution.py:17
  128.8 3.4 %collective-permute-start.28 = (f32[8,128]{1,0:T(8,128)S(1)}, f32[8,128]{1,0:T(8,128)S(1)}, u32[]{:S(2)}, u32[]{:S(2)}) collective-permute-start(f32[8,128]{1,0:T(8,128)S(1)} %add.7.refs_0_), channel_id=1, source_target_pairs={{0,4},{1,5},{2,6},{3,7},{4,0},{5,1},{6,2},{7,3},{8,12},{9,13},{10,... | collective-permute-start | bytes 12296 | tf_op jit(solution)/shard_map/ppermute | solution.py:17
  128.8 3.4 %collective-permute-start.29 = (f32[8,128]{1,0:T(8,128)S(1)}, f32[8,128]{1,0:T(8,128)S(1)}, u32[]{:S(2)}, u32[]{:S(2)}) collective-permute-start(f32[8,128]{1,0:T(8,128)S(1)} %add.7.refs_0_), channel_id=1, source_target_pairs={{0,2},{1,3},{2,0},{3,1},{4,6},{5,7},{6,4},{7,5},{8,10},{9,11},{10,... | collective-permute-start | bytes 12296 | tf_op jit(solution)/shard_map/ppermute | solution.py:17

commit v6 on v5

--- a/solution.py
+++ b/solution.py
@@ -448,20 +448,22 @@
     own_rows = {(None, (0,)): mine, (None, (1,)): got}
     total = project([(staged[0], own_rows)], parts, None, layers, False)
 
-    def is_late(k, key):
-        return len(key[1]) == 1 or (k == final and key[0] != 0 and key[0] not in far)
-
-    late, early = [], {}
-    for k in order:
-        early[k] = {key: piece for key, piece in pieces[k].items() if not is_late(k, key)}
-        held = {key: piece for key, piece in pieces[k].items() if is_late(k, key)}
-        if held:
-            late.append((staged[k], held))
-    steps = [(k, [(staged[k], early[k])]) for k in order[-2::-1] + order[-1:]]
-    if late:
-        steps.append((None, late))
-    for n, (k, groups_of) in enumerate(steps):
-        last = n == len(steps) - 1
+    def held_by(k, kind):
+        return {key: piece for key, piece in pieces[k].items() if kind(*key)}
+
+    def is_far(j, which):
+        return j in far and len(which) == 2
+
+    near = {k: held_by(k, lambda j, which: j not in far) for k in order}
+    passed = [(staged[k], held_by(k, lambda j, which: len(which) == 1)) for k in order]
+    distant = [(staged[k], held_by(k, is_far)) for k in order]
+    steps = [(f"acc{k}", [(staged[k], near[k])]) for k in order[-2::-1]]
+    steps.append((f"acc{final}", [(staged[final], near[final])]))
+    steps.append(("last", distant + passed))
+    steps = [(name, [group for group in groups_of if group[1]]) for name, groups_of in steps]
+    steps = [step for step in steps if step[1]]
+    for name, groups_of in steps:
+        last = name == steps[-1][0]
         total = project(groups_of, parts, total, layers, last)
     split, sums = total
 

time: 134 us -> 127 us (0.948)
  waiting for transfers between devices: 70.8 us -> 64.4 us
    ppermute x29, waiting for transfers between devices: 67.9 us -> 61.1 us  [swap(): lax.ppermute(block, axis, [(i, i ^ mask) for i in range(lax.axis_size(axi...]
  transfers between devices with their start and end apart: 30 -> 30, of which waited for: 17 -> 15; matrix products, arithmetic and copies ran while one was open for 1% -> 1% of each run, Pallas kernels for 6% -> 6%
where the time goes in v6:
time: 127 us; the launch traced here: 126 us
  waiting for transfers between devices  64.4 us (51%)
  starting transfers between devices  42.1 us (33%)
  Pallas kernels  11.1 us (9%)
  local copies, waits for them, and re-layouts  7.57 us (6%)
    ppermute x29, waiting for transfers between devices, swap(): lax.ppermute(block, axis, [(i, i ^ mask) for i in range(lax.axis_size(axi...  61.1 us
    ppermute x29, starting transfers between devices, swap(): lax.ppermute(block, axis, [(i, i ^ mask) for i in range(lax.axis_size(axi...  39.5 us
    unnamed x7, local copies, waits for them, and re-layouts  6.58 us
    pallas_call x5, Pallas kernels, project(): pl.pallas_call(functools.partial(project_kernel, keys, parts, len(started...  5.43 us
    ppermute x1, waiting for transfers between devices, local(): second = lax.ppermute(second, 'section', route + [(b, a) for a, b in route])  3.32 us
    ppermute x1, starting transfers between devices, local(): second = lax.ppermute(second, 'section', route + [(b, a) for a, b in route])  2.56 us
  transfers between devices with their start and end apart: 30, of which 15 were waited for; matrix products, arithmetic and copies ran while one was open for 1% of the time, Pallas kernels for 6%

profile of v6, /device:TPU:5, one launch (start us, length us, event | category | flops | bytes accessed | tf_op | source)
XLA Modules:
  0.0 126.3 jit_solution(9063237607425626644)
XLA Ops:
  0.6 1.0 constant_dynamic-slice_fusion.proj
  1.9 0.7 collective-permute-start.6
  2.7 3.4 %copy-done.1 = bf16[2,256,8192]{2,1,0:T(8,128)(2,1)S(1)} copy-done((bf16[2,256,8192]{2,1,0:T(8,128)(2,1)S(1)}, bf16[2,256,8192]{2,1,0:T(8,128)(2,1)}, u32[]{:S(2)}) %copy-start.1) | copy-done | bytes 8388632
  7.3 0.7 deal.2
  8.1 1.7 %copy-done.2 = bf16[2,256,8192]{2,1,0:T(8,128)(2,1)S(1)} copy-done((bf16[2,256,8192]{2,1,0:T(8,128)(2,1)S(1)}, bf16[2,256,8192]{2,1,0:T(8,128)(2,1)}, u32[]{:S(2)}) %copy-start.2) | copy-done | bytes 8388632
  10.4 2.4 %collective-permute-start.7 = (bf16[512,256]{1,0:T(8,128)(2,1)S(1)}, bf16[512,256]{1,0:T(8,128)(2,1)S(1)}, u32[]{:S(2)}, u32[]{:S(2)}) collective-permute-start(bf16[512,256]{1,0:T(8,128)(2,1)S(1)} %join.1), channel_id=1, source_target_pairs={{0,4},{1,5},{2,6},{3,7},{4,0},{5,1},{6,2},{7,3},{8,12},{9,13},{10,... | collective-permute-start | bytes 786440 | tf_op jit(solution)/shard_map/ppermute | solution.py:17
  13.1 0.8 collective-permute-start
  13.9 10.5 %collective-permute-done.7.refs_2_ = bf16[512,256]{1,0:T(8,128)(2,1)S(1)} collective-permute-done((bf16[512,256]{1,0:T(8,128)(2,1)S(1)}, bf16[512,256]{1,0:T(8,128)(2,1)S(1)}, u32[]{:S(2)}, u32[]{:S(2)}) %collective-permute-start.7) | collective-permute-done | bytes 262176 | tf_op jit(solution)/shard_map/ppermute | solution.py:17
  24.4 1.2 collective-permute-start.15
  25.9 5.0 %collective-permute-done.15.refs_2_ = bf16[512,256]{1,0:T(8,128)(2,1)S(1)} collective-permute-done((bf16[512,256]{1,0:T(8,128)(2,1)S(1)}, bf16[512,256]{1,0:T(8,128)(2,1)S(1)}, u32[]{:S(2)}, u32[]{:S(2)}) %collective-permute-start.15) | collective-permute-done | bytes 262176 | tf_op jit(solution)/shard_map/ppermute | solution.py:17
  30.9 2.2 %collective-permute-start.1 = (bf16[512,2048]{1,0:T(8,128)(2,1)S(1)}, bf16[512,2048]{1,0:T(8,128)(2,1)S(1)}, u32[]{:S(2)}, u32[]{:S(2)}) collective-permute-start(bf16[512,2048]{1,0:T(8,128)(2,1)S(1)} %stage.5.refs_0_.refs_2_), channel_id=1, source_target_pairs={{0,1},{1,0},{2,3},{3,2},{4,5},{5,4},{6,7},{7,6},{8,9},{9,8},{10,11... | collective-permute-start | bytes 6291464 | tf_op jit(solution)/shard_map/ppermute | solution.py:17
  33.1 1.2 collective-permute-start.10
  34.3 6.7 %collective-permute-done.10.refs_3_ = bf16[512,256]{1,0:T(8,128)(2,1)S(1)} collective-permute-done((bf16[512,256]{1,0:T(8,128)(2,1)S(1)}, bf16[512,256]{1,0:T(8,128)(2,1)S(1)}, u32[]{:S(2)}, u32[]{:S(2)}) %collective-permute-start.10) | collective-permute-done | bytes 262176 | tf_op jit(solution)/shard_map/ppermute | solution.py:17
  41.4 6.6 %collective-permute-done.8.refs_4_ = bf16[512,256]{1,0:T(8,128)(2,1)S(1)} collective-permute-done((bf16[512,256]{1,0:T(8,128)(2,1)S(1)}, bf16[512,256]{1,0:T(8,128)(2,1)S(1)}, u32[]{:S(2)}, u32[]{:S(2)}) %collective-permute-start.8) | collective-permute-done | bytes 262176 | tf_op jit(solution)/shard_map/ppermute | solution.py:17
  48.0 1.2 collective-permute-start.16
  49.2 4.9 %collective-permute-done.16.refs_3_ = bf16[512,256]{1,0:T(8,128)(2,1)S(1)} collective-permute-done((bf16[512,256]{1,0:T(8,128)(2,1)S(1)}, bf16[512,256]{1,0:T(8,128)(2,1)S(1)}, u32[]{:S(2)}, u32[]{:S(2)}) %collective-permute-start.16) | collective-permute-done | bytes 262176 | tf_op jit(solution)/shard_map/ppermute | solution.py:17
  54.6 4.8 %collective-permute-done.17.refs_4_ = bf16[512,256]{1,0:T(8,128)(2,1)S(1)} collective-permute-done((bf16[512,256]{1,0:T(8,128)(2,1)S(1)}, bf16[512,256]{1,0:T(8,128)(2,1)S(1)}, u32[]{:S(2)}, u32[]{:S(2)}) %collective-permute-start.17) | collective-permute-done | bytes 262176 | tf_op jit(solution)/shard_map/ppermute | solution.py:17
  59.3 1.2 collective-permute-start.12
  60.6 4.0 %collective-permute-done.12.refs_2_ = bf16[512,256]{1,0:T(8,128)(2,1)S(1)} collective-permute-done((bf16[512,256]{1,0:T(8,128)(2,1)S(1)}, bf16[512,256]{1,0:T(8,128)(2,1)S(1)}, u32[]{:S(2)}, u32[]{:S(2)}) %collective-permute-start.12) | collective-permute-done | bytes 262176 | tf_op jit(solution)/shard_map/ppermute | solution.py:17
  64.6 1.2 collective-permute-start.13
  65.8 4.0 %collective-permute-done.13.refs_3_ = bf16[512,256]{1,0:T(8,128)(2,1)S(1)} collective-permute-done((bf16[512,256]{1,0:T(8,128)(2,1)S(1)}, bf16[512,256]{1,0:T(8,128)(2,1)S(1)}, u32[]{:S(2)}, u32[]{:S(2)}) %collective-permute-start.13) | collective-permute-done | bytes 262176 | tf_op jit(solution)/shard_map/ppermute | solution.py:17
  70.3 1.1 collective-permute-start.4
  71.4 2.9 %collective-permute-start.5 = (bf16[512,256]{1,0:T(8,128)(2,1)S(1)}, bf16[512,256]{1,0:T(8,128)(2,1)S(1)}, u32[]{:S(2)}, u32[]{:S(2)}) collective-permute-start(bf16[512,256]{1,0:T(8,128)(2,1)S(1)} %pick.1), channel_id=1, source_target_pairs={{0,6},{1,7},{2,4},{3,5},{4,2},{5,3},{6,0},{7,1},{8,14},{9,15},{10,... | collective-permute-start | bytes 786440 | tf_op jit(solution)/shard_map/ppermute | solution.py:17
  74.3 1.2 project.5.refs_5_
  75.5 1.0 project.6.refs_5_
  76.5 1.3 %collective-permute-start.11 = (bf16[256,256]{1,0:T(8,128)(2,1)S(1)}, bf16[256,256]{1,0:T(8,128)(2,1)S(1)}, u32[]{:S(2)}, u32[]{:S(2)}) collective-permute-start(bf16[256,256]{1,0:T(8,128)(2,1)S(1)} %slice.9), channel_id=1, source_target_pairs={{0,16},{8,24},{16,0},{24,8},{1,17},{9,25},{17,1},{25,9},{2,18},{10... | collective-permute-start | bytes 393224 | tf_op jit(solution)/shard_map/ppermute | solution.py:17
  77.9 1.2 collective-permute-start.9
  79.1 1.0 project.7.refs_5_
  80.1 1.0 project.8.refs_10_
  81.1 1.0 collective-permute-done.11.refs_9_
  82.1 1.2 project.9
  83.4 7.8 %collective-permute-start.19 = (bf16[2,2,512,256]{3,2,1,0:T(8,128)(2,1)S(1)}, bf16[2,2,512,256]{3,2,1,0:T(8,128)(2,1)S(1)}, u32[]{:S(2)}, u32[]{:S(2)}) collective-permute-start(bf16[2,2,512,256]{3,2,1,0:T(8,128)(2,1)S(1)} %get-tuple-element.20.own), channel_id=1, source_target_pairs={{0,1},{1,0},{2,3},{3,2},{4,5},{5,4},{6,7},{7,6},{8,9},{9,8},{10,11... | collective-permute-start | bytes 3145736 | tf_op jit(solution)/shard_map/ppermute | solution.py:17
  91.9 1.6 %collective-permute-done.20.oth_sums = f32[8,256]{1,0:T(8,128)S(1)} collective-permute-done((f32[8,256]{1,0:T(8,128)S(1)}, f32[8,256]{1,0:T(8,128)S(1)}, u32[]{:S(2)}, u32[]{:S(2)}) %collective-permute-start.20) | collective-permute-done | bytes 8224 | tf_op jit(solution)/shard_map/ppermute | solution.py:17
  93.5 1.0 gram.1
  94.5 2.3 %collective-permute-start.21 = (f16[136,512]{1,0:T(8,128)(2,1)S(1)}, f16[136,512]{1,0:T(8,128)(2,1)S(1)}, u32[]{:S(2)}, u32[]{:S(2)}) collective-permute-start(f16[136,512]{1,0:T(8,128)(2,1)S(1)} %convert_element_type.18), channel_id=1, source_target_pairs={{0,6},{1,7},{2,4},{3,5},{4,2},{5,3},{6,0},{7,1},{8,14},{9,15},{10,... | collective-permute-start | bytes 417800 | tf_op jit(solution)/shard_map/ppermute | solution.py:17
  97.0 1.3 %collective-permute-start.23 = (f16[136,512]{1,0:T(8,128)(2,1)S(1)}, f16[136,512]{1,0:T(8,128)(2,1)S(1)}, u32[]{:S(2)}, u32[]{:S(2)}) collective-permute-start(f16[136,512]{1,0:T(8,128)(2,1)S(1)} %convert_element_type.22), channel_id=1, source_target_pairs={{0,2},{1,3},{2,0},{3,1},{4,6},{5,7},{6,4},{7,5},{8,10},{9,11},{10,... | collective-permute-start | bytes 417800 | tf_op jit(solution)/shard_map/ppermute | solution.py:17
  98.3 3.0 %collective-permute-done.21 = f16[136,512]{1,0:T(8,128)(2,1)S(1)} collective-permute-done((f16[136,512]{1,0:T(8,128)(2,1)S(1)}, f16[136,512]{1,0:T(8,128)(2,1)S(1)}, u32[]{:S(2)}, u32[]{:S(2)}) %collective-permute-start.21) | collective-permute-done | bytes 139296 | tf_op jit(solution)/shard_map/ppermute | solution.py:17
  101.3 7.4 %collective-permute-done.22 = f16[136,512]{1,0:T(8,128)(2,1)S(1)} collective-permute-done((f16[136,512]{1,0:T(8,128)(2,1)S(1)}, f16[136,512]{1,0:T(8,128)(2,1)S(1)}, u32[]{:S(2)}, u32[]{:S(2)}) %collective-permute-start.22) | collective-permute-done | bytes 139296 | tf_op jit(solution)/shard_map/ppermute | solution.py:17
  109.3 1.3 %collective-permute-start.24 = (bf16[64,512]{1,0:T(8,128)(2,1)S(1)}, bf16[64,512]{1,0:T(8,128)(2,1)S(1)}, u32[]{:S(2)}, u32[]{:S(2)}) collective-permute-start(bf16[64,512]{1,0:T(8,128)(2,1)S(1)} %get-tuple-element.28), channel_id=1, source_target_pairs={{0,8},{8,0},{16,24},{24,16},{1,9},{9,1},{17,25},{25,17},{2,10},{10... | collective-permute-start | bytes 196616 | tf_op jit(solution)/shard_map/ppermute | solution.py:17
  110.5 2.6 %collective-permute-start.25 = (bf16[64,512]{1,0:T(8,128)(2,1)S(1)}, bf16[64,512]{1,0:T(8,128)(2,1)S(1)}, u32[]{:S(2)}, u32[]{:S(2)}) collective-permute-start(bf16[64,512]{1,0:T(8,128)(2,1)S(1)} %get-tuple-element.29), channel_id=1, source_target_pairs={{8,16},{16,8},{9,17},{17,9},{10,18},{18,10},{11,19},{19,11},{12,20... | collective-permute-start | bytes 196616 | tf_op jit(solution)/shard_map/ppermute | solution.py:480
  113.1 3.3 %collective-permute-done.25.two = bf16[64,512]{1,0:T(8,128)(2,1)S(1)} collective-permute-done((bf16[64,512]{1,0:T(8,128)(2,1)S(1)}, bf16[64,512]{1,0:T(8,128)(2,1)S(1)}, u32[]{:S(2)}, u32[]{:S(2)}) %collective-permute-start.25) | collective-permute-done | bytes 65568 | tf_op jit(solution)/shard_map/ppermute | solution.py:480
  116.7 2.7 %collective-permute-start.26 = (f32[8,128]{1,0:T(8,128)S(1)}, f32[8,128]{1,0:T(8,128)S(1)}, u32[]{:S(2)}, u32[]{:S(2)}) collective-permute-start(f32[8,128]{1,0:T(8,128)S(1)} %products.1), channel_id=1, source_target_pairs={{0,1},{1,0},{2,3},{3,2},{4,5},{5,4},{6,7},{7,6},{8,9},{9,8},{10,11... | collective-permute-start | bytes 12296 | tf_op jit(solution)/shard_map/ppermute | solution.py:17
  119.4 0.8 collective-permute-done.26
  120.3 1.7 %collective-permute-start.27 = (f32[8,128]{1,0:T(8,128)S(1)}, f32[8,128]{1,0:T(8,128)S(1)}, u32[]{:S(2)}, u32[]{:S(2)}) collective-permute-start(f32[8,128]{1,0:T(8,128)S(1)} %add.7.refs_0_), channel_id=1, source_target_pairs={{0,6},{1,7},{2,4},{3,5},{4,2},{5,3},{6,0},{7,1},{8,14},{9,15},{10,... | collective-permute-start | bytes 12296 | tf_op jit(solution)/shard_map/ppermute | solution.py:17
  122.0 1.8 %collective-permute-start.29 = (f32[8,128]{1,0:T(8,128)S(1)}, f32[8,128]{1,0:T(8,128)S(1)}, u32[]{:S(2)}, u32[]{:S(2)}) collective-permute-start(f32[8,128]{1,0:T(8,128)S(1)} %add.7.refs_0_), channel_id=1, source_target_pairs={{0,2},{1,3},{2,0},{3,1},{4,6},{5,7},{6,4},{7,5},{8,10},{9,11},{10,... | collective-permute-start | bytes 12296 | tf_op jit(solution)/shard_map/ppermute | solution.py:17
  123.8 0.9 copy.4
  124.7 0.9 collective-permute-done.28.refs_2_
  125.6 0.7 ratios.1
  (47 shorter events, 5.9 us)
Async XLA Ops:
  1.9 8.4 %collective-permute-start.6 = (bf16[256,256]{1,0:T(8,128)(2,1)S(1)}, bf16[256,256]{1,0:T(8,128)(2,1)S(1)}, u32[]{:S(2)}, u32[]{:S(2)}) collective-permute-start(bf16[256,256]{1,0:T(8,128)(2,1)S(1)} %get-tuple-element.19), channel_id=1, source_target_pairs={{0,1},{1,0},{2,3},{3,2},{4,5},{5,4},{6,7},{7,6},{8,9},{9,8},{10,11... | collective-permute-start | bytes 393224 | tf_op jit(solution)/shard_map/ppermute | solution.py:17
  2.7 3.4 %copy-start.1 = (bf16[2,256,8192]{2,1,0:T(8,128)(2,1)S(1)}, bf16[2,256,8192]{2,1,0:T(8,128)(2,1)}, u32[]{:S(2)}) copy-start(bf16[2,256,8192]{2,1,0:T(8,128)(2,1)} %param.2) | copy-start | bytes 25165828
  6.1 1.2 copy-start
  6.1 3.7 %copy-start.2 = (bf16[2,256,8192]{2,1,0:T(8,128)(2,1)S(1)}, bf16[2,256,8192]{2,1,0:T(8,128)(2,1)}, u32[]{:S(2)}) copy-start(bf16[2,256,8192]{2,1,0:T(8,128)(2,1)} %param.2) | copy-start | bytes 25165828
  6.6 63.7 %collective-permute-start.18 = (bf16[512,2048]{1,0:T(8,128)(2,1)S(1)}, bf16[512,2048]{1,0:T(8,128)(2,1)S(1)}, u32[]{:S(2)}, u32[]{:S(2)}) collective-permute-start(bf16[512,2048]{1,0:T(8,128)(2,1)S(1)} %stage.7.refs_0_), channel_id=1, source_target_pairs={{0,1},{1,0},{2,3},{3,2},{4,5},{5,4},{6,7},{7,6},{8,9},{9,8},{10,11... | collective-permute-start | bytes 6291464 | tf_op jit(solution)/shard_map/ppermute | solution.py:17
  8.0 25.1 %collective-permute-start.3 = (bf16[1024,256]{1,0:T(8,128)(2,1)S(1)}, bf16[1024,256]{1,0:T(8,128)(2,1)S(1)}, u32[]{:S(2)}, u32[]{:S(2)}) collective-permute-start(bf16[1024,256]{1,0:T(8,128)(2,1)S(1)} %get-tuple-element.17), channel_id=1, source_target_pairs={{0,1},{1,0},{2,3},{3,2},{4,5},{5,4},{6,7},{7,6},{8,9},{9,8},{10,11... | collective-permute-start | bytes 1572872 | tf_op jit(solution)/shard_map/ppermute | solution.py:17
  10.3 61.1 %collective-permute-start.2 = (bf16[512,2048]{1,0:T(8,128)(2,1)S(1)}, bf16[512,2048]{1,0:T(8,128)(2,1)S(1)}, u32[]{:S(2)}, u32[]{:S(2)}) collective-permute-start(bf16[512,2048]{1,0:T(8,128)(2,1)S(1)} %stage.6.refs_0_.refs_4_), channel_id=1, source_target_pairs={{0,1},{1,0},{2,3},{3,2},{4,5},{5,4},{6,7},{7,6},{8,9},{9,8},{10,11... | collective-permute-start | bytes 6291464 | tf_op jit(solution)/shard_map/ppermute | solution.py:17
  10.4 14.0 %collective-permute-start.7 = (bf16[512,256]{1,0:T(8,128)(2,1)S(1)}, bf16[512,256]{1,0:T(8,128)(2,1)S(1)}, u32[]{:S(2)}, u32[]{:S(2)}) collective-permute-start(bf16[512,256]{1,0:T(8,128)(2,1)S(1)} %join.1), channel_id=1, source_target_pairs={{0,4},{1,5},{2,6},{3,7},{4,0},{5,1},{6,2},{7,3},{8,12},{9,13},{10,... | collective-permute-start | bytes 786440 | tf_op jit(solution)/shard_map/ppermute | solution.py:17
  13.1 64.8 %collective-permute-start = (bf16[512,2048]{1,0:T(8,128)(2,1)S(1)}, bf16[512,2048]{1,0:T(8,128)(2,1)S(1)}, u32[]{:S(2)}, u32[]{:S(2)}) collective-permute-start(bf16[512,2048]{1,0:T(8,128)(2,1)S(1)} %stage.4.refs_0_), channel_id=1, source_target_pairs={{0,1},{1,0},{2,3},{3,2},{4,5},{5,4},{6,7},{7,6},{8,9},{9,8},{10,11... | collective-permute-start | bytes 6291464 | tf_op jit(solution)/shard_map/ppermute | solution.py:17
  24.4 6.5 %collective-permute-start.15 = (bf16[512,256]{1,0:T(8,128)(2,1)S(1)}, bf16[512,256]{1,0:T(8,128)(2,1)S(1)}, u32[]{:S(2)}, u32[]{:S(2)}) collective-permute-start(bf16[512,256]{1,0:T(8,128)(2,1)S(1)} %join.1), channel_id=1, source_target_pairs={{0,2},{1,3},{2,0},{3,1},{4,6},{5,7},{6,4},{7,5},{8,10},{9,11},{10,... | collective-permute-start | bytes 786440 | tf_op jit(solution)/shard_map/ppermute | solution.py:17
  30.9 49.2 %collective-permute-start.1 = (bf16[512,2048]{1,0:T(8,128)(2,1)S(1)}, bf16[512,2048]{1,0:T(8,128)(2,1)S(1)}, u32[]{:S(2)}, u32[]{:S(2)}) collective-permute-start(bf16[512,2048]{1,0:T(8,128)(2,1)S(1)} %stage.5.refs_0_.refs_2_), channel_id=1, source_target_pairs={{0,1},{1,0},{2,3},{3,2},{4,5},{5,4},{6,7},{7,6},{8,9},{9,8},{10,11... | collective-permute-start | bytes 6291464 | tf_op jit(solution)/shard_map/ppermute | solution.py:17
  33.1 7.9 %collective-permute-start.10 = (bf16[512,256]{1,0:T(8,128)(2,1)S(1)}, bf16[512,256]{1,0:T(8,128)(2,1)S(1)}, u32[]{:S(2)}, u32[]{:S(2)}) collective-permute-start(bf16[512,256]{1,0:T(8,128)(2,1)S(1)} %collective-permute-done.7.refs_2_), channel_id=1, source_target_pairs={{0,8},{8,0},{16,24},{24,16},{1,9},{9,1},{17,25},{25,17},{2,10},{10... | collective-permute-start | bytes 786440 | tf_op jit(solution)/shard_map/ppermute | solution.py:17
  41.0 7.0 %collective-permute-start.8 = (bf16[512,256]{1,0:T(8,128)(2,1)S(1)}, bf16[512,256]{1,0:T(8,128)(2,1)S(1)}, u32[]{:S(2)}, u32[]{:S(2)}) collective-permute-start(bf16[512,256]{1,0:T(8,128)(2,1)S(1)} %collective-permute-done.7.refs_2_), channel_id=1, source_target_pairs={{0,16},{8,24},{16,0},{24,8},{1,17},{9,25},{17,1},{25,9},{2,18},{10... | collective-permute-start | bytes 786440 | tf_op jit(solution)/shard_map/ppermute | solution.py:17
  48.0 6.1 %collective-permute-start.16 = (bf16[512,256]{1,0:T(8,128)(2,1)S(1)}, bf16[512,256]{1,0:T(8,128)(2,1)S(1)}, u32[]{:S(2)}, u32[]{:S(2)}) collective-permute-start(bf16[512,256]{1,0:T(8,128)(2,1)S(1)} %collective-permute-done.15.refs_2_), channel_id=1, source_target_pairs={{0,8},{8,0},{16,24},{24,16},{1,9},{9,1},{17,25},{25,17},{2,10},{10... | collective-permute-start | bytes 786440 | tf_op jit(solution)/shard_map/ppermute | solution.py:17
  54.1 5.2 %collective-permute-start.17 = (bf16[512,256]{1,0:T(8,128)(2,1)S(1)}, bf16[512,256]{1,0:T(8,128)(2,1)S(1)}, u32[]{:S(2)}, u32[]{:S(2)}) collective-permute-start(bf16[512,256]{1,0:T(8,128)(2,1)S(1)} %collective-permute-done.15.refs_2_), channel_id=1, source_target_pairs={{0,16},{8,24},{16,0},{24,8},{1,17},{9,25},{17,1},{25,9},{2,18},{10... | collective-permute-start | bytes 786440 | tf_op jit(solution)/shard_map/ppermute | solution.py:17
  59.3 5.2 %collective-permute-start.12 = (bf16[512,256]{1,0:T(8,128)(2,1)S(1)}, bf16[512,256]{1,0:T(8,128)(2,1)S(1)}, u32[]{:S(2)}, u32[]{:S(2)}) collective-permute-start(bf16[512,256]{1,0:T(8,128)(2,1)S(1)} %collective-permute-done.7.refs_2_), channel_id=1, source_target_pairs={{0,2},{1,3},{2,0},{3,1},{4,6},{5,7},{6,4},{7,5},{8,10},{9,11},{10,... | collective-permute-start | bytes 786440 | tf_op jit(solution)/shard_map/ppermute | solution.py:17
  64.6 5.2 %collective-permute-start.13 = (bf16[512,256]{1,0:T(8,128)(2,1)S(1)}, bf16[512,256]{1,0:T(8,128)(2,1)S(1)}, u32[]{:S(2)}, u32[]{:S(2)}) collective-permute-start(bf16[512,256]{1,0:T(8,128)(2,1)S(1)} %collective-permute-done.12.refs_2_), channel_id=1, source_target_pairs={{0,8},{8,0},{16,24},{24,16},{1,9},{9,1},{17,25},{25,17},{2,10},{10... | collective-permute-start | bytes 786440 | tf_op jit(solution)/shard_map/ppermute | solution.py:17
  69.8 6.8 %collective-permute-start.14 = (bf16[512,256]{1,0:T(8,128)(2,1)S(1)}, bf16[512,256]{1,0:T(8,128)(2,1)S(1)}, u32[]{:S(2)}, u32[]{:S(2)}) collective-permute-start(bf16[512,256]{1,0:T(8,128)(2,1)S(1)} %collective-permute-done.12.refs_2_), channel_id=1, source_target_pairs={{0,16},{8,24},{16,0},{24,8},{1,17},{9,25},{17,1},{25,9},{2,18},{10... | collective-permute-start | bytes 786440 | tf_op jit(solution)/shard_map/ppermute | solution.py:17
  70.3 10.8 %collective-permute-start.4 = (bf16[512,256]{1,0:T(8,128)(2,1)S(1)}, bf16[512,256]{1,0:T(8,128)(2,1)S(1)}, u32[]{:S(2)}, u32[]{:S(2)}) collective-permute-start(bf16[512,256]{1,0:T(8,128)(2,1)S(1)} %pick.1), channel_id=1, source_target_pairs={{0,2},{1,3},{2,0},{3,1},{4,6},{5,7},{6,4},{7,5},{8,10},{9,11},{10,... | collective-permute-start | bytes 786440 | tf_op jit(solution)/shard_map/ppermute | solution.py:17
  71.4 9.7 %collective-permute-start.5 = (bf16[512,256]{1,0:T(8,128)(2,1)S(1)}, bf16[512,256]{1,0:T(8,128)(2,1)S(1)}, u32[]{:S(2)}, u32[]{:S(2)}) collective-permute-start(bf16[512,256]{1,0:T(8,128)(2,1)S(1)} %pick.1), channel_id=1, source_target_pairs={{0,6},{1,7},{2,4},{3,5},{4,2},{5,3},{6,0},{7,1},{8,14},{9,15},{10,... | collective-permute-start | bytes 786440 | tf_op jit(solution)/shard_map/ppermute | solution.py:17
  76.5 5.6 %collective-permute-start.11 = (bf16[256,256]{1,0:T(8,128)(2,1)S(1)}, bf16[256,256]{1,0:T(8,128)(2,1)S(1)}, u32[]{:S(2)}, u32[]{:S(2)}) collective-permute-start(bf16[256,256]{1,0:T(8,128)(2,1)S(1)} %slice.9), channel_id=1, source_target_pairs={{0,16},{8,24},{16,0},{24,8},{1,17},{9,25},{17,1},{25,9},{2,18},{10... | collective-permute-start | bytes 393224 | tf_op jit(solution)/shard_map/ppermute | solution.py:17
  77.9 4.3 %collective-permute-start.9 = (bf16[256,256]{1,0:T(8,128)(2,1)S(1)}, bf16[256,256]{1,0:T(8,128)(2,1)S(1)}, u32[]{:S(2)}, u32[]{:S(2)}) collective-permute-start(bf16[256,256]{1,0:T(8,128)(2,1)S(1)} %slice.8), channel_id=1, source_target_pairs={{0,8},{8,0},{16,24},{24,16},{1,9},{9,1},{17,25},{25,17},{2,10},{10... | collective-permute-start | bytes 393224 | tf_op jit(solution)/shard_map/ppermute | solution.py:17
  83.4 10.1 %collective-permute-start.19 = (bf16[2,2,512,256]{3,2,1,0:T(8,128)(2,1)S(1)}, bf16[2,2,512,256]{3,2,1,0:T(8,128)(2,1)S(1)}, u32[]{:S(2)}, u32[]{:S(2)}) collective-permute-start(bf16[2,2,512,256]{3,2,1,0:T(8,128)(2,1)S(1)} %get-tuple-element.20.own), channel_id=1, source_target_pairs={{0,1},{1,0},{2,3},{3,2},{4,5},{5,4},{6,7},{7,6},{8,9},{9,8},{10,11... | collective-permute-start | bytes 3145736 | tf_op jit(solution)/shard_map/ppermute | solution.py:17
  91.2 2.3 %collective-permute-start.20 = (f32[8,256]{1,0:T(8,128)S(1)}, f32[8,256]{1,0:T(8,128)S(1)}, u32[]{:S(2)}, u32[]{:S(2)}) collective-permute-start(f32[8,256]{1,0:T(8,128)S(1)} %get-tuple-element.21.own_sums), channel_id=1, source_target_pairs={{0,1},{1,0},{2,3},{3,2},{4,5},{5,4},{6,7},{7,6},{8,9},{9,8},{10,11... | collective-permute-start | bytes 24584 | tf_op jit(solution)/shard_map/ppermute | solution.py:17
  94.5 6.8 %collective-permute-start.21 = (f16[136,512]{1,0:T(8,128)(2,1)S(1)}, f16[136,512]{1,0:T(8,128)(2,1)S(1)}, u32[]{:S(2)}, u32[]{:S(2)}) collective-permute-start(f16[136,512]{1,0:T(8,128)(2,1)S(1)} %convert_element_type.18), channel_id=1, source_target_pairs={{0,6},{1,7},{2,4},{3,5},{4,2},{5,3},{6,0},{7,1},{8,14},{9,15},{10,... | collective-permute-start | bytes 417800 | tf_op jit(solution)/shard_map/ppermute | solution.py:17
  96.9 11.8 %collective-permute-start.22 = (f16[136,512]{1,0:T(8,128)(2,1)S(1)}, f16[136,512]{1,0:T(8,128)(2,1)S(1)}, u32[]{:S(2)}, u32[]{:S(2)}) collective-permute-start(f16[136,512]{1,0:T(8,128)(2,1)S(1)} %convert_element_type.20), channel_id=1, source_target_pairs={{0,4},{1,5},{2,6},{3,7},{4,0},{5,1},{6,2},{7,3},{8,12},{9,13},{10,... | collective-permute-start | bytes 417800 | tf_op jit(solution)/shard_map/ppermute | solution.py:17
  97.0 11.7 %collective-permute-start.23 = (f16[136,512]{1,0:T(8,128)(2,1)S(1)}, f16[136,512]{1,0:T(8,128)(2,1)S(1)}, u32[]{:S(2)}, u32[]{:S(2)}) collective-permute-start(f16[136,512]{1,0:T(8,128)(2,1)S(1)} %convert_element_type.22), channel_id=1, source_target_pairs={{0,2},{1,3},{2,0},{3,1},{4,6},{5,7},{6,4},{7,5},{8,10},{9,11},{10,... | collective-permute-start | bytes 417800 | tf_op jit(solution)/shard_map/ppermute | solution.py:17
  109.3 3.8 %collective-permute-start.24 = (bf16[64,512]{1,0:T(8,128)(2,1)S(1)}, bf16[64,512]{1,0:T(8,128)(2,1)S(1)}, u32[]{:S(2)}, u32[]{:S(2)}) collective-permute-start(bf16[64,512]{1,0:T(8,128)(2,1)S(1)} %get-tuple-element.28), channel_id=1, source_target_pairs={{0,8},{8,0},{16,24},{24,16},{1,9},{9,1},{17,25},{25,17},{2,10},{10... | collective-permute-start | bytes 196616 | tf_op jit(solution)/shard_map/ppermute | solution.py:17
  110.5 5.9 %collective-permute-start.25 = (bf16[64,512]{1,0:T(8,128)(2,1)S(1)}, bf16[64,512]{1,0:T(8,128)(2,1)S(1)}, u32[]{:S(2)}, u32[]{:S(2)}) collective-permute-start(bf16[64,512]{1,0:T(8,128)(2,1)S(1)} %get-tuple-element.29), channel_id=1, source_target_pairs={{8,16},{16,8},{9,17},{17,9},{10,18},{18,10},{11,19},{19,11},{12,20... | collective-permute-start | bytes 196616 | tf_op jit(solution)/shard_map/ppermute | solution.py:480
  116.7 3.6 %collective-permute-start.26 = (f32[8,128]{1,0:T(8,128)S(1)}, f32[8,128]{1,0:T(8,128)S(1)}, u32[]{:S(2)}, u32[]{:S(2)}) collective-permute-start(f32[8,128]{1,0:T(8,128)S(1)} %products.1), channel_id=1, source_target_pairs={{0,1},{1,0},{2,3},{3,2},{4,5},{5,4},{6,7},{7,6},{8,9},{9,8},{10,11... | collective-permute-start | bytes 12296 | tf_op jit(solution)/shard_map/ppermute | solution.py:17
  120.3 4.4 %collective-permute-start.27 = (f32[8,128]{1,0:T(8,128)S(1)}, f32[8,128]{1,0:T(8,128)S(1)}, u32[]{:S(2)}, u32[]{:S(2)}) collective-permute-start(f32[8,128]{1,0:T(8,128)S(1)} %add.7.refs_0_), channel_id=1, source_target_pairs={{0,6},{1,7},{2,4},{3,5},{4,2},{5,3},{6,0},{7,1},{8,14},{9,15},{10,... | collective-permute-start | bytes 12296 | tf_op jit(solution)/shard_map/ppermute | solution.py:17
  122.0 3.6 %collective-permute-start.28 = (f32[8,128]{1,0:T(8,128)S(1)}, f32[8,128]{1,0:T(8,128)S(1)}, u32[]{:S(2)}, u32[]{:S(2)}) collective-permute-start(f32[8,128]{1,0:T(8,128)S(1)} %add.7.refs_0_), channel_id=1, source_target_pairs={{0,4},{1,5},{2,6},{3,7},{4,0},{5,1},{6,2},{7,3},{8,12},{9,13},{10,... | collective-permute-start | bytes 12296 | tf_op jit(solution)/shard_map/ppermute | solution.py:17
  122.0 3.6 %collective-permute-start.29 = (f32[8,128]{1,0:T(8,128)S(1)}, f32[8,128]{1,0:T(8,128)S(1)}, u32[]{:S(2)}, u32[]{:S(2)}) collective-permute-start(f32[8,128]{1,0:T(8,128)S(1)} %add.7.refs_0_), channel_id=1, source_target_pairs={{0,2},{1,3},{2,0},{3,1},{4,6},{5,7},{6,4},{7,5},{8,10},{9,11},{10,... | collective-permute-start | bytes 12296 | tf_op jit(solution)/shard_map/ppermute | solution.py:17

commit v7 on v6

--- a/solution.py
+++ b/solution.py
@@ -291,12 +291,11 @@
 
 
 def finish_kernel(layers, tokens, *refs):
-    messages, (sketch, turned, first_out, second_out) = refs[:-4], refs[-4:]
+    messages, (turned, first_out, second_out) = refs[:-3], refs[-3:]
     chips = len(messages)
-    chip, core, section = place()
+    chip, _, section = place()
     rank = messages[0].shape[1]
     width = (messages[0].shape[0] - tail_rows(layers)) // layers
-    half = rank // 2
     here = lax.broadcasted_iota(jnp.int32, (width, rank), 1)
     here = here == lax.broadcasted_iota(jnp.int32, (width, rank), 0) + chip * width
     kept = []
@@ -316,13 +315,6 @@
             value = value + (tokens // chips) * lifted * drift
         turned[layer] = value
         kept.append(value)
-        flipped = value.T
-        for i in range(chips):
-            for side in range(2):
-                at = side * half + i * width
-                to = 2 * width * i + width * (core if side == 0 else 1 - core)
-                rows = pl.ds(pl.multiple_of(to, 8), width)
-                sketch[layer, rows, :] = flipped[at : at + width]
     odd = section % 2 == 1
     first_out[...] = jnp.where(odd, kept[0], kept[-1]).astype(BF16)
     second_out[...] = jnp.where(odd, kept[-1], kept[0]).astype(BF16)
@@ -335,17 +327,42 @@
     return pl.pallas_call(
         functools.partial(finish_kernel, layers, tokens),
         out_shape=(
-            jax.ShapeDtypeStruct((layers, rank, width), F32),
             jax.ShapeDtypeStruct((layers, width, rank), F32),
             edge,
             edge,
         ),
         in_specs=[VMEM] * len(messages),
-        out_specs=(VMEM,) * 4,
+        out_specs=(VMEM,) * 3,
         compiler_params=params(6),
         cost_estimate=cost(1e6, 2e6),
         name="finish",
     )(*messages)
+
+
+def upright_kernel(turned, sketch):
+    core = place()[1]
+    layers, width, rank = turned.shape
+    for layer in range(layers):
+        flipped = turned[layer].T
+        for i in range(rank // (2 * width)):
+            for side in range(2):
+                at = side * (rank // 2) + i * width
+                to = 2 * width * i + width * (core if side == 0 else 1 - core)
+                rows = pl.ds(pl.multiple_of(to, 8), width)
+                sketch[layer, rows, :] = flipped[at : at + width]
+
+
+def upright(turned):
+    layers, width, rank = turned.shape
+    return pl.pallas_call(
+        upright_kernel,
+        out_shape=jax.ShapeDtypeStruct((layers, rank, width), F32),
+        in_specs=[VMEM],
+        out_specs=VMEM,
+        compiler_params=params(6),
+        cost_estimate=cost(1e6, 2e6),
+        name="upright",
+    )(turned)
 
 
 def products_kernel(layers, sections, turned, one, two, out):
@@ -474,11 +491,12 @@
     arrived = [messages[0]]
     for k in reversed(range(1, chips)):
         arrived.append(swap(messages[k].astype(jnp.float16), "tok", 2 * k).astype(F32))
-    sketch, turned, first, second = finish(arrived, layers, tok_rows * groups)
+    turned, first, second = finish(arrived, layers, tok_rows * groups)
 
     route = [(i, i + 1) for i in range(1, sections - 1, 2)]
     second = lax.ppermute(second, "section", route + [(b, a) for a, b in route])
     first = swap(first, "section", 1)
+    sketch = upright(turned)
     value = products(turned, first, second, sections)
     value = value + swap(value, "tok", 1)
     if chips <= 4:

time: 127 us -> 127 us (level)
  no operation moved by 1% of the time
where the time goes in v7:
time: 127 us; the launch traced here: 126 us
  waiting for transfers between devices  64.2 us (51%)
  starting transfers between devices  42.1 us (33%)
  Pallas kernels  11.2 us (9%)
  local copies, waits for them, and re-layouts  7.58 us (6%)
    ppermute x29, waiting for transfers between devices, swap(): lax.ppermute(block, axis, [(i, i ^ mask) for i in range(lax.axis_size(axi...  60.9 us
    ppermute x29, starting transfers between devices, swap(): lax.ppermute(block, axis, [(i, i ^ mask) for i in range(lax.axis_size(axi...  39.5 us
    unnamed x7, local copies, waits for them, and re-layouts  6.58 us
    pallas_call x5, Pallas kernels, project(): pl.pallas_call(functools.partial(project_kernel, keys, parts, len(started...  5.43 us
    ppermute x1, waiting for transfers between devices, local(): second = lax.ppermute(second, 'section', route + [(b, a) for a, b in route])  3.32 us
    ppermute x1, starting transfers between devices, local(): second = lax.ppermute(second, 'section', route + [(b, a) for a, b in route])  2.56 us
  transfers between devices with their start and end apart: 30, of which 15 were waited for; matrix products, arithmetic and copies ran while one was open for 1% of the time, Pallas kernels for 6%

profile of v7, /device:TPU:5, one launch (start us, length us, event | category | flops | bytes accessed | tf_op | source)
XLA Modules:
  0.0 126.2 jit_solution(6934302614690175456)
XLA Ops:
  0.6 1.0 constant_dynamic-slice_fusion.proj
  1.9 0.7 collective-permute-start.6
  2.7 3.4 %copy-done.1 = bf16[2,256,8192]{2,1,0:T(8,128)(2,1)S(1)} copy-done((bf16[2,256,8192]{2,1,0:T(8,128)(2,1)S(1)}, bf16[2,256,8192]{2,1,0:T(8,128)(2,1)}, u32[]{:S(2)}) %copy-start.1) | copy-done | bytes 8388632
  7.3 0.7 deal.2
  8.1 1.7 %copy-done.2 = bf16[2,256,8192]{2,1,0:T(8,128)(2,1)S(1)} copy-done((bf16[2,256,8192]{2,1,0:T(8,128)(2,1)S(1)}, bf16[2,256,8192]{2,1,0:T(8,128)(2,1)}, u32[]{:S(2)}) %copy-start.2) | copy-done | bytes 8388632
  10.4 2.4 %collective-permute-start.7 = (bf16[512,256]{1,0:T(8,128)(2,1)S(1)}, bf16[512,256]{1,0:T(8,128)(2,1)S(1)}, u32[]{:S(2)}, u32[]{:S(2)}) collective-permute-start(bf16[512,256]{1,0:T(8,128)(2,1)S(1)} %join.1), channel_id=1, source_target_pairs={{0,4},{1,5},{2,6},{3,7},{4,0},{5,1},{6,2},{7,3},{8,12},{9,13},{10,... | collective-permute-start | bytes 786440 | tf_op jit(solution)/shard_map/ppermute | solution.py:17
  13.1 0.8 collective-permute-start
  13.9 10.5 %collective-permute-done.7.refs_2_ = bf16[512,256]{1,0:T(8,128)(2,1)S(1)} collective-permute-done((bf16[512,256]{1,0:T(8,128)(2,1)S(1)}, bf16[512,256]{1,0:T(8,128)(2,1)S(1)}, u32[]{:S(2)}, u32[]{:S(2)}) %collective-permute-start.7) | collective-permute-done | bytes 262176 | tf_op jit(solution)/shard_map/ppermute | solution.py:17
  24.4 1.2 collective-permute-start.15
  25.9 5.0 %collective-permute-done.15.refs_2_ = bf16[512,256]{1,0:T(8,128)(2,1)S(1)} collective-permute-done((bf16[512,256]{1,0:T(8,128)(2,1)S(1)}, bf16[512,256]{1,0:T(8,128)(2,1)S(1)}, u32[]{:S(2)}, u32[]{:S(2)}) %collective-permute-start.15) | collective-permute-done | bytes 262176 | tf_op jit(solution)/shard_map/ppermute | solution.py:17
  30.9 2.2 %collective-permute-start.1 = (bf16[512,2048]{1,0:T(8,128)(2,1)S(1)}, bf16[512,2048]{1,0:T(8,128)(2,1)S(1)}, u32[]{:S(2)}, u32[]{:S(2)}) collective-permute-start(bf16[512,2048]{1,0:T(8,128)(2,1)S(1)} %stage.5.refs_0_.refs_2_), channel_id=1, source_target_pairs={{0,1},{1,0},{2,3},{3,2},{4,5},{5,4},{6,7},{7,6},{8,9},{9,8},{10,11... | collective-permute-start | bytes 6291464 | tf_op jit(solution)/shard_map/ppermute | solution.py:17
  33.1 1.2 collective-permute-start.10
  34.3 6.7 %collective-permute-done.10.refs_3_ = bf16[512,256]{1,0:T(8,128)(2,1)S(1)} collective-permute-done((bf16[512,256]{1,0:T(8,128)(2,1)S(1)}, bf16[512,256]{1,0:T(8,128)(2,1)S(1)}, u32[]{:S(2)}, u32[]{:S(2)}) %collective-permute-start.10) | collective-permute-done | bytes 262176 | tf_op jit(solution)/shard_map/ppermute | solution.py:17
  41.4 6.6 %collective-permute-done.8.refs_4_ = bf16[512,256]{1,0:T(8,128)(2,1)S(1)} collective-permute-done((bf16[512,256]{1,0:T(8,128)(2,1)S(1)}, bf16[512,256]{1,0:T(8,128)(2,1)S(1)}, u32[]{:S(2)}, u32[]{:S(2)}) %collective-permute-start.8) | collective-permute-done | bytes 262176 | tf_op jit(solution)/shard_map/ppermute | solution.py:17
  48.0 1.2 collective-permute-start.16
  49.2 4.9 %collective-permute-done.16.refs_3_ = bf16[512,256]{1,0:T(8,128)(2,1)S(1)} collective-permute-done((bf16[512,256]{1,0:T(8,128)(2,1)S(1)}, bf16[512,256]{1,0:T(8,128)(2,1)S(1)}, u32[]{:S(2)}, u32[]{:S(2)}) %collective-permute-start.16) | collective-permute-done | bytes 262176 | tf_op jit(solution)/shard_map/ppermute | solution.py:17
  54.6 4.8 %collective-permute-done.17.refs_4_ = bf16[512,256]{1,0:T(8,128)(2,1)S(1)} collective-permute-done((bf16[512,256]{1,0:T(8,128)(2,1)S(1)}, bf16[512,256]{1,0:T(8,128)(2,1)S(1)}, u32[]{:S(2)}, u32[]{:S(2)}) %collective-permute-start.17) | collective-permute-done | bytes 262176 | tf_op jit(solution)/shard_map/ppermute | solution.py:17
  59.3 1.2 collective-permute-start.12
  60.6 4.0 %collective-permute-done.12.refs_2_ = bf16[512,256]{1,0:T(8,128)(2,1)S(1)} collective-permute-done((bf16[512,256]{1,0:T(8,128)(2,1)S(1)}, bf16[512,256]{1,0:T(8,128)(2,1)S(1)}, u32[]{:S(2)}, u32[]{:S(2)}) %collective-permute-start.12) | collective-permute-done | bytes 262176 | tf_op jit(solution)/shard_map/ppermute | solution.py:17
  64.6 1.2 collective-permute-start.13
  65.8 4.0 %collective-permute-done.13.refs_3_ = bf16[512,256]{1,0:T(8,128)(2,1)S(1)} collective-permute-done((bf16[512,256]{1,0:T(8,128)(2,1)S(1)}, bf16[512,256]{1,0:T(8,128)(2,1)S(1)}, u32[]{:S(2)}, u32[]{:S(2)}) %collective-permute-start.13) | collective-permute-done | bytes 262176 | tf_op jit(solution)/shard_map/ppermute | solution.py:17
  70.3 1.1 collective-permute-start.4
  71.4 2.9 %collective-permute-start.5 = (bf16[512,256]{1,0:T(8,128)(2,1)S(1)}, bf16[512,256]{1,0:T(8,128)(2,1)S(1)}, u32[]{:S(2)}, u32[]{:S(2)}) collective-permute-start(bf16[512,256]{1,0:T(8,128)(2,1)S(1)} %pick.1), channel_id=1, source_target_pairs={{0,6},{1,7},{2,4},{3,5},{4,2},{5,3},{6,0},{7,1},{8,14},{9,15},{10,... | collective-permute-start | bytes 786440 | tf_op jit(solution)/shard_map/ppermute | solution.py:17
  74.3 1.2 project.5.refs_5_
  75.5 1.0 project.6.refs_5_
  76.5 1.3 %collective-permute-start.11 = (bf16[256,256]{1,0:T(8,128)(2,1)S(1)}, bf16[256,256]{1,0:T(8,128)(2,1)S(1)}, u32[]{:S(2)}, u32[]{:S(2)}) collective-permute-start(bf16[256,256]{1,0:T(8,128)(2,1)S(1)} %slice.9), channel_id=1, source_target_pairs={{0,16},{8,24},{16,0},{24,8},{1,17},{9,25},{17,1},{25,9},{2,18},{10... | collective-permute-start | bytes 393224 | tf_op jit(solution)/shard_map/ppermute | solution.py:17
  77.9 1.2 collective-permute-start.9
  79.1 1.0 project.7.refs_5_
  80.1 1.0 project.8.refs_10_
  81.1 1.0 collective-permute-done.11.refs_9_
  82.1 1.2 project.9
  83.4 7.8 %collective-permute-start.19 = (bf16[2,2,512,256]{3,2,1,0:T(8,128)(2,1)S(1)}, bf16[2,2,512,256]{3,2,1,0:T(8,128)(2,1)S(1)}, u32[]{:S(2)}, u32[]{:S(2)}) collective-permute-start(bf16[2,2,512,256]{3,2,1,0:T(8,128)(2,1)S(1)} %get-tuple-element.19.own), channel_id=1, source_target_pairs={{0,1},{1,0},{2,3},{3,2},{4,5},{5,4},{6,7},{7,6},{8,9},{9,8},{10,11... | collective-permute-start | bytes 3145736 | tf_op jit(solution)/shard_map/ppermute | solution.py:17
  91.9 1.6 %collective-permute-done.20.oth_sums = f32[8,256]{1,0:T(8,128)S(1)} collective-permute-done((f32[8,256]{1,0:T(8,128)S(1)}, f32[8,256]{1,0:T(8,128)S(1)}, u32[]{:S(2)}, u32[]{:S(2)}) %collective-permute-start.20) | collective-permute-done | bytes 8224 | tf_op jit(solution)/shard_map/ppermute | solution.py:17
  93.5 1.0 gram.1
  94.5 2.3 %collective-permute-start.21 = (f16[136,512]{1,0:T(8,128)(2,1)S(1)}, f16[136,512]{1,0:T(8,128)(2,1)S(1)}, u32[]{:S(2)}, u32[]{:S(2)}) collective-permute-start(f16[136,512]{1,0:T(8,128)(2,1)S(1)} %convert_element_type.18), channel_id=1, source_target_pairs={{0,6},{1,7},{2,4},{3,5},{4,2},{5,3},{6,0},{7,1},{8,14},{9,15},{10,... | collective-permute-start | bytes 417800 | tf_op jit(solution)/shard_map/ppermute | solution.py:17
  97.0 1.3 %collective-permute-start.23 = (f16[136,512]{1,0:T(8,128)(2,1)S(1)}, f16[136,512]{1,0:T(8,128)(2,1)S(1)}, u32[]{:S(2)}, u32[]{:S(2)}) collective-permute-start(f16[136,512]{1,0:T(8,128)(2,1)S(1)} %convert_element_type.22), channel_id=1, source_target_pairs={{0,2},{1,3},{2,0},{3,1},{4,6},{5,7},{6,4},{7,5},{8,10},{9,11},{10,... | collective-permute-start | bytes 417800 | tf_op jit(solution)/shard_map/ppermute | solution.py:17
  98.3 3.0 %collective-permute-done.21 = f16[136,512]{1,0:T(8,128)(2,1)S(1)} collective-permute-done((f16[136,512]{1,0:T(8,128)(2,1)S(1)}, f16[136,512]{1,0:T(8,128)(2,1)S(1)}, u32[]{:S(2)}, u32[]{:S(2)}) %collective-permute-start.21) | collective-permute-done | bytes 139296 | tf_op jit(solution)/shard_map/ppermute | solution.py:17
  101.3 7.4 %collective-permute-done.22 = f16[136,512]{1,0:T(8,128)(2,1)S(1)} collective-permute-done((f16[136,512]{1,0:T(8,128)(2,1)S(1)}, f16[136,512]{1,0:T(8,128)(2,1)S(1)}, u32[]{:S(2)}, u32[]{:S(2)}) %collective-permute-start.22) | collective-permute-done | bytes 139296 | tf_op jit(solution)/shard_map/ppermute | solution.py:17
  109.2 1.3 %collective-permute-start.24 = (bf16[64,512]{1,0:T(8,128)(2,1)S(1)}, bf16[64,512]{1,0:T(8,128)(2,1)S(1)}, u32[]{:S(2)}, u32[]{:S(2)}) collective-permute-start(bf16[64,512]{1,0:T(8,128)(2,1)S(1)} %get-tuple-element.26), channel_id=1, source_target_pairs={{0,8},{8,0},{16,24},{24,16},{1,9},{9,1},{17,25},{25,17},{2,10},{10... | collective-permute-start | bytes 196616 | tf_op jit(solution)/shard_map/ppermute | solution.py:17
  110.5 2.6 %collective-permute-start.25 = (bf16[64,512]{1,0:T(8,128)(2,1)S(1)}, bf16[64,512]{1,0:T(8,128)(2,1)S(1)}, u32[]{:S(2)}, u32[]{:S(2)}) collective-permute-start(bf16[64,512]{1,0:T(8,128)(2,1)S(1)} %get-tuple-element.27), channel_id=1, source_target_pairs={{8,16},{16,8},{9,17},{17,9},{10,18},{18,10},{11,19},{19,11},{12,20... | collective-permute-start | bytes 196616 | tf_op jit(solution)/shard_map/ppermute | solution.py:497
  113.0 3.3 %collective-permute-done.25.two = bf16[64,512]{1,0:T(8,128)(2,1)S(1)} collective-permute-done((bf16[64,512]{1,0:T(8,128)(2,1)S(1)}, bf16[64,512]{1,0:T(8,128)(2,1)S(1)}, u32[]{:S(2)}, u32[]{:S(2)}) %collective-permute-start.25) | collective-permute-done | bytes 65568 | tf_op jit(solution)/shard_map/ppermute | solution.py:497
  116.6 2.7 %collective-permute-start.26 = (f32[8,128]{1,0:T(8,128)S(1)}, f32[8,128]{1,0:T(8,128)S(1)}, u32[]{:S(2)}, u32[]{:S(2)}) collective-permute-start(f32[8,128]{1,0:T(8,128)S(1)} %products.1), channel_id=1, source_target_pairs={{0,1},{1,0},{2,3},{3,2},{4,5},{5,4},{6,7},{7,6},{8,9},{9,8},{10,11... | collective-permute-start | bytes 12296 | tf_op jit(solution)/shard_map/ppermute | solution.py:17
  119.3 0.8 collective-permute-done.26
  120.2 1.7 %collective-permute-start.27 = (f32[8,128]{1,0:T(8,128)S(1)}, f32[8,128]{1,0:T(8,128)S(1)}, u32[]{:S(2)}, u32[]{:S(2)}) collective-permute-start(f32[8,128]{1,0:T(8,128)S(1)} %add.7.refs_0_), channel_id=1, source_target_pairs={{0,6},{1,7},{2,4},{3,5},{4,2},{5,3},{6,0},{7,1},{8,14},{9,15},{10,... | collective-permute-start | bytes 12296 | tf_op jit(solution)/shard_map/ppermute | solution.py:17
  121.9 1.8 %collective-permute-start.29 = (f32[8,128]{1,0:T(8,128)S(1)}, f32[8,128]{1,0:T(8,128)S(1)}, u32[]{:S(2)}, u32[]{:S(2)}) collective-permute-start(f32[8,128]{1,0:T(8,128)S(1)} %add.7.refs_0_), channel_id=1, source_target_pairs={{0,2},{1,3},{2,0},{3,1},{4,6},{5,7},{6,4},{7,5},{8,10},{9,11},{10,... | collective-permute-start | bytes 12296 | tf_op jit(solution)/shard_map/ppermute | solution.py:17
  123.9 0.9 copy.4
  124.8 0.7 collective-permute-done.28.refs_2_
  125.5 0.7 ratios.1
  (48 shorter events, 6.0 us)
Async XLA Ops:
  1.9 8.4 %collective-permute-start.6 = (bf16[256,256]{1,0:T(8,128)(2,1)S(1)}, bf16[256,256]{1,0:T(8,128)(2,1)S(1)}, u32[]{:S(2)}, u32[]{:S(2)}) collective-permute-start(bf16[256,256]{1,0:T(8,128)(2,1)S(1)} %get-tuple-element.18), channel_id=1, source_target_pairs={{0,1},{1,0},{2,3},{3,2},{4,5},{5,4},{6,7},{7,6},{8,9},{9,8},{10,11... | collective-permute-start | bytes 393224 | tf_op jit(solution)/shard_map/ppermute | solution.py:17
  2.7 3.4 %copy-start.1 = (bf16[2,256,8192]{2,1,0:T(8,128)(2,1)S(1)}, bf16[2,256,8192]{2,1,0:T(8,128)(2,1)}, u32[]{:S(2)}) copy-start(bf16[2,256,8192]{2,1,0:T(8,128)(2,1)} %param.2) | copy-start | bytes 25165828
  6.1 1.2 copy-start
  6.1 3.7 %copy-start.2 = (bf16[2,256,8192]{2,1,0:T(8,128)(2,1)S(1)}, bf16[2,256,8192]{2,1,0:T(8,128)(2,1)}, u32[]{:S(2)}) copy-start(bf16[2,256,8192]{2,1,0:T(8,128)(2,1)} %param.2) | copy-start | bytes 25165828
  6.6 63.7 %collective-permute-start.18 = (bf16[512,2048]{1,0:T(8,128)(2,1)S(1)}, bf16[512,2048]{1,0:T(8,128)(2,1)S(1)}, u32[]{:S(2)}, u32[]{:S(2)}) collective-permute-start(bf16[512,2048]{1,0:T(8,128)(2,1)S(1)} %stage.7.refs_0_), channel_id=1, source_target_pairs={{0,1},{1,0},{2,3},{3,2},{4,5},{5,4},{6,7},{7,6},{8,9},{9,8},{10,11... | collective-permute-start | bytes 6291464 | tf_op jit(solution)/shard_map/ppermute | solution.py:17
  8.0 25.1 %collective-permute-start.3 = (bf16[1024,256]{1,0:T(8,128)(2,1)S(1)}, bf16[1024,256]{1,0:T(8,128)(2,1)S(1)}, u32[]{:S(2)}, u32[]{:S(2)}) collective-permute-start(bf16[1024,256]{1,0:T(8,128)(2,1)S(1)} %get-tuple-element.16), channel_id=1, source_target_pairs={{0,1},{1,0},{2,3},{3,2},{4,5},{5,4},{6,7},{7,6},{8,9},{9,8},{10,11... | collective-permute-start | bytes 1572872 | tf_op jit(solution)/shard_map/ppermute | solution.py:17
  10.3 61.1 %collective-permute-start.2 = (bf16[512,2048]{1,0:T(8,128)(2,1)S(1)}, bf16[512,2048]{1,0:T(8,128)(2,1)S(1)}, u32[]{:S(2)}, u32[]{:S(2)}) collective-permute-start(bf16[512,2048]{1,0:T(8,128)(2,1)S(1)} %stage.6.refs_0_.refs_4_), channel_id=1, source_target_pairs={{0,1},{1,0},{2,3},{3,2},{4,5},{5,4},{6,7},{7,6},{8,9},{9,8},{10,11... | collective-permute-start | bytes 6291464 | tf_op jit(solution)/shard_map/ppermute | solution.py:17
  10.4 14.0 %collective-permute-start.7 = (bf16[512,256]{1,0:T(8,128)(2,1)S(1)}, bf16[512,256]{1,0:T(8,128)(2,1)S(1)}, u32[]{:S(2)}, u32[]{:S(2)}) collective-permute-start(bf16[512,256]{1,0:T(8,128)(2,1)S(1)} %join.1), channel_id=1, source_target_pairs={{0,4},{1,5},{2,6},{3,7},{4,0},{5,1},{6,2},{7,3},{8,12},{9,13},{10,... | collective-permute-start | bytes 786440 | tf_op jit(solution)/shard_map/ppermute | solution.py:17
  13.1 64.8 %collective-permute-start = (bf16[512,2048]{1,0:T(8,128)(2,1)S(1)}, bf16[512,2048]{1,0:T(8,128)(2,1)S(1)}, u32[]{:S(2)}, u32[]{:S(2)}) collective-permute-start(bf16[512,2048]{1,0:T(8,128)(2,1)S(1)} %stage.4.refs_0_), channel_id=1, source_target_pairs={{0,1},{1,0},{2,3},{3,2},{4,5},{5,4},{6,7},{7,6},{8,9},{9,8},{10,11... | collective-permute-start | bytes 6291464 | tf_op jit(solution)/shard_map/ppermute | solution.py:17
  24.4 6.5 %collective-permute-start.15 = (bf16[512,256]{1,0:T(8,128)(2,1)S(1)}, bf16[512,256]{1,0:T(8,128)(2,1)S(1)}, u32[]{:S(2)}, u32[]{:S(2)}) collective-permute-start(bf16[512,256]{1,0:T(8,128)(2,1)S(1)} %join.1), channel_id=1, source_target_pairs={{0,2},{1,3},{2,0},{3,1},{4,6},{5,7},{6,4},{7,5},{8,10},{9,11},{10,... | collective-permute-start | bytes 786440 | tf_op jit(solution)/shard_map/ppermute | solution.py:17
  30.9 49.2 %collective-permute-start.1 = (bf16[512,2048]{1,0:T(8,128)(2,1)S(1)}, bf16[512,2048]{1,0:T(8,128)(2,1)S(1)}, u32[]{:S(2)}, u32[]{:S(2)}) collective-permute-start(bf16[512,2048]{1,0:T(8,128)(2,1)S(1)} %stage.5.refs_0_.refs_2_), channel_id=1, source_target_pairs={{0,1},{1,0},{2,3},{3,2},{4,5},{5,4},{6,7},{7,6},{8,9},{9,8},{10,11... | collective-permute-start | bytes 6291464 | tf_op jit(solution)/shard_map/ppermute | solution.py:17
  33.1 7.9 %collective-permute-start.10 = (bf16[512,256]{1,0:T(8,128)(2,1)S(1)}, bf16[512,256]{1,0:T(8,128)(2,1)S(1)}, u32[]{:S(2)}, u32[]{:S(2)}) collective-permute-start(bf16[512,256]{1,0:T(8,128)(2,1)S(1)} %collective-permute-done.7.refs_2_), channel_id=1, source_target_pairs={{0,8},{8,0},{16,24},{24,16},{1,9},{9,1},{17,25},{25,17},{2,10},{10... | collective-permute-start | bytes 786440 | tf_op jit(solution)/shard_map/ppermute | solution.py:17
  41.0 7.0 %collective-permute-start.8 = (bf16[512,256]{1,0:T(8,128)(2,1)S(1)}, bf16[512,256]{1,0:T(8,128)(2,1)S(1)}, u32[]{:S(2)}, u32[]{:S(2)}) collective-permute-start(bf16[512,256]{1,0:T(8,128)(2,1)S(1)} %collective-permute-done.7.refs_2_), channel_id=1, source_target_pairs={{0,16},{8,24},{16,0},{24,8},{1,17},{9,25},{17,1},{25,9},{2,18},{10... | collective-permute-start | bytes 786440 | tf_op jit(solution)/shard_map/ppermute | solution.py:17
  48.0 6.1 %collective-permute-start.16 = (bf16[512,256]{1,0:T(8,128)(2,1)S(1)}, bf16[512,256]{1,0:T(8,128)(2,1)S(1)}, u32[]{:S(2)}, u32[]{:S(2)}) collective-permute-start(bf16[512,256]{1,0:T(8,128)(2,1)S(1)} %collective-permute-done.15.refs_2_), channel_id=1, source_target_pairs={{0,8},{8,0},{16,24},{24,16},{1,9},{9,1},{17,25},{25,17},{2,10},{10... | collective-permute-start | bytes 786440 | tf_op jit(solution)/shard_map/ppermute | solution.py:17
  54.1 5.2 %collective-permute-start.17 = (bf16[512,256]{1,0:T(8,128)(2,1)S(1)}, bf16[512,256]{1,0:T(8,128)(2,1)S(1)}, u32[]{:S(2)}, u32[]{:S(2)}) collective-permute-start(bf16[512,256]{1,0:T(8,128)(2,1)S(1)} %collective-permute-done.15.refs_2_), channel_id=1, source_target_pairs={{0,16},{8,24},{16,0},{24,8},{1,17},{9,25},{17,1},{25,9},{2,18},{10... | collective-permute-start | bytes 786440 | tf_op jit(solution)/shard_map/ppermute | solution.py:17
  59.3 5.2 %collective-permute-start.12 = (bf16[512,256]{1,0:T(8,128)(2,1)S(1)}, bf16[512,256]{1,0:T(8,128)(2,1)S(1)}, u32[]{:S(2)}, u32[]{:S(2)}) collective-permute-start(bf16[512,256]{1,0:T(8,128)(2,1)S(1)} %collective-permute-done.7.refs_2_), channel_id=1, source_target_pairs={{0,2},{1,3},{2,0},{3,1},{4,6},{5,7},{6,4},{7,5},{8,10},{9,11},{10,... | collective-permute-start | bytes 786440 | tf_op jit(solution)/shard_map/ppermute | solution.py:17
  64.6 5.2 %collective-permute-start.13 = (bf16[512,256]{1,0:T(8,128)(2,1)S(1)}, bf16[512,256]{1,0:T(8,128)(2,1)S(1)}, u32[]{:S(2)}, u32[]{:S(2)}) collective-permute-start(bf16[512,256]{1,0:T(8,128)(2,1)S(1)} %collective-permute-done.12.refs_2_), channel_id=1, source_target_pairs={{0,8},{8,0},{16,24},{24,16},{1,9},{9,1},{17,25},{25,17},{2,10},{10... | collective-permute-start | bytes 786440 | tf_op jit(solution)/shard_map/ppermute | solution.py:17
  69.8 6.8 %collective-permute-start.14 = (bf16[512,256]{1,0:T(8,128)(2,1)S(1)}, bf16[512,256]{1,0:T(8,128)(2,1)S(1)}, u32[]{:S(2)}, u32[]{:S(2)}) collective-permute-start(bf16[512,256]{1,0:T(8,128)(2,1)S(1)} %collective-permute-done.12.refs_2_), channel_id=1, source_target_pairs={{0,16},{8,24},{16,0},{24,8},{1,17},{9,25},{17,1},{25,9},{2,18},{10... | collective-permute-start | bytes 786440 | tf_op jit(solution)/shard_map/ppermute | solution.py:17
  70.3 10.8 %collective-permute-start.4 = (bf16[512,256]{1,0:T(8,128)(2,1)S(1)}, bf16[512,256]{1,0:T(8,128)(2,1)S(1)}, u32[]{:S(2)}, u32[]{:S(2)}) collective-permute-start(bf16[512,256]{1,0:T(8,128)(2,1)S(1)} %pick.1), channel_id=1, source_target_pairs={{0,2},{1,3},{2,0},{3,1},{4,6},{5,7},{6,4},{7,5},{8,10},{9,11},{10,... | collective-permute-start | bytes 786440 | tf_op jit(solution)/shard_map/ppermute | solution.py:17
  71.4 9.7 %collective-permute-start.5 = (bf16[512,256]{1,0:T(8,128)(2,1)S(1)}, bf16[512,256]{1,0:T(8,128)(2,1)S(1)}, u32[]{:S(2)}, u32[]{:S(2)}) collective-permute-start(bf16[512,256]{1,0:T(8,128)(2,1)S(1)} %pick.1), channel_id=1, source_target_pairs={{0,6},{1,7},{2,4},{3,5},{4,2},{5,3},{6,0},{7,1},{8,14},{9,15},{10,... | collective-permute-start | bytes 786440 | tf_op jit(solution)/shard_map/ppermute | solution.py:17
  76.5 5.6 %collective-permute-start.11 = (bf16[256,256]{1,0:T(8,128)(2,1)S(1)}, bf16[256,256]{1,0:T(8,128)(2,1)S(1)}, u32[]{:S(2)}, u32[]{:S(2)}) collective-permute-start(bf16[256,256]{1,0:T(8,128)(2,1)S(1)} %slice.9), channel_id=1, source_target_pairs={{0,16},{8,24},{16,0},{24,8},{1,17},{9,25},{17,1},{25,9},{2,18},{10... | collective-permute-start | bytes 393224 | tf_op jit(solution)/shard_map/ppermute | solution.py:17
  77.9 4.3 %collective-permute-start.9 = (bf16[256,256]{1,0:T(8,128)(2,1)S(1)}, bf16[256,256]{1,0:T(8,128)(2,1)S(1)}, u32[]{:S(2)}, u32[]{:S(2)}) collective-permute-start(bf16[256,256]{1,0:T(8,128)(2,1)S(1)} %slice.8), channel_id=1, source_target_pairs={{0,8},{8,0},{16,24},{24,16},{1,9},{9,1},{17,25},{25,17},{2,10},{10... | collective-permute-start | bytes 393224 | tf_op jit(solution)/shard_map/ppermute | solution.py:17
  83.4 10.1 %collective-permute-start.19 = (bf16[2,2,512,256]{3,2,1,0:T(8,128)(2,1)S(1)}, bf16[2,2,512,256]{3,2,1,0:T(8,128)(2,1)S(1)}, u32[]{:S(2)}, u32[]{:S(2)}) collective-permute-start(bf16[2,2,512,256]{3,2,1,0:T(8,128)(2,1)S(1)} %get-tuple-element.19.own), channel_id=1, source_target_pairs={{0,1},{1,0},{2,3},{3,2},{4,5},{5,4},{6,7},{7,6},{8,9},{9,8},{10,11... | collective-permute-start | bytes 3145736 | tf_op jit(solution)/shard_map/ppermute | solution.py:17
  91.2 2.3 %collective-permute-start.20 = (f32[8,256]{1,0:T(8,128)S(1)}, f32[8,256]{1,0:T(8,128)S(1)}, u32[]{:S(2)}, u32[]{:S(2)}) collective-permute-start(f32[8,256]{1,0:T(8,128)S(1)} %get-tuple-element.20.own_sums), channel_id=1, source_target_pairs={{0,1},{1,0},{2,3},{3,2},{4,5},{5,4},{6,7},{7,6},{8,9},{9,8},{10,11... | collective-permute-start | bytes 24584 | tf_op jit(solution)/shard_map/ppermute | solution.py:17
  94.5 6.8 %collective-permute-start.21 = (f16[136,512]{1,0:T(8,128)(2,1)S(1)}, f16[136,512]{1,0:T(8,128)(2,1)S(1)}, u32[]{:S(2)}, u32[]{:S(2)}) collective-permute-start(f16[136,512]{1,0:T(8,128)(2,1)S(1)} %convert_element_type.18), channel_id=1, source_target_pairs={{0,6},{1,7},{2,4},{3,5},{4,2},{5,3},{6,0},{7,1},{8,14},{9,15},{10,... | collective-permute-start | bytes 417800 | tf_op jit(solution)/shard_map/ppermute | solution.py:17
  96.9 11.8 %collective-permute-start.22 = (f16[136,512]{1,0:T(8,128)(2,1)S(1)}, f16[136,512]{1,0:T(8,128)(2,1)S(1)}, u32[]{:S(2)}, u32[]{:S(2)}) collective-permute-start(f16[136,512]{1,0:T(8,128)(2,1)S(1)} %convert_element_type.20), channel_id=1, source_target_pairs={{0,4},{1,5},{2,6},{3,7},{4,0},{5,1},{6,2},{7,3},{8,12},{9,13},{10,... | collective-permute-start | bytes 417800 | tf_op jit(solution)/shard_map/ppermute | solution.py:17
  97.0 11.7 %collective-permute-start.23 = (f16[136,512]{1,0:T(8,128)(2,1)S(1)}, f16[136,512]{1,0:T(8,128)(2,1)S(1)}, u32[]{:S(2)}, u32[]{:S(2)}) collective-permute-start(f16[136,512]{1,0:T(8,128)(2,1)S(1)} %convert_element_type.22), channel_id=1, source_target_pairs={{0,2},{1,3},{2,0},{3,1},{4,6},{5,7},{6,4},{7,5},{8,10},{9,11},{10,... | collective-permute-start | bytes 417800 | tf_op jit(solution)/shard_map/ppermute | solution.py:17
  109.2 3.8 %collective-permute-start.24 = (bf16[64,512]{1,0:T(8,128)(2,1)S(1)}, bf16[64,512]{1,0:T(8,128)(2,1)S(1)}, u32[]{:S(2)}, u32[]{:S(2)}) collective-permute-start(bf16[64,512]{1,0:T(8,128)(2,1)S(1)} %get-tuple-element.26), channel_id=1, source_target_pairs={{0,8},{8,0},{16,24},{24,16},{1,9},{9,1},{17,25},{25,17},{2,10},{10... | collective-permute-start | bytes 196616 | tf_op jit(solution)/shard_map/ppermute | solution.py:17
  110.5 5.9 %collective-permute-start.25 = (bf16[64,512]{1,0:T(8,128)(2,1)S(1)}, bf16[64,512]{1,0:T(8,128)(2,1)S(1)}, u32[]{:S(2)}, u32[]{:S(2)}) collective-permute-start(bf16[64,512]{1,0:T(8,128)(2,1)S(1)} %get-tuple-element.27), channel_id=1, source_target_pairs={{8,16},{16,8},{9,17},{17,9},{10,18},{18,10},{11,19},{19,11},{12,20... | collective-permute-start | bytes 196616 | tf_op jit(solution)/shard_map/ppermute | solution.py:497
  116.6 3.6 %collective-permute-start.26 = (f32[8,128]{1,0:T(8,128)S(1)}, f32[8,128]{1,0:T(8,128)S(1)}, u32[]{:S(2)}, u32[]{:S(2)}) collective-permute-start(f32[8,128]{1,0:T(8,128)S(1)} %products.1), channel_id=1, source_target_pairs={{0,1},{1,0},{2,3},{3,2},{4,5},{5,4},{6,7},{7,6},{8,9},{9,8},{10,11... | collective-permute-start | bytes 12296 | tf_op jit(solution)/shard_map/ppermute | solution.py:17
  120.2 4.6 %collective-permute-start.27 = (f32[8,128]{1,0:T(8,128)S(1)}, f32[8,128]{1,0:T(8,128)S(1)}, u32[]{:S(2)}, u32[]{:S(2)}) collective-permute-start(f32[8,128]{1,0:T(8,128)S(1)} %add.7.refs_0_), channel_id=1, source_target_pairs={{0,6},{1,7},{2,4},{3,5},{4,2},{5,3},{6,0},{7,1},{8,14},{9,15},{10,... | collective-permute-start | bytes 12296 | tf_op jit(solution)/shard_map/ppermute | solution.py:17
  121.9 3.6 %collective-permute-start.28 = (f32[8,128]{1,0:T(8,128)S(1)}, f32[8,128]{1,0:T(8,128)S(1)}, u32[]{:S(2)}, u32[]{:S(2)}) collective-permute-start(f32[8,128]{1,0:T(8,128)S(1)} %add.7.refs_0_), channel_id=1, source_target_pairs={{0,4},{1,5},{2,6},{3,7},{4,0},{5,1},{6,2},{7,3},{8,12},{9,13},{10,... | collective-permute-start | bytes 12296 | tf_op jit(solution)/shard_map/ppermute | solution.py:17
  121.9 3.6 %collective-permute-start.29 = (f32[8,128]{1,0:T(8,128)S(1)}, f32[8,128]{1,0:T(8,128)S(1)}, u32[]{:S(2)}, u32[]{:S(2)}) collective-permute-start(f32[8,128]{1,0:T(8,128)S(1)} %add.7.refs_0_), channel_id=1, source_target_pairs={{0,2},{1,3},{2,0},{3,1},{4,6},{5,7},{6,4},{7,5},{8,10},{9,11},{10,... | collective-permute-start | bytes 12296 | tf_op jit(solution)/shard_map/ppermute | solution.py:17

commit v8 on v7

--- a/solution.py
+++ b/solution.py
@@ -140,13 +140,17 @@
     spots = [(n, pl.ds(pl.multiple_of(at, 128), deep)) for n, at, deep in spots]
     weights = jnp.concatenate([piece[...] for piece in pieces], axis=0)
     rows = arrays[0].shape[0] // layers
+    left = [
+        jnp.concatenate([arrays[2 * n + side][:, columns] for n, columns in spots], axis=1)
+        for side in range(2)
+    ]
+    product = jnp.dot(jnp.concatenate(left, axis=0), weights, preferred_element_type=F32)
     kept = []
     for side in range(2):
         for layer in range(layers):
             span = pl.ds(layer * rows, rows)
-            left = [arrays[2 * n + side][span, columns] for n, columns in spots]
-            left = jnp.concatenate(left, axis=1)
-            value = jnp.dot(left, weights, preferred_element_type=F32)
+            at = (side * layers + layer) * rows
+            value = product[at : at + rows]
             if started:
                 value = value + total[side, span, :]
             if last:

time: 127 us -> 127 us (level)
  no operation moved by 1% of the time
where the time goes in v8:
time: 127 us; the launch traced here: 126 us
  waiting for transfers between devices  64.2 us (51%)
  starting transfers between devices  42.1 us (33%)
  Pallas kernels  11.2 us (9%)
  local copies, waits for them, and re-layouts  7.58 us (6%)
    ppermute x29, waiting for transfers between devices, swap(): lax.ppermute(block, axis, [(i, i ^ mask) for i in range(lax.axis_size(axi...  60.9 us
    ppermute x29, starting transfers between devices, swap(): lax.ppermute(block, axis, [(i, i ^ mask) for i in range(lax.axis_size(axi...  39.5 us
    unnamed x7, local copies, waits for them, and re-layouts  6.58 us
    pallas_call x5, Pallas kernels, project(): pl.pallas_call(functools.partial(project_kernel, keys, parts, len(started...  5.41 us
    ppermute x1, waiting for transfers between devices, local(): second = lax.ppermute(second, 'section', route + [(b, a) for a, b in route])  3.34 us
  transfers between devices with their start and end apart: 30, of which 15 were waited for; matrix products, arithmetic and copies ran while one was open for 1% of the time, Pallas kernels for 6%

profile of v8, /device:TPU:5, one launch (start us, length us, event | category | flops | bytes accessed | tf_op | source)
XLA Modules:
  0.0 126.2 jit_solution(10529774007373750648)
XLA Ops:
  0.6 1.0 constant_dynamic-slice_fusion.proj
  1.9 0.7 collective-permute-start.6
  2.7 3.4 %copy-done.1 = bf16[2,256,8192]{2,1,0:T(8,128)(2,1)S(1)} copy-done((bf16[2,256,8192]{2,1,0:T(8,128)(2,1)S(1)}, bf16[2,256,8192]{2,1,0:T(8,128)(2,1)}, u32[]{:S(2)}) %copy-start.1) | copy-done | bytes 8388632
  7.3 0.7 deal.2
  8.1 1.7 %copy-done.2 = bf16[2,256,8192]{2,1,0:T(8,128)(2,1)S(1)} copy-done((bf16[2,256,8192]{2,1,0:T(8,128)(2,1)S(1)}, bf16[2,256,8192]{2,1,0:T(8,128)(2,1)}, u32[]{:S(2)}) %copy-start.2) | copy-done | bytes 8388632
  10.4 2.4 %collective-permute-start.7 = (bf16[512,256]{1,0:T(8,128)(2,1)S(1)}, bf16[512,256]{1,0:T(8,128)(2,1)S(1)}, u32[]{:S(2)}, u32[]{:S(2)}) collective-permute-start(bf16[512,256]{1,0:T(8,128)(2,1)S(1)} %join.1), channel_id=1, source_target_pairs={{0,4},{1,5},{2,6},{3,7},{4,0},{5,1},{6,2},{7,3},{8,12},{9,13},{10,... | collective-permute-start | bytes 786440 | tf_op jit(solution)/shard_map/ppermute | solution.py:17
  13.1 0.8 collective-permute-start
  13.9 10.5 %collective-permute-done.7.refs_2_ = bf16[512,256]{1,0:T(8,128)(2,1)S(1)} collective-permute-done((bf16[512,256]{1,0:T(8,128)(2,1)S(1)}, bf16[512,256]{1,0:T(8,128)(2,1)S(1)}, u32[]{:S(2)}, u32[]{:S(2)}) %collective-permute-start.7) | collective-permute-done | bytes 262176 | tf_op jit(solution)/shard_map/ppermute | solution.py:17
  24.4 1.2 collective-permute-start.15
  25.9 5.0 %collective-permute-done.15.refs_2_ = bf16[512,256]{1,0:T(8,128)(2,1)S(1)} collective-permute-done((bf16[512,256]{1,0:T(8,128)(2,1)S(1)}, bf16[512,256]{1,0:T(8,128)(2,1)S(1)}, u32[]{:S(2)}, u32[]{:S(2)}) %collective-permute-start.15) | collective-permute-done | bytes 262176 | tf_op jit(solution)/shard_map/ppermute | solution.py:17
  30.9 2.2 %collective-permute-start.1 = (bf16[512,2048]{1,0:T(8,128)(2,1)S(1)}, bf16[512,2048]{1,0:T(8,128)(2,1)S(1)}, u32[]{:S(2)}, u32[]{:S(2)}) collective-permute-start(bf16[512,2048]{1,0:T(8,128)(2,1)S(1)} %stage.5.refs_0_.refs_2_), channel_id=1, source_target_pairs={{0,1},{1,0},{2,3},{3,2},{4,5},{5,4},{6,7},{7,6},{8,9},{9,8},{10,11... | collective-permute-start | bytes 6291464 | tf_op jit(solution)/shard_map/ppermute | solution.py:17
  33.1 1.2 collective-permute-start.10
  34.3 6.7 %collective-permute-done.10.refs_3_ = bf16[512,256]{1,0:T(8,128)(2,1)S(1)} collective-permute-done((bf16[512,256]{1,0:T(8,128)(2,1)S(1)}, bf16[512,256]{1,0:T(8,128)(2,1)S(1)}, u32[]{:S(2)}, u32[]{:S(2)}) %collective-permute-start.10) | collective-permute-done | bytes 262176 | tf_op jit(solution)/shard_map/ppermute | solution.py:17
  41.4 6.6 %collective-permute-done.8.refs_4_ = bf16[512,256]{1,0:T(8,128)(2,1)S(1)} collective-permute-done((bf16[512,256]{1,0:T(8,128)(2,1)S(1)}, bf16[512,256]{1,0:T(8,128)(2,1)S(1)}, u32[]{:S(2)}, u32[]{:S(2)}) %collective-permute-start.8) | collective-permute-done | bytes 262176 | tf_op jit(solution)/shard_map/ppermute | solution.py:17
  48.0 1.2 collective-permute-start.16
  49.2 4.9 %collective-permute-done.16.refs_3_ = bf16[512,256]{1,0:T(8,128)(2,1)S(1)} collective-permute-done((bf16[512,256]{1,0:T(8,128)(2,1)S(1)}, bf16[512,256]{1,0:T(8,128)(2,1)S(1)}, u32[]{:S(2)}, u32[]{:S(2)}) %collective-permute-start.16) | collective-permute-done | bytes 262176 | tf_op jit(solution)/shard_map/ppermute | solution.py:17
  54.6 4.8 %collective-permute-done.17.refs_4_ = bf16[512,256]{1,0:T(8,128)(2,1)S(1)} collective-permute-done((bf16[512,256]{1,0:T(8,128)(2,1)S(1)}, bf16[512,256]{1,0:T(8,128)(2,1)S(1)}, u32[]{:S(2)}, u32[]{:S(2)}) %collective-permute-start.17) | collective-permute-done | bytes 262176 | tf_op jit(solution)/shard_map/ppermute | solution.py:17
  59.3 1.2 collective-permute-start.12
  60.6 4.0 %collective-permute-done.12.refs_2_ = bf16[512,256]{1,0:T(8,128)(2,1)S(1)} collective-permute-done((bf16[512,256]{1,0:T(8,128)(2,1)S(1)}, bf16[512,256]{1,0:T(8,128)(2,1)S(1)}, u32[]{:S(2)}, u32[]{:S(2)}) %collective-permute-start.12) | collective-permute-done | bytes 262176 | tf_op jit(solution)/shard_map/ppermute | solution.py:17
  64.6 1.2 collective-permute-start.13
  65.8 4.0 %collective-permute-done.13.refs_3_ = bf16[512,256]{1,0:T(8,128)(2,1)S(1)} collective-permute-done((bf16[512,256]{1,0:T(8,128)(2,1)S(1)}, bf16[512,256]{1,0:T(8,128)(2,1)S(1)}, u32[]{:S(2)}, u32[]{:S(2)}) %collective-permute-start.13) | collective-permute-done | bytes 262176 | tf_op jit(solution)/shard_map/ppermute | solution.py:17
  70.3 1.1 collective-permute-start.4
  71.4 2.9 %collective-permute-start.5 = (bf16[512,256]{1,0:T(8,128)(2,1)S(1)}, bf16[512,256]{1,0:T(8,128)(2,1)S(1)}, u32[]{:S(2)}, u32[]{:S(2)}) collective-permute-start(bf16[512,256]{1,0:T(8,128)(2,1)S(1)} %pick.1), channel_id=1, source_target_pairs={{0,6},{1,7},{2,4},{3,5},{4,2},{5,3},{6,0},{7,1},{8,14},{9,15},{10,... | collective-permute-start | bytes 786440 | tf_op jit(solution)/shard_map/ppermute | solution.py:17
  74.3 1.2 project.5.refs_5_
  75.5 1.0 project.6.refs_5_
  76.5 1.3 %collective-permute-start.11 = (bf16[256,256]{1,0:T(8,128)(2,1)S(1)}, bf16[256,256]{1,0:T(8,128)(2,1)S(1)}, u32[]{:S(2)}, u32[]{:S(2)}) collective-permute-start(bf16[256,256]{1,0:T(8,128)(2,1)S(1)} %slice.9), channel_id=1, source_target_pairs={{0,16},{8,24},{16,0},{24,8},{1,17},{9,25},{17,1},{25,9},{2,18},{10... | collective-permute-start | bytes 393224 | tf_op jit(solution)/shard_map/ppermute | solution.py:17
  77.9 1.2 collective-permute-start.9
  79.1 1.0 project.7.refs_5_
  80.1 1.0 project.8.refs_10_
  81.1 1.0 collective-permute-done.11.refs_9_
  82.1 1.2 project.9
  83.3 7.8 %collective-permute-start.19 = (bf16[2,2,512,256]{3,2,1,0:T(8,128)(2,1)S(1)}, bf16[2,2,512,256]{3,2,1,0:T(8,128)(2,1)S(1)}, u32[]{:S(2)}, u32[]{:S(2)}) collective-permute-start(bf16[2,2,512,256]{3,2,1,0:T(8,128)(2,1)S(1)} %get-tuple-element.19.own), channel_id=1, source_target_pairs={{0,1},{1,0},{2,3},{3,2},{4,5},{5,4},{6,7},{7,6},{8,9},{9,8},{10,11... | collective-permute-start | bytes 3145736 | tf_op jit(solution)/shard_map/ppermute | solution.py:17
  91.9 1.6 %collective-permute-done.20.oth_sums = f32[8,256]{1,0:T(8,128)S(1)} collective-permute-done((f32[8,256]{1,0:T(8,128)S(1)}, f32[8,256]{1,0:T(8,128)S(1)}, u32[]{:S(2)}, u32[]{:S(2)}) %collective-permute-start.20) | collective-permute-done | bytes 8224 | tf_op jit(solution)/shard_map/ppermute | solution.py:17
  93.5 1.0 gram.1
  94.5 2.3 %collective-permute-start.21 = (f16[136,512]{1,0:T(8,128)(2,1)S(1)}, f16[136,512]{1,0:T(8,128)(2,1)S(1)}, u32[]{:S(2)}, u32[]{:S(2)}) collective-permute-start(f16[136,512]{1,0:T(8,128)(2,1)S(1)} %convert_element_type.18), channel_id=1, source_target_pairs={{0,6},{1,7},{2,4},{3,5},{4,2},{5,3},{6,0},{7,1},{8,14},{9,15},{10,... | collective-permute-start | bytes 417800 | tf_op jit(solution)/shard_map/ppermute | solution.py:17
  97.0 1.3 %collective-permute-start.23 = (f16[136,512]{1,0:T(8,128)(2,1)S(1)}, f16[136,512]{1,0:T(8,128)(2,1)S(1)}, u32[]{:S(2)}, u32[]{:S(2)}) collective-permute-start(f16[136,512]{1,0:T(8,128)(2,1)S(1)} %convert_element_type.22), channel_id=1, source_target_pairs={{0,2},{1,3},{2,0},{3,1},{4,6},{5,7},{6,4},{7,5},{8,10},{9,11},{10,... | collective-permute-start | bytes 417800 | tf_op jit(solution)/shard_map/ppermute | solution.py:17
  98.3 3.0 %collective-permute-done.21 = f16[136,512]{1,0:T(8,128)(2,1)S(1)} collective-permute-done((f16[136,512]{1,0:T(8,128)(2,1)S(1)}, f16[136,512]{1,0:T(8,128)(2,1)S(1)}, u32[]{:S(2)}, u32[]{:S(2)}) %collective-permute-start.21) | collective-permute-done | bytes 139296 | tf_op jit(solution)/shard_map/ppermute | solution.py:17
  101.3 7.4 %collective-permute-done.22 = f16[136,512]{1,0:T(8,128)(2,1)S(1)} collective-permute-done((f16[136,512]{1,0:T(8,128)(2,1)S(1)}, f16[136,512]{1,0:T(8,128)(2,1)S(1)}, u32[]{:S(2)}, u32[]{:S(2)}) %collective-permute-start.22) | collective-permute-done | bytes 139296 | tf_op jit(solution)/shard_map/ppermute | solution.py:17
  109.2 1.3 %collective-permute-start.24 = (bf16[64,512]{1,0:T(8,128)(2,1)S(1)}, bf16[64,512]{1,0:T(8,128)(2,1)S(1)}, u32[]{:S(2)}, u32[]{:S(2)}) collective-permute-start(bf16[64,512]{1,0:T(8,128)(2,1)S(1)} %get-tuple-element.26), channel_id=1, source_target_pairs={{0,8},{8,0},{16,24},{24,16},{1,9},{9,1},{17,25},{25,17},{2,10},{10... | collective-permute-start | bytes 196616 | tf_op jit(solution)/shard_map/ppermute | solution.py:17
  110.5 2.5 %collective-permute-start.25 = (bf16[64,512]{1,0:T(8,128)(2,1)S(1)}, bf16[64,512]{1,0:T(8,128)(2,1)S(1)}, u32[]{:S(2)}, u32[]{:S(2)}) collective-permute-start(bf16[64,512]{1,0:T(8,128)(2,1)S(1)} %get-tuple-element.27), channel_id=1, source_target_pairs={{8,16},{16,8},{9,17},{17,9},{10,18},{18,10},{11,19},{19,11},{12,20... | collective-permute-start | bytes 196616 | tf_op jit(solution)/shard_map/ppermute | solution.py:501
  113.0 3.3 %collective-permute-done.25.two = bf16[64,512]{1,0:T(8,128)(2,1)S(1)} collective-permute-done((bf16[64,512]{1,0:T(8,128)(2,1)S(1)}, bf16[64,512]{1,0:T(8,128)(2,1)S(1)}, u32[]{:S(2)}, u32[]{:S(2)}) %collective-permute-start.25) | collective-permute-done | bytes 65568 | tf_op jit(solution)/shard_map/ppermute | solution.py:501
  116.6 2.7 %collective-permute-start.26 = (f32[8,128]{1,0:T(8,128)S(1)}, f32[8,128]{1,0:T(8,128)S(1)}, u32[]{:S(2)}, u32[]{:S(2)}) collective-permute-start(f32[8,128]{1,0:T(8,128)S(1)} %products.1), channel_id=1, source_target_pairs={{0,1},{1,0},{2,3},{3,2},{4,5},{5,4},{6,7},{7,6},{8,9},{9,8},{10,11... | collective-permute-start | bytes 12296 | tf_op jit(solution)/shard_map/ppermute | solution.py:17
  119.3 0.8 collective-permute-done.26
  120.2 1.7 %collective-permute-start.27 = (f32[8,128]{1,0:T(8,128)S(1)}, f32[8,128]{1,0:T(8,128)S(1)}, u32[]{:S(2)}, u32[]{:S(2)}) collective-permute-start(f32[8,128]{1,0:T(8,128)S(1)} %add.7.refs_0_), channel_id=1, source_target_pairs={{0,6},{1,7},{2,4},{3,5},{4,2},{5,3},{6,0},{7,1},{8,14},{9,15},{10,... | collective-permute-start | bytes 12296 | tf_op jit(solution)/shard_map/ppermute | solution.py:17
  121.9 1.8 %collective-permute-start.29 = (f32[8,128]{1,0:T(8,128)S(1)}, f32[8,128]{1,0:T(8,128)S(1)}, u32[]{:S(2)}, u32[]{:S(2)}) collective-permute-start(f32[8,128]{1,0:T(8,128)S(1)} %add.7.refs_0_), channel_id=1, source_target_pairs={{0,2},{1,3},{2,0},{3,1},{4,6},{5,7},{6,4},{7,5},{8,10},{9,11},{10,... | collective-permute-start | bytes 12296 | tf_op jit(solution)/shard_map/ppermute | solution.py:17
  123.9 0.9 copy.4
  124.8 0.7 collective-permute-done.28.refs_2_
  125.5 0.7 ratios.1
  (48 shorter events, 6.0 us)
Async XLA Ops:
  1.9 8.4 %collective-permute-start.6 = (bf16[256,256]{1,0:T(8,128)(2,1)S(1)}, bf16[256,256]{1,0:T(8,128)(2,1)S(1)}, u32[]{:S(2)}, u32[]{:S(2)}) collective-permute-start(bf16[256,256]{1,0:T(8,128)(2,1)S(1)} %get-tuple-element.18), channel_id=1, source_target_pairs={{0,1},{1,0},{2,3},{3,2},{4,5},{5,4},{6,7},{7,6},{8,9},{9,8},{10,11... | collective-permute-start | bytes 393224 | tf_op jit(solution)/shard_map/ppermute | solution.py:17
  2.7 3.4 %copy-start.1 = (bf16[2,256,8192]{2,1,0:T(8,128)(2,1)S(1)}, bf16[2,256,8192]{2,1,0:T(8,128)(2,1)}, u32[]{:S(2)}) copy-start(bf16[2,256,8192]{2,1,0:T(8,128)(2,1)} %param.2) | copy-start | bytes 25165828
  6.1 1.2 copy-start
  6.1 3.7 %copy-start.2 = (bf16[2,256,8192]{2,1,0:T(8,128)(2,1)S(1)}, bf16[2,256,8192]{2,1,0:T(8,128)(2,1)}, u32[]{:S(2)}) copy-start(bf16[2,256,8192]{2,1,0:T(8,128)(2,1)} %param.2) | copy-start | bytes 25165828
  6.6 63.7 %collective-permute-start.18 = (bf16[512,2048]{1,0:T(8,128)(2,1)S(1)}, bf16[512,2048]{1,0:T(8,128)(2,1)S(1)}, u32[]{:S(2)}, u32[]{:S(2)}) collective-permute-start(bf16[512,2048]{1,0:T(8,128)(2,1)S(1)} %stage.7.refs_0_), channel_id=1, source_target_pairs={{0,1},{1,0},{2,3},{3,2},{4,5},{5,4},{6,7},{7,6},{8,9},{9,8},{10,11... | collective-permute-start | bytes 6291464 | tf_op jit(solution)/shard_map/ppermute | solution.py:17
  8.0 25.1 %collective-permute-start.3 = (bf16[1024,256]{1,0:T(8,128)(2,1)S(1)}, bf16[1024,256]{1,0:T(8,128)(2,1)S(1)}, u32[]{:S(2)}, u32[]{:S(2)}) collective-permute-start(bf16[1024,256]{1,0:T(8,128)(2,1)S(1)} %get-tuple-element.16), channel_id=1, source_target_pairs={{0,1},{1,0},{2,3},{3,2},{4,5},{5,4},{6,7},{7,6},{8,9},{9,8},{10,11... | collective-permute-start | bytes 1572872 | tf_op jit(solution)/shard_map/ppermute | solution.py:17
  10.3 61.1 %collective-permute-start.2 = (bf16[512,2048]{1,0:T(8,128)(2,1)S(1)}, bf16[512,2048]{1,0:T(8,128)(2,1)S(1)}, u32[]{:S(2)}, u32[]{:S(2)}) collective-permute-start(bf16[512,2048]{1,0:T(8,128)(2,1)S(1)} %stage.6.refs_0_.refs_4_), channel_id=1, source_target_pairs={{0,1},{1,0},{2,3},{3,2},{4,5},{5,4},{6,7},{7,6},{8,9},{9,8},{10,11... | collective-permute-start | bytes 6291464 | tf_op jit(solution)/shard_map/ppermute | solution.py:17
  10.4 14.0 %collective-permute-start.7 = (bf16[512,256]{1,0:T(8,128)(2,1)S(1)}, bf16[512,256]{1,0:T(8,128)(2,1)S(1)}, u32[]{:S(2)}, u32[]{:S(2)}) collective-permute-start(bf16[512,256]{1,0:T(8,128)(2,1)S(1)} %join.1), channel_id=1, source_target_pairs={{0,4},{1,5},{2,6},{3,7},{4,0},{5,1},{6,2},{7,3},{8,12},{9,13},{10,... | collective-permute-start | bytes 786440 | tf_op jit(solution)/shard_map/ppermute | solution.py:17
  13.1 64.8 %collective-permute-start = (bf16[512,2048]{1,0:T(8,128)(2,1)S(1)}, bf16[512,2048]{1,0:T(8,128)(2,1)S(1)}, u32[]{:S(2)}, u32[]{:S(2)}) collective-permute-start(bf16[512,2048]{1,0:T(8,128)(2,1)S(1)} %stage.4.refs_0_), channel_id=1, source_target_pairs={{0,1},{1,0},{2,3},{3,2},{4,5},{5,4},{6,7},{7,6},{8,9},{9,8},{10,11... | collective-permute-start | bytes 6291464 | tf_op jit(solution)/shard_map/ppermute | solution.py:17
  24.4 6.5 %collective-permute-start.15 = (bf16[512,256]{1,0:T(8,128)(2,1)S(1)}, bf16[512,256]{1,0:T(8,128)(2,1)S(1)}, u32[]{:S(2)}, u32[]{:S(2)}) collective-permute-start(bf16[512,256]{1,0:T(8,128)(2,1)S(1)} %join.1), channel_id=1, source_target_pairs={{0,2},{1,3},{2,0},{3,1},{4,6},{5,7},{6,4},{7,5},{8,10},{9,11},{10,... | collective-permute-start | bytes 786440 | tf_op jit(solution)/shard_map/ppermute | solution.py:17
  30.9 49.2 %collective-permute-start.1 = (bf16[512,2048]{1,0:T(8,128)(2,1)S(1)}, bf16[512,2048]{1,0:T(8,128)(2,1)S(1)}, u32[]{:S(2)}, u32[]{:S(2)}) collective-permute-start(bf16[512,2048]{1,0:T(8,128)(2,1)S(1)} %stage.5.refs_0_.refs_2_), channel_id=1, source_target_pairs={{0,1},{1,0},{2,3},{3,2},{4,5},{5,4},{6,7},{7,6},{8,9},{9,8},{10,11... | collective-permute-start | bytes 6291464 | tf_op jit(solution)/shard_map/ppermute | solution.py:17
  33.1 7.9 %collective-permute-start.10 = (bf16[512,256]{1,0:T(8,128)(2,1)S(1)}, bf16[512,256]{1,0:T(8,128)(2,1)S(1)}, u32[]{:S(2)}, u32[]{:S(2)}) collective-permute-start(bf16[512,256]{1,0:T(8,128)(2,1)S(1)} %collective-permute-done.7.refs_2_), channel_id=1, source_target_pairs={{0,8},{8,0},{16,24},{24,16},{1,9},{9,1},{17,25},{25,17},{2,10},{10... | collective-permute-start | bytes 786440 | tf_op jit(solution)/shard_map/ppermute | solution.py:17
  41.0 7.0 %collective-permute-start.8 = (bf16[512,256]{1,0:T(8,128)(2,1)S(1)}, bf16[512,256]{1,0:T(8,128)(2,1)S(1)}, u32[]{:S(2)}, u32[]{:S(2)}) collective-permute-start(bf16[512,256]{1,0:T(8,128)(2,1)S(1)} %collective-permute-done.7.refs_2_), channel_id=1, source_target_pairs={{0,16},{8,24},{16,0},{24,8},{1,17},{9,25},{17,1},{25,9},{2,18},{10... | collective-permute-start | bytes 786440 | tf_op jit(solution)/shard_map/ppermute | solution.py:17
  48.0 6.1 %collective-permute-start.16 = (bf16[512,256]{1,0:T(8,128)(2,1)S(1)}, bf16[512,256]{1,0:T(8,128)(2,1)S(1)}, u32[]{:S(2)}, u32[]{:S(2)}) collective-permute-start(bf16[512,256]{1,0:T(8,128)(2,1)S(1)} %collective-permute-done.15.refs_2_), channel_id=1, source_target_pairs={{0,8},{8,0},{16,24},{24,16},{1,9},{9,1},{17,25},{25,17},{2,10},{10... | collective-permute-start | bytes 786440 | tf_op jit(solution)/shard_map/ppermute | solution.py:17
  54.1 5.2 %collective-permute-start.17 = (bf16[512,256]{1,0:T(8,128)(2,1)S(1)}, bf16[512,256]{1,0:T(8,128)(2,1)S(1)}, u32[]{:S(2)}, u32[]{:S(2)}) collective-permute-start(bf16[512,256]{1,0:T(8,128)(2,1)S(1)} %collective-permute-done.15.refs_2_), channel_id=1, source_target_pairs={{0,16},{8,24},{16,0},{24,8},{1,17},{9,25},{17,1},{25,9},{2,18},{10... | collective-permute-start | bytes 786440 | tf_op jit(solution)/shard_map/ppermute | solution.py:17
  59.3 5.2 %collective-permute-start.12 = (bf16[512,256]{1,0:T(8,128)(2,1)S(1)}, bf16[512,256]{1,0:T(8,128)(2,1)S(1)}, u32[]{:S(2)}, u32[]{:S(2)}) collective-permute-start(bf16[512,256]{1,0:T(8,128)(2,1)S(1)} %collective-permute-done.7.refs_2_), channel_id=1, source_target_pairs={{0,2},{1,3},{2,0},{3,1},{4,6},{5,7},{6,4},{7,5},{8,10},{9,11},{10,... | collective-permute-start | bytes 786440 | tf_op jit(solution)/shard_map/ppermute | solution.py:17
  64.6 5.2 %collective-permute-start.13 = (bf16[512,256]{1,0:T(8,128)(2,1)S(1)}, bf16[512,256]{1,0:T(8,128)(2,1)S(1)}, u32[]{:S(2)}, u32[]{:S(2)}) collective-permute-start(bf16[512,256]{1,0:T(8,128)(2,1)S(1)} %collective-permute-done.12.refs_2_), channel_id=1, source_target_pairs={{0,8},{8,0},{16,24},{24,16},{1,9},{9,1},{17,25},{25,17},{2,10},{10... | collective-permute-start | bytes 786440 | tf_op jit(solution)/shard_map/ppermute | solution.py:17
  69.8 6.8 %collective-permute-start.14 = (bf16[512,256]{1,0:T(8,128)(2,1)S(1)}, bf16[512,256]{1,0:T(8,128)(2,1)S(1)}, u32[]{:S(2)}, u32[]{:S(2)}) collective-permute-start(bf16[512,256]{1,0:T(8,128)(2,1)S(1)} %collective-permute-done.12.refs_2_), channel_id=1, source_target_pairs={{0,16},{8,24},{16,0},{24,8},{1,17},{9,25},{17,1},{25,9},{2,18},{10... | collective-permute-start | bytes 786440 | tf_op jit(solution)/shard_map/ppermute | solution.py:17
  70.3 10.8 %collective-permute-start.4 = (bf16[512,256]{1,0:T(8,128)(2,1)S(1)}, bf16[512,256]{1,0:T(8,128)(2,1)S(1)}, u32[]{:S(2)}, u32[]{:S(2)}) collective-permute-start(bf16[512,256]{1,0:T(8,128)(2,1)S(1)} %pick.1), channel_id=1, source_target_pairs={{0,2},{1,3},{2,0},{3,1},{4,6},{5,7},{6,4},{7,5},{8,10},{9,11},{10,... | collective-permute-start | bytes 786440 | tf_op jit(solution)/shard_map/ppermute | solution.py:17
  71.4 9.7 %collective-permute-start.5 = (bf16[512,256]{1,0:T(8,128)(2,1)S(1)}, bf16[512,256]{1,0:T(8,128)(2,1)S(1)}, u32[]{:S(2)}, u32[]{:S(2)}) collective-permute-start(bf16[512,256]{1,0:T(8,128)(2,1)S(1)} %pick.1), channel_id=1, source_target_pairs={{0,6},{1,7},{2,4},{3,5},{4,2},{5,3},{6,0},{7,1},{8,14},{9,15},{10,... | collective-permute-start | bytes 786440 | tf_op jit(solution)/shard_map/ppermute | solution.py:17
  76.5 5.6 %collective-permute-start.11 = (bf16[256,256]{1,0:T(8,128)(2,1)S(1)}, bf16[256,256]{1,0:T(8,128)(2,1)S(1)}, u32[]{:S(2)}, u32[]{:S(2)}) collective-permute-start(bf16[256,256]{1,0:T(8,128)(2,1)S(1)} %slice.9), channel_id=1, source_target_pairs={{0,16},{8,24},{16,0},{24,8},{1,17},{9,25},{17,1},{25,9},{2,18},{10... | collective-permute-start | bytes 393224 | tf_op jit(solution)/shard_map/ppermute | solution.py:17
  77.9 4.3 %collective-permute-start.9 = (bf16[256,256]{1,0:T(8,128)(2,1)S(1)}, bf16[256,256]{1,0:T(8,128)(2,1)S(1)}, u32[]{:S(2)}, u32[]{:S(2)}) collective-permute-start(bf16[256,256]{1,0:T(8,128)(2,1)S(1)} %slice.8), channel_id=1, source_target_pairs={{0,8},{8,0},{16,24},{24,16},{1,9},{9,1},{17,25},{25,17},{2,10},{10... | collective-permute-start | bytes 393224 | tf_op jit(solution)/shard_map/ppermute | solution.py:17
  83.3 10.1 %collective-permute-start.19 = (bf16[2,2,512,256]{3,2,1,0:T(8,128)(2,1)S(1)}, bf16[2,2,512,256]{3,2,1,0:T(8,128)(2,1)S(1)}, u32[]{:S(2)}, u32[]{:S(2)}) collective-permute-start(bf16[2,2,512,256]{3,2,1,0:T(8,128)(2,1)S(1)} %get-tuple-element.19.own), channel_id=1, source_target_pairs={{0,1},{1,0},{2,3},{3,2},{4,5},{5,4},{6,7},{7,6},{8,9},{9,8},{10,11... | collective-permute-start | bytes 3145736 | tf_op jit(solution)/shard_map/ppermute | solution.py:17
  91.2 2.3 %collective-permute-start.20 = (f32[8,256]{1,0:T(8,128)S(1)}, f32[8,256]{1,0:T(8,128)S(1)}, u32[]{:S(2)}, u32[]{:S(2)}) collective-permute-start(f32[8,256]{1,0:T(8,128)S(1)} %get-tuple-element.20.own_sums), channel_id=1, source_target_pairs={{0,1},{1,0},{2,3},{3,2},{4,5},{5,4},{6,7},{7,6},{8,9},{9,8},{10,11... | collective-permute-start | bytes 24584 | tf_op jit(solution)/shard_map/ppermute | solution.py:17
  94.5 6.8 %collective-permute-start.21 = (f16[136,512]{1,0:T(8,128)(2,1)S(1)}, f16[136,512]{1,0:T(8,128)(2,1)S(1)}, u32[]{:S(2)}, u32[]{:S(2)}) collective-permute-start(f16[136,512]{1,0:T(8,128)(2,1)S(1)} %convert_element_type.18), channel_id=1, source_target_pairs={{0,6},{1,7},{2,4},{3,5},{4,2},{5,3},{6,0},{7,1},{8,14},{9,15},{10,... | collective-permute-start | bytes 417800 | tf_op jit(solution)/shard_map/ppermute | solution.py:17
  96.9 11.8 %collective-permute-start.22 = (f16[136,512]{1,0:T(8,128)(2,1)S(1)}, f16[136,512]{1,0:T(8,128)(2,1)S(1)}, u32[]{:S(2)}, u32[]{:S(2)}) collective-permute-start(f16[136,512]{1,0:T(8,128)(2,1)S(1)} %convert_element_type.20), channel_id=1, source_target_pairs={{0,4},{1,5},{2,6},{3,7},{4,0},{5,1},{6,2},{7,3},{8,12},{9,13},{10,... | collective-permute-start | bytes 417800 | tf_op jit(solution)/shard_map/ppermute | solution.py:17
  97.0 11.7 %collective-permute-start.23 = (f16[136,512]{1,0:T(8,128)(2,1)S(1)}, f16[136,512]{1,0:T(8,128)(2,1)S(1)}, u32[]{:S(2)}, u32[]{:S(2)}) collective-permute-start(f16[136,512]{1,0:T(8,128)(2,1)S(1)} %convert_element_type.22), channel_id=1, source_target_pairs={{0,2},{1,3},{2,0},{3,1},{4,6},{5,7},{6,4},{7,5},{8,10},{9,11},{10,... | collective-permute-start | bytes 417800 | tf_op jit(solution)/shard_map/ppermute | solution.py:17
  109.2 3.8 %collective-permute-start.24 = (bf16[64,512]{1,0:T(8,128)(2,1)S(1)}, bf16[64,512]{1,0:T(8,128)(2,1)S(1)}, u32[]{:S(2)}, u32[]{:S(2)}) collective-permute-start(bf16[64,512]{1,0:T(8,128)(2,1)S(1)} %get-tuple-element.26), channel_id=1, source_target_pairs={{0,8},{8,0},{16,24},{24,16},{1,9},{9,1},{17,25},{25,17},{2,10},{10... | collective-permute-start | bytes 196616 | tf_op jit(solution)/shard_map/ppermute | solution.py:17
  110.5 5.9 %collective-permute-start.25 = (bf16[64,512]{1,0:T(8,128)(2,1)S(1)}, bf16[64,512]{1,0:T(8,128)(2,1)S(1)}, u32[]{:S(2)}, u32[]{:S(2)}) collective-permute-start(bf16[64,512]{1,0:T(8,128)(2,1)S(1)} %get-tuple-element.27), channel_id=1, source_target_pairs={{8,16},{16,8},{9,17},{17,9},{10,18},{18,10},{11,19},{19,11},{12,20... | collective-permute-start | bytes 196616 | tf_op jit(solution)/shard_map/ppermute | solution.py:501
  116.6 3.6 %collective-permute-start.26 = (f32[8,128]{1,0:T(8,128)S(1)}, f32[8,128]{1,0:T(8,128)S(1)}, u32[]{:S(2)}, u32[]{:S(2)}) collective-permute-start(f32[8,128]{1,0:T(8,128)S(1)} %products.1), channel_id=1, source_target_pairs={{0,1},{1,0},{2,3},{3,2},{4,5},{5,4},{6,7},{7,6},{8,9},{9,8},{10,11... | collective-permute-start | bytes 12296 | tf_op jit(solution)/shard_map/ppermute | solution.py:17
  120.2 4.6 %collective-permute-start.27 = (f32[8,128]{1,0:T(8,128)S(1)}, f32[8,128]{1,0:T(8,128)S(1)}, u32[]{:S(2)}, u32[]{:S(2)}) collective-permute-start(f32[8,128]{1,0:T(8,128)S(1)} %add.7.refs_0_), channel_id=1, source_target_pairs={{0,6},{1,7},{2,4},{3,5},{4,2},{5,3},{6,0},{7,1},{8,14},{9,15},{10,... | collective-permute-start | bytes 12296 | tf_op jit(solution)/shard_map/ppermute | solution.py:17
  121.9 3.6 %collective-permute-start.28 = (f32[8,128]{1,0:T(8,128)S(1)}, f32[8,128]{1,0:T(8,128)S(1)}, u32[]{:S(2)}, u32[]{:S(2)}) collective-permute-start(f32[8,128]{1,0:T(8,128)S(1)} %add.7.refs_0_), channel_id=1, source_target_pairs={{0,4},{1,5},{2,6},{3,7},{4,0},{5,1},{6,2},{7,3},{8,12},{9,13},{10,... | collective-permute-start | bytes 12296 | tf_op jit(solution)/shard_map/ppermute | solution.py:17
  121.9 3.6 %collective-permute-start.29 = (f32[8,128]{1,0:T(8,128)S(1)}, f32[8,128]{1,0:T(8,128)S(1)}, u32[]{:S(2)}, u32[]{:S(2)}) collective-permute-start(f32[8,128]{1,0:T(8,128)S(1)} %add.7.refs_0_), channel_id=1, source_target_pairs={{0,2},{1,3},{2,0},{3,1},{4,6},{5,7},{6,4},{7,5},{8,10},{9,11},{10,... | collective-permute-start | bytes 12296 | tf_op jit(solution)/shard_map/ppermute | solution.py:17
